TPU v7x, 512 devices: a whole 4x4x16 slice. The times are simulated.
512 devices in a mesh: tile: 64 (over z, y), level: 8 (over x, core).
Axes of the slice: x: 4, y: 4, z: 16, core: 2. Of those that a mesh axis runs over, the one named last changes fastest.
Arguments:
- anomalies: bfloat16 [512, 32, 8192], P(None, 'level', 'tile'), may hold values from -6 to 6
- footprint: bfloat16 [32768, 128], P('tile'), may hold values from -0.5 to 0.5
- weighting: float32 [32, 32768], P('level', 'tile'), may hold values from 0.02 to 0.3
- dual_rows: bfloat16 [32768, 512], P(('tile', 'level')), may hold values from -6 to 6
- taper_blocks: bfloat16 [4, 128, 512], replicated, may hold values from 0.099609375 to 1
- obs_count: int32 [64], replicated, may hold values from 1 to 512, 16384 in all
- near_tiles: int32 [64, 6], replicated, may hold values from 0 to 63, as said below
- taper_class: int32 [64, 6], P('tile'), may hold values from 0 to 3
Outputs:
- increment: float32 [512, 32, 8192], P(None, 'level', 'tile')
Inputs may be any that keep to these rules, and one draw needn't show every extreme that they name: `near_tiles`: row t lists 6 different tiles, each within cyclic distance 4 of t, that is (t + d) mod 64 with |d| <= 4.
All inputs are finite; a program needn't handle non-finite values.
Results may differ from a plain program's by a relative error of at most 0.004.
Values may be sent and summed in bfloat16 or wider, within the bound.
No kernel may reach another device: no remote copies, remote signals or barrier semaphores. Data moves between devices by JAX's collectives and lax.ppermute only.
A program may use at most 64 MiB of HBM per device.

v0:
```python
import jax
import jax.numpy as jnp
from jax import lax
from jax.sharding import PartitionSpec as P

SPAN = 256
REACH = 4


def split_up(x, dim, devices):
    before, after = (x.shape[:dim], x.shape[dim + 1 :])
    return jnp.moveaxis(x.reshape(*before, devices, -1, *after), dim, 0)


def sum_at_owner(x, axis, dim):
    blocks = split_up(x, dim, lax.axis_size(axis))
    arrived = lax.all_to_all(blocks, axis, split_axis=0, concat_axis=0, tiled=True)
    return arrived.sum(axis=0)


def from_behind(value, axis, steps):
    count = lax.axis_size(axis)
    pairs = [(source, (source + steps) % count) for source in range(count)]
    return lax.ppermute(value, axis, pairs)


def side_by_side(arrays, axis, dim, along):
    widths = [a.shape[along] for a in arrays]
    both = jnp.concatenate(arrays, axis=along)
    whole = lax.all_gather(both, axis, axis=dim, tiled=True)
    return tuple(jnp.split(whole, [sum(widths[:k]) for k in range(1, len(widths))], axis=along))


def pick_near(stacked_y, stacked_w, sources, tile_id, tile_count):
    offset = (sources - tile_id) % tile_count
    offset = jnp.where(offset > REACH, offset - tile_count, offset) + REACH
    return (jnp.take(stacked_y, offset, axis=0), jnp.take(stacked_w, offset, axis=0))


def shards(
    anomalies, footprint, weighting, dual_rows, taper_blocks, obs_count, near_tiles, taper_class
):
    members, lev_dev, points = anomalies.shape
    owned = dual_rows.shape[0]
    tile_id = lax.axis_index("tile")
    level_id = lax.axis_index("level")
    tile_count = lax.axis_size("tile")
    summed = jnp.zeros((owned * lax.axis_size("level"), members), jnp.float32)
    for level_num in range(lev_dev):
        projected = lax.dot_general(
            footprint,
            anomalies[:, level_num, :],
            (((1,), (1,)), ((), ())),
            preferred_element_type=jnp.float32,
        )
        summed = summed + weighting[level_num][:, None] * projected
    observed = sum_at_owner(summed, "level", 0)
    slot_ids = level_id * owned + jnp.arange(owned, dtype=jnp.int32)
    present = slot_ids < obs_count[tile_id]
    rows_y = jnp.where(present[:, None], observed, 0.0).astype(jnp.bfloat16)
    sources = lax.dynamic_index_in_dim(near_tiles, tile_id, 0, keepdims=False)
    classes = taper_class[0]
    cells = lev_dev * points
    flat_state = anomalies.reshape(members, cells)
    initial = jnp.zeros((members, cells), jnp.float32)
    found_y = []
    found_w = []
    for distance in range(-REACH, REACH + 1):
        if distance == 0:
            found_y.append(rows_y)
            found_w.append(dual_rows)
        else:
            moved_y, moved_w = from_behind((rows_y, dual_rows), "tile", -distance)
            found_y.append(moved_y)
            found_w.append(moved_w)
    near_y, near_w = pick_near(jnp.stack(found_y), jnp.stack(found_w), sources, tile_id, tile_count)
    whole_y, whole_w = side_by_side((near_y, near_w), "level", 1, 0)
    running = initial
    row_total = whole_y.shape[1]
    for block_first in range(0, row_total, SPAN):
        block_size = min(SPAN, row_total - block_first)
        for which in range(whole_y.shape[0]):

            def add_block(carried, which=which, block_first=block_first, block_size=block_size):
                block_y = whole_y[which, block_first : block_first + block_size]
                block_w = whole_w[which, block_first : block_first + block_size]
                taper_all = lax.dynamic_index_in_dim(
                    taper_blocks, classes[which], 0, keepdims=False
                )
                taper = lax.dynamic_slice_in_dim(taper_all, block_first, block_size, 1)
                covar = lax.dot_general(
                    flat_state,
                    block_y,
                    (((0,), (1,)), ((), ())),
                    preferred_element_type=jnp.float32,
                )
                scaled = taper.astype(jnp.float32) / jnp.float32(members - 1)
                tapered = (
                    (covar.reshape(lev_dev, points, block_size) * scaled[None])
                    .reshape(cells, block_size)
                    .astype(jnp.bfloat16)
                )
                return carried + lax.dot_general(
                    block_w, tapered, (((0,), (1,)), ((), ())), preferred_element_type=jnp.float32
                )

            running = add_block(running)
    return running.reshape(members, lev_dev, points)


def solution(mesh):
    return jax.shard_map(
        shards,
        mesh=mesh,
        in_specs=(
            P(None, "level", "tile"),
            P("tile", None),
            P("level", "tile"),
            P(("tile", "level"), None),
            P(),
            P(),
            P(),
            P("tile", None),
        ),
        out_specs=P(None, "level", "tile"),
        check_vma=False,
    )
```

profile of v0, /device:TPU:1, one launch (start us, length us, event | category | flops | bytes accessed | tf_op | source)
XLA Modules:
  0.0 174.0 jit_solution(11459399696371541118)
XLA Ops:
  6.5 4.5 %collective-permute-start.8 = (bf16[64,512]{1,0:T(8,128)(2,1)}, bf16[64,512]{1,0:T(8,128)(2,1)S(1)}, u32[]{:S(2)}, u32[]{:S(2)}) collective-permute-start(bf16[64,512]{1,0:T(8,128)(2,1)} %param.13), channel_id=1, source_target_pairs={{0,32},{8,40},{16,48},{24,56},{32,64},{40,72},{48,80},{56,88},{64,... | collective-permute-start | bytes 196616 | tf_op jit(solution)/shard_map/ppermute | solution.py:24
  11.0 4.6 %collective-permute-start.9 = (bf16[64,512]{1,0:T(8,128)(2,1)}, bf16[64,512]{1,0:T(8,128)(2,1)S(1)}, u32[]{:S(2)}, u32[]{:S(2)}) collective-permute-start(bf16[64,512]{1,0:T(8,128)(2,1)} %param.13), channel_id=1, source_target_pairs={{0,24},{8,32},{16,40},{24,48},{32,56},{40,64},{48,72},{56,80},{64,... | collective-permute-start | bytes 196616 | tf_op jit(solution)/shard_map/ppermute | solution.py:24
  15.7 3.6 %collective-permute-start.10 = (bf16[64,512]{1,0:T(8,128)(2,1)}, bf16[64,512]{1,0:T(8,128)(2,1)S(1)}, u32[]{:S(2)}, u32[]{:S(2)}) collective-permute-start(bf16[64,512]{1,0:T(8,128)(2,1)} %param.13), channel_id=1, source_target_pairs={{0,16},{8,24},{16,32},{24,40},{32,48},{40,56},{48,64},{56,72},{64,... | collective-permute-start | bytes 196616 | tf_op jit(solution)/shard_map/ppermute | solution.py:24
  19.3 2.6 %collective-permute-start.11 = (bf16[64,512]{1,0:T(8,128)(2,1)}, bf16[64,512]{1,0:T(8,128)(2,1)S(1)}, u32[]{:S(2)}, u32[]{:S(2)}) collective-permute-start(bf16[64,512]{1,0:T(8,128)(2,1)} %param.13), channel_id=1, source_target_pairs={{0,8},{8,16},{16,24},{24,32},{32,40},{40,48},{48,56},{56,64},{64,7... | collective-permute-start | bytes 196616 | tf_op jit(solution)/shard_map/ppermute | solution.py:24
  21.9 6.9 %collective-permute-start.12 = (bf16[64,512]{1,0:T(8,128)(2,1)}, bf16[64,512]{1,0:T(8,128)(2,1)S(1)}, u32[]{:S(2)}, u32[]{:S(2)}) collective-permute-start(bf16[64,512]{1,0:T(8,128)(2,1)} %param.13), channel_id=1, source_target_pairs={{0,504},{8,0},{16,8},{24,16},{32,24},{40,32},{48,40},{56,48},{64,5... | collective-permute-start | bytes 196616 | tf_op jit(solution)/shard_map/ppermute | solution.py:24
  28.8 2.9 %fusion.103 = (bf16[512,1,128]{2,1,0:T(2,128)(2,1)S(1)}, bf16[512,1,128]{2,1,0:T(2,128)(2,1)S(1)}, bf16[512,1,128]{2,1,0:T(2,128)(2,1)S(1)}, bf16[512,1,128]{2,1,0:T(2,128)(2,1)S(1)}) fusion(bf16[512,4,128]{2,1,0:T(4,128)(2,1)} %param.10), kind=kLoop, calls=%fused_computation.185 | loop fusion | bytes 1048576 | tf_op jit(solution)/shard_map/slice | solution.py:52
  31.6 0.9 fusion.104
  33.5 1.3 fusion.2
  34.7 5.7 %all-to-all-start = ((f32[8,64,512]{2,1,0:T(8,128)}), f32[8,64,512]{2,1,0:T(8,128)S(1)}, u32[]{:S(2)}, u32[]{:S(2)}) async-start(f32[8,64,512]{2,1,0:T(8,128)} %bitcast.9), calls=%async_computation | async-start | bytes 2097152 | tf_op jit(solution)/shard_map/all_to_all | solution.py:17
  42.0 4.3 %collective-permute-start.13 = (bf16[64,512]{1,0:T(8,128)(2,1)S(1)}, bf16[64,512]{1,0:T(8,128)(2,1)S(1)}, u32[]{:S(2)}, u32[]{:S(2)}) collective-permute-start(bf16[64,512]{1,0:T(8,128)(2,1)S(1)} %copy-done.3), channel_id=1, source_target_pairs={{0,496},{8,504},{16,0},{24,8},{32,16},{40,24},{48,32},{56,40},{64,... | collective-permute-start | bytes 196616 | tf_op jit(solution)/shard_map/ppermute | solution.py:24
  46.3 4.5 %collective-permute-start.14 = (bf16[64,512]{1,0:T(8,128)(2,1)S(1)}, bf16[64,512]{1,0:T(8,128)(2,1)S(1)}, u32[]{:S(2)}, u32[]{:S(2)}) collective-permute-start(bf16[64,512]{1,0:T(8,128)(2,1)S(1)} %copy-done.3), channel_id=1, source_target_pairs={{0,488},{8,496},{16,504},{24,0},{32,8},{40,16},{48,24},{56,32},{64... | collective-permute-start | bytes 196616 | tf_op jit(solution)/shard_map/ppermute | solution.py:24
  50.9 3.6 %collective-permute-start.15 = (bf16[64,512]{1,0:T(8,128)(2,1)S(1)}, bf16[64,512]{1,0:T(8,128)(2,1)S(1)}, u32[]{:S(2)}, u32[]{:S(2)}) collective-permute-start(bf16[64,512]{1,0:T(8,128)(2,1)S(1)} %copy-done.3), channel_id=1, source_target_pairs={{0,480},{8,488},{16,496},{24,504},{32,0},{40,8},{48,16},{56,24},{6... | collective-permute-start | bytes 196616 | tf_op jit(solution)/shard_map/ppermute | solution.py:24
  55.5 2.3 %collective-permute-start = (bf16[64,512]{1,0:T(8,128)(2,1)S(1)}, bf16[64,512]{1,0:T(8,128)(2,1)S(1)}, u32[]{:S(2)}, u32[]{:S(2)}) collective-permute-start(bf16[64,512]{1,0:T(8,128)(2,1)S(1)} %select_convert_fusion), channel_id=1, source_target_pairs={{0,32},{8,40},{16,48},{24,56},{32,64},{40,72},{48,80},{56,88},{64,... | collective-permute-start | bytes 196616 | tf_op jit(solution)/shard_map/ppermute | solution.py:24
  58.5 3.3 %collective-permute-start.1 = (bf16[64,512]{1,0:T(8,128)(2,1)S(1)}, bf16[64,512]{1,0:T(8,128)(2,1)S(1)}, u32[]{:S(2)}, u32[]{:S(2)}) collective-permute-start(bf16[64,512]{1,0:T(8,128)(2,1)S(1)} %select_convert_fusion), channel_id=1, source_target_pairs={{0,24},{8,32},{16,40},{24,48},{32,56},{40,64},{48,72},{56,80},{64,... | collective-permute-start | bytes 196616 | tf_op jit(solution)/shard_map/ppermute | solution.py:24
  61.8 3.4 %collective-permute-start.2 = (bf16[64,512]{1,0:T(8,128)(2,1)S(1)}, bf16[64,512]{1,0:T(8,128)(2,1)S(1)}, u32[]{:S(2)}, u32[]{:S(2)}) collective-permute-start(bf16[64,512]{1,0:T(8,128)(2,1)S(1)} %select_convert_fusion), channel_id=1, source_target_pairs={{0,16},{8,24},{16,32},{24,40},{32,48},{40,56},{48,64},{56,72},{64,... | collective-permute-start | bytes 196616 | tf_op jit(solution)/shard_map/ppermute | solution.py:24
  65.3 3.0 %collective-permute-start.3 = (bf16[64,512]{1,0:T(8,128)(2,1)S(1)}, bf16[64,512]{1,0:T(8,128)(2,1)S(1)}, u32[]{:S(2)}, u32[]{:S(2)}) collective-permute-start(bf16[64,512]{1,0:T(8,128)(2,1)S(1)} %select_convert_fusion), channel_id=1, source_target_pairs={{0,8},{8,16},{16,24},{24,32},{32,40},{40,48},{48,56},{56,64},{64,7... | collective-permute-start | bytes 196616 | tf_op jit(solution)/shard_map/ppermute | solution.py:24
  68.3 6.4 %collective-permute-start.4 = (bf16[64,512]{1,0:T(8,128)(2,1)S(1)}, bf16[64,512]{1,0:T(8,128)(2,1)S(1)}, u32[]{:S(2)}, u32[]{:S(2)}) collective-permute-start(bf16[64,512]{1,0:T(8,128)(2,1)S(1)} %select_convert_fusion), channel_id=1, source_target_pairs={{0,504},{8,0},{16,8},{24,16},{32,24},{40,32},{48,40},{56,48},{64,5... | collective-permute-start | bytes 196616 | tf_op jit(solution)/shard_map/ppermute | solution.py:24
  74.7 3.1 %collective-permute-start.5 = (bf16[64,512]{1,0:T(8,128)(2,1)S(1)}, bf16[64,512]{1,0:T(8,128)(2,1)S(1)}, u32[]{:S(2)}, u32[]{:S(2)}) collective-permute-start(bf16[64,512]{1,0:T(8,128)(2,1)S(1)} %select_convert_fusion), channel_id=1, source_target_pairs={{0,496},{8,504},{16,0},{24,8},{32,16},{40,24},{48,32},{56,40},{64,... | collective-permute-start | bytes 196616 | tf_op jit(solution)/shard_map/ppermute | solution.py:24
  77.8 1.9 %collective-permute-start.6 = (bf16[64,512]{1,0:T(8,128)(2,1)S(1)}, bf16[64,512]{1,0:T(8,128)(2,1)S(1)}, u32[]{:S(2)}, u32[]{:S(2)}) collective-permute-start(bf16[64,512]{1,0:T(8,128)(2,1)S(1)} %select_convert_fusion), channel_id=1, source_target_pairs={{0,488},{8,496},{16,504},{24,0},{32,8},{40,16},{48,24},{56,32},{64... | collective-permute-start | bytes 196616 | tf_op jit(solution)/shard_map/ppermute | solution.py:24
  79.8 3.8 %collective-permute-start.7 = (bf16[64,512]{1,0:T(8,128)(2,1)S(1)}, bf16[64,512]{1,0:T(8,128)(2,1)S(1)}, u32[]{:S(2)}, u32[]{:S(2)}) collective-permute-start(bf16[64,512]{1,0:T(8,128)(2,1)S(1)} %select_convert_fusion), channel_id=1, source_target_pairs={{0,480},{8,488},{16,496},{24,504},{32,0},{40,8},{48,16},{56,24},{6... | collective-permute-start | bytes 196616 | tf_op jit(solution)/shard_map/ppermute | solution.py:24
  83.7 1.0 collective-permute-done.6
  86.1 0.9 pad_maximum_fusion
  99.9 0.8 copy.34
  101.5 0.8 copy.36
  102.2 0.7 copy.37
  103.7 0.7 copy.39
  105.4 30.9 %all-gather.2.cloned.1.call-done = bf16[12,512,512]{2,1,0:T(8,128)(2,1)} async-done(((bf16[12,64,512]{2,1,0:T(8,128)(2,1)}), bf16[12,512,512]{2,1,0:T(8,128)(2,1)}) %all-gather.2.cloned.1.call-update) | async-done | bytes 6291472 | tf_op jit(solution)/shard_map/all_gather | solution.py:30
  136.4 1.6 fusion.27
  138.1 1.6 convolution_add_fusion.10
  139.8 1.0 mul.194
  140.8 1.6 convolution_add_fusion.9
  142.4 1.0 mul.197
  143.4 1.6 convolution_add_fusion.8
  145.1 1.0 mul.200
  146.1 1.6 convolution_add_fusion.7
  147.7 1.0 mul.203
  148.7 1.6 convolution_add_fusion.6
  150.4 1.0 mul.206
  151.4 1.6 convolution_add_fusion.5
  153.0 1.0 mul.209
  154.0 1.6 convolution_add_fusion.4
  155.7 1.0 mul.212
  156.7 1.6 convolution_add_fusion.3
  158.3 1.0 mul.215
  159.3 2.6 %convolution_add_fusion.2 = f32[512,512]{0,1:T(8,128)} fusion(f32[512,512]{0,1:T(8,128)S(1)} %convolution_add_fusion.3, f32[32,8,4,128]{3,2,1,0:T(4,128)S(1)} %bitcast.417, bf16[12,512,512]{2,1,0:T(8,128)(2,1)} %all-gather.2.cloned.1.call-done, bf16[64,8,4,128]{3,2,1,0:T(4,128)(2,1)S(1)} %bitcast.404), kind=kOutput, calls=%fused_computation.11 | convolution fusion | flops 268959744 | bytes 3670016 | tf_op jit(solution)/shard_map/dot_general | solution.py:103
  162.0 2.0 %convolution_add_fusion.1 = f32[512,512]{0,1:T(8,128)S(1)} fusion(f32[512,512]{0,1:T(8,128)} %convolution_add_fusion.2, f32[32,8,4,128]{3,2,1,0:T(4,128)S(1)} %bitcast.418, bf16[12,512,512]{2,1,0:T(8,128)(2,1)} %all-gather.2.cloned.1.call-done, bf16[64,8,4,128]{3,2,1,0:T(4,128)(2,1)S(1)} %bitcast.405), kind=kOutput, calls=%fused_computation.10 | convolution fusion | flops 268959744 | bytes 3670016 | tf_op jit(solution)/shard_map/dot_general | solution.py:103
  164.2 1.6 convolution_add_fusion
  165.8 1.3 copy.43
  (80 shorter events, 10.1 us)
Async XLA Ops:
  6.5 26.0 %copy-start = (bf16[512,128]{1,0:T(8,128)(2,1)S(1)}, bf16[512,128]{1,0:T(8,128)(2,1)}, u32[]{:S(2)}) copy-start(bf16[512,128]{1,0:T(8,128)(2,1)} %param.11) | copy-start | bytes 393220
  6.5 35.5 %copy-start.3 = (bf16[64,512]{1,0:T(8,128)(2,1)S(1)}, bf16[64,512]{1,0:T(8,128)(2,1)}, u32[]{:S(2)}) copy-start(bf16[64,512]{1,0:T(8,128)(2,1)} %param.13) | copy-start | bytes 196612
  6.5 33.9 %copy-start.6 = (s32[64]{0:T(128)S(1)}, s32[64]{0:T(128)}, u32[]{:S(2)}) copy-start(s32[64]{0:T(128)} %param.15) | copy-start | bytes 772
  6.5 34.5 %copy-start.5 = (s32[64,6]{0,1:T(8,128)S(1)}, s32[64,6]{0,1:T(8,128)}, u32[]{:S(2)}) copy-start(s32[64,6]{0,1:T(8,128)} %param.16) | copy-start | bytes 4612
  6.5 35.5 %collective-permute-start.8 = (bf16[64,512]{1,0:T(8,128)(2,1)}, bf16[64,512]{1,0:T(8,128)(2,1)S(1)}, u32[]{:S(2)}, u32[]{:S(2)}) collective-permute-start(bf16[64,512]{1,0:T(8,128)(2,1)} %param.13), channel_id=1, source_target_pairs={{0,32},{8,40},{16,48},{24,56},{32,64},{40,72},{48,80},{56,88},{64,... | collective-permute-start | bytes 196616 | tf_op jit(solution)/shard_map/ppermute | solution.py:24
  11.0 35.3 %collective-permute-start.9 = (bf16[64,512]{1,0:T(8,128)(2,1)}, bf16[64,512]{1,0:T(8,128)(2,1)S(1)}, u32[]{:S(2)}, u32[]{:S(2)}) collective-permute-start(bf16[64,512]{1,0:T(8,128)(2,1)} %param.13), channel_id=1, source_target_pairs={{0,24},{8,32},{16,40},{24,48},{32,56},{40,64},{48,72},{56,80},{64,... | collective-permute-start | bytes 196616 | tf_op jit(solution)/shard_map/ppermute | solution.py:24
  15.7 35.2 %collective-permute-start.10 = (bf16[64,512]{1,0:T(8,128)(2,1)}, bf16[64,512]{1,0:T(8,128)(2,1)S(1)}, u32[]{:S(2)}, u32[]{:S(2)}) collective-permute-start(bf16[64,512]{1,0:T(8,128)(2,1)} %param.13), channel_id=1, source_target_pairs={{0,16},{8,24},{16,32},{24,40},{32,48},{40,56},{48,64},{56,72},{64,... | collective-permute-start | bytes 196616 | tf_op jit(solution)/shard_map/ppermute | solution.py:24
  19.3 35.3 %collective-permute-start.11 = (bf16[64,512]{1,0:T(8,128)(2,1)}, bf16[64,512]{1,0:T(8,128)(2,1)S(1)}, u32[]{:S(2)}, u32[]{:S(2)}) collective-permute-start(bf16[64,512]{1,0:T(8,128)(2,1)} %param.13), channel_id=1, source_target_pairs={{0,8},{8,16},{16,24},{24,32},{32,40},{40,48},{48,56},{56,64},{64,7... | collective-permute-start | bytes 196616 | tf_op jit(solution)/shard_map/ppermute | solution.py:24
  21.9 32.7 %collective-permute-start.12 = (bf16[64,512]{1,0:T(8,128)(2,1)}, bf16[64,512]{1,0:T(8,128)(2,1)S(1)}, u32[]{:S(2)}, u32[]{:S(2)}) collective-permute-start(bf16[64,512]{1,0:T(8,128)(2,1)} %param.13), channel_id=1, source_target_pairs={{0,504},{8,0},{16,8},{24,16},{32,24},{40,32},{48,40},{56,48},{64,5... | collective-permute-start | bytes 196616 | tf_op jit(solution)/shard_map/ppermute | solution.py:24
  34.7 52.3 %copy-start.4 = (s32[1,6]{1,0:T(1,128)S(1)}, s32[1,6]{1,0:T(1,128)}, u32[]{:S(2)}) copy-start(s32[1,6]{1,0:T(1,128)} %param.17) | copy-start | bytes 76
  34.7 64.0 %copy-start.2 = (bf16[4,128,512]{2,1,0:T(8,128)(2,1)S(1)}, bf16[4,128,512]{2,1,0:T(8,128)(2,1)}, u32[]{:S(2)}) copy-start(bf16[4,128,512]{2,1,0:T(8,128)(2,1)} %param.14) | copy-start | bytes 1572868
  34.7 20.6 %all-to-all-start = ((f32[8,64,512]{2,1,0:T(8,128)}), f32[8,64,512]{2,1,0:T(8,128)S(1)}, u32[]{:S(2)}, u32[]{:S(2)}) async-start(f32[8,64,512]{2,1,0:T(8,128)} %bitcast.9), calls=%async_computation | async-start | bytes 2097152 | tf_op jit(solution)/shard_map/all_to_all | solution.py:17
  40.4 95.9 %all-gather.2.cloned.1.call-start = ((), (), s32[]{:S(2)}) async-start(), calls=%async_computation.1 | async-start | bytes 7077888 | tf_op jit(solution)/shard_map/all_gather | solution.py:30
  42.0 12.6 %collective-permute-start.13 = (bf16[64,512]{1,0:T(8,128)(2,1)S(1)}, bf16[64,512]{1,0:T(8,128)(2,1)S(1)}, u32[]{:S(2)}, u32[]{:S(2)}) collective-permute-start(bf16[64,512]{1,0:T(8,128)(2,1)S(1)} %copy-done.3), channel_id=1, source_target_pairs={{0,496},{8,504},{16,0},{24,8},{32,16},{40,24},{48,32},{56,40},{64,... | collective-permute-start | bytes 196616 | tf_op jit(solution)/shard_map/ppermute | solution.py:24
  46.3 8.3 %collective-permute-start.14 = (bf16[64,512]{1,0:T(8,128)(2,1)S(1)}, bf16[64,512]{1,0:T(8,128)(2,1)S(1)}, u32[]{:S(2)}, u32[]{:S(2)}) collective-permute-start(bf16[64,512]{1,0:T(8,128)(2,1)S(1)} %copy-done.3), channel_id=1, source_target_pairs={{0,488},{8,496},{16,504},{24,0},{32,8},{40,16},{48,24},{56,32},{64... | collective-permute-start | bytes 196616 | tf_op jit(solution)/shard_map/ppermute | solution.py:24
  50.9 7.0 %collective-permute-start.15 = (bf16[64,512]{1,0:T(8,128)(2,1)S(1)}, bf16[64,512]{1,0:T(8,128)(2,1)S(1)}, u32[]{:S(2)}, u32[]{:S(2)}) collective-permute-start(bf16[64,512]{1,0:T(8,128)(2,1)S(1)} %copy-done.3), channel_id=1, source_target_pairs={{0,480},{8,488},{16,496},{24,504},{32,0},{40,8},{48,16},{56,24},{6... | collective-permute-start | bytes 196616 | tf_op jit(solution)/shard_map/ppermute | solution.py:24
  55.5 19.2 %collective-permute-start = (bf16[64,512]{1,0:T(8,128)(2,1)S(1)}, bf16[64,512]{1,0:T(8,128)(2,1)S(1)}, u32[]{:S(2)}, u32[]{:S(2)}) collective-permute-start(bf16[64,512]{1,0:T(8,128)(2,1)S(1)} %select_convert_fusion), channel_id=1, source_target_pairs={{0,32},{8,40},{16,48},{24,56},{32,64},{40,72},{48,80},{56,88},{64,... | collective-permute-start | bytes 196616 | tf_op jit(solution)/shard_map/ppermute | solution.py:24
  58.5 19.3 %collective-permute-start.1 = (bf16[64,512]{1,0:T(8,128)(2,1)S(1)}, bf16[64,512]{1,0:T(8,128)(2,1)S(1)}, u32[]{:S(2)}, u32[]{:S(2)}) collective-permute-start(bf16[64,512]{1,0:T(8,128)(2,1)S(1)} %select_convert_fusion), channel_id=1, source_target_pairs={{0,24},{8,32},{16,40},{24,48},{32,56},{40,64},{48,72},{56,80},{64,... | collective-permute-start | bytes 196616 | tf_op jit(solution)/shard_map/ppermute | solution.py:24
  61.8 18.0 %collective-permute-start.2 = (bf16[64,512]{1,0:T(8,128)(2,1)S(1)}, bf16[64,512]{1,0:T(8,128)(2,1)S(1)}, u32[]{:S(2)}, u32[]{:S(2)}) collective-permute-start(bf16[64,512]{1,0:T(8,128)(2,1)S(1)} %select_convert_fusion), channel_id=1, source_target_pairs={{0,16},{8,24},{16,32},{24,40},{32,48},{40,56},{48,64},{56,72},{64,... | collective-permute-start | bytes 196616 | tf_op jit(solution)/shard_map/ppermute | solution.py:24
  65.3 18.3 %collective-permute-start.3 = (bf16[64,512]{1,0:T(8,128)(2,1)S(1)}, bf16[64,512]{1,0:T(8,128)(2,1)S(1)}, u32[]{:S(2)}, u32[]{:S(2)}) collective-permute-start(bf16[64,512]{1,0:T(8,128)(2,1)S(1)} %select_convert_fusion), channel_id=1, source_target_pairs={{0,8},{8,16},{16,24},{24,32},{32,40},{40,48},{48,56},{56,64},{64,7... | collective-permute-start | bytes 196616 | tf_op jit(solution)/shard_map/ppermute | solution.py:24
  68.3 15.4 %collective-permute-start.4 = (bf16[64,512]{1,0:T(8,128)(2,1)S(1)}, bf16[64,512]{1,0:T(8,128)(2,1)S(1)}, u32[]{:S(2)}, u32[]{:S(2)}) collective-permute-start(bf16[64,512]{1,0:T(8,128)(2,1)S(1)} %select_convert_fusion), channel_id=1, source_target_pairs={{0,504},{8,0},{16,8},{24,16},{32,24},{40,32},{48,40},{56,48},{64,5... | collective-permute-start | bytes 196616 | tf_op jit(solution)/shard_map/ppermute | solution.py:24
  74.7 9.0 %collective-permute-start.5 = (bf16[64,512]{1,0:T(8,128)(2,1)S(1)}, bf16[64,512]{1,0:T(8,128)(2,1)S(1)}, u32[]{:S(2)}, u32[]{:S(2)}) collective-permute-start(bf16[64,512]{1,0:T(8,128)(2,1)S(1)} %select_convert_fusion), channel_id=1, source_target_pairs={{0,496},{8,504},{16,0},{24,8},{32,16},{40,24},{48,32},{56,40},{64,... | collective-permute-start | bytes 196616 | tf_op jit(solution)/shard_map/ppermute | solution.py:24
  77.8 6.9 %collective-permute-start.6 = (bf16[64,512]{1,0:T(8,128)(2,1)S(1)}, bf16[64,512]{1,0:T(8,128)(2,1)S(1)}, u32[]{:S(2)}, u32[]{:S(2)}) collective-permute-start(bf16[64,512]{1,0:T(8,128)(2,1)S(1)} %select_convert_fusion), channel_id=1, source_target_pairs={{0,488},{8,496},{16,504},{24,0},{32,8},{40,16},{48,24},{56,32},{64... | collective-permute-start | bytes 196616 | tf_op jit(solution)/shard_map/ppermute | solution.py:24
  79.8 5.6 %collective-permute-start.7 = (bf16[64,512]{1,0:T(8,128)(2,1)S(1)}, bf16[64,512]{1,0:T(8,128)(2,1)S(1)}, u32[]{:S(2)}, u32[]{:S(2)}) collective-permute-start(bf16[64,512]{1,0:T(8,128)(2,1)S(1)} %select_convert_fusion), channel_id=1, source_target_pairs={{0,480},{8,488},{16,496},{24,504},{32,0},{40,8},{48,16},{56,24},{6... | collective-permute-start | bytes 196616 | tf_op jit(solution)/shard_map/ppermute | solution.py:24
  85.4 51.0 %copy-start.1 = (bf16[512,4,128]{2,1,0:T(4,128)(2,1)S(1)}, bf16[512,4,128]{2,1,0:T(4,128)(2,1)}, u32[]{:S(2)}) copy-start(bf16[512,4,128]{2,1,0:T(4,128)(2,1)} %param.10) | copy-start | bytes 1572868
Sparse Core Ops, SparseCore 0:
  87.2 49.0 all-gather.1
where the time goes:
time: 175 us; the launch traced here: 174 us
  starting transfers between devices  67.6 us (39%)
  waiting for transfers between devices  33.2 us (19%)
  between operations  25.1 us (14%)
  matrix products  23.3 us (13%)
  local copies, waits for them, and re-layouts  22.4 us (13%)
  other arithmetic  2.38 us (1%)
    ppermute x16, starting transfers between devices, from_behind(): return lax.ppermute(value, axis, pairs)  61.9 us
    all_gather x1, waiting for transfers between devices, side_by_side(): whole = lax.all_gather(both, axis, axis=dim, tiled=True)  30.9 us
    dot_general x12, matrix products, add_block(): lax.dot_general(block_w, tapered, (((0,), (1,)), ((), ())), preferred_ele...  21.1 us
    mul x12, local copies, waits for them, and re-layouts, add_block(): covar.reshape(lev_dev, points, block_size) * scaled[None]  8.33 us
    div x12, local copies, waits for them, and re-layouts, add_block(): scaled = taper.astype(jnp.float32) / jnp.float32(members - 1)  6.33 us
    all_to_all x1, starting transfers between devices, sum_at_owner(): lax.all_to_all(blocks, axis, split_axis=0, concat_axis=0, tiled=True)  5.65 us
  transfers between devices with their start and end apart: 18, of which 4 were waited for; matrix products, arithmetic and copies ran while one was open for 9% of the time, Pallas kernels for 0%

commit v1 on v0

v1 whole, which is shorter than its diff:
```python
import functools

import jax
import jax.numpy as jnp
from jax import lax
from jax.experimental import pallas as pl
from jax.experimental.pallas import tpu as pltpu
from jax.sharding import Mesh
from jax.sharding import PartitionSpec as P

REACH = 4
F32 = jnp.float32
BF16 = jnp.bfloat16
VMEM = pl.BlockSpec(memory_space=pltpu.VMEM)
SMEM = pl.BlockSpec(memory_space=pltpu.SMEM)
NT = (((1,), (1,)), ((), ()))
RELS = 4


def cost(flops, moved):
    return pl.CostEstimate(flops=int(flops), bytes_accessed=int(moved), transcendentals=0)


def move(value, axis, steps):
    count = lax.axis_size(axis)
    return lax.ppermute(value, axis, [(i, (i + steps) % count) for i in range(count)])


def project_body(meta, foot, own, other, w_own, duals, mine, pay1, pay2, pay3, cells, a32, w_oth, acc):
    members = cells.shape[0]
    points = own.shape[1]
    levels = own.shape[0] // members
    owned = duals.shape[0]
    x, c = meta[12], meta[13]
    rows = own.shape[0]
    wide = other[rows:, :].astype(F32)
    half = wide.shape[0] // 2
    w_sum = wide[:half] + wide[half:]
    for j in range(RELS):
        w_oth[j] = w_sum[j * levels : (j + 1) * levels]
    parts = []
    columns = []
    for r in range(RELS):
        chip = lax.rem(x + r, RELS)
        start = pl.multiple_of(chip * 2 * owned + c * owned, owned)
        parts.append(foot[pl.ds(start, owned), :])
        both = jnp.concatenate([w_own[chip], w_oth[chip]], axis=0).T
        columns.append(jnp.where(c == 0, both[:owned], both[owned:]))
    picked = jnp.concatenate(parts, axis=0)
    column = jnp.concatenate(columns, axis=0)
    for h in range(2):
        a32[...] = (own if h == 0 else other)[:rows, :].astype(F32)
        for l in range(levels):
            plane = a32[pl.ds(l, members, stride=levels), :].astype(BF16)
            at = (h * levels + l) * points
            cells[:, at : at + points] = plane
            got = lax.dot_general(picked, plane, NT, preferred_element_type=F32)
            k = h * levels + l
            term = column[:, k : k + 1] * got
            if k == 0:
                acc[...] = term
            else:
                acc[...] += term
    mine[...] = acc[:owned]
    for r, pay in ((1, pay1), (2, pay2), (3, pay3)):
        pay[:owned] = acc[r * owned : (r + 1) * owned].astype(BF16)
        pay[owned:] = duals[...]


def project(meta, foot, own, other, w_own, duals):
    owned, members = duals.shape
    points = foot.shape[1]
    levels = own.shape[0] // members
    pay = jax.ShapeDtypeStruct((2 * owned, members), BF16)
    return pl.pallas_call(
        project_body,
        out_shape=(
            jax.ShapeDtypeStruct((owned, members), F32),
            pay,
            pay,
            pay,
            jax.ShapeDtypeStruct((members, 2 * levels * points), BF16),
        ),
        in_specs=[SMEM] + [VMEM] * 5,
        out_specs=(VMEM,) * 5,
        scratch_shapes=[
            pltpu.VMEM(own.shape, F32),
            pltpu.VMEM((RELS, levels, 2 * owned), F32),
            pltpu.VMEM((RELS * owned, members), F32),
        ],
        cost_estimate=cost(2 * 4 * owned * points * members * 2 * levels, 3e6),
        name="project",
    )(meta, foot, own, other, w_own, duals)


def pick_body(meta, low, mid, high, out):
    owned = out.shape[0] // 6
    for k in range(6):
        place = meta[k]
        group = place // 3
        start = pl.multiple_of(lax.rem(place, 3) * owned, owned)
        for g, source in enumerate((low, mid, high)):

            @pl.when(group == g)
            def _(source=source):
                out[k * owned : (k + 1) * owned] = source[pl.ds(start, owned), :]


def pick(meta, low, mid, high):
    members = mid.shape[1]
    return pl.pallas_call(
        pick_body,
        out_shape=jax.ShapeDtypeStruct((2 * mid.shape[0], members), BF16),
        in_specs=[SMEM] + [VMEM] * 3,
        out_specs=VMEM,
        cost_estimate=cost(1e8, 8e5),
        name="pick",
    )(meta, low, mid, high)


def prepare_body(meta, low, mid, high, taper, dual_t, scaled, sel, tall):
    x, c = meta[12], meta[13]
    members = mid.shape[1]
    owned = sel.shape[0] // 6
    classes = taper.shape[0]
    for q in range(classes):
        tall[q] = taper[q].astype(F32).T / F32(members - 1)
    for r in range(RELS):
        chip = lax.rem(x + r, RELS)
        col = pl.multiple_of(chip * 2 * owned + c * owned, owned)
        for k in range(6):
            place = meta[k]
            group = place // 3
            start = pl.multiple_of(lax.rem(place, 3) * (RELS * owned) + r * owned, owned)
            for g, source in enumerate((low, mid, high)):

                @pl.when(group == g)
                def _(source=source):
                    sel[k * owned : (k + 1) * owned] = source[pl.ds(start, owned), :]

            scaled[r, k * owned : (k + 1) * owned] = tall[meta[6 + k], pl.ds(col, owned), :]
        dual_t[r] = sel[...].T


def prepare(meta, low, mid, high, taper):
    members = mid.shape[1]
    owned = mid.shape[0] // (3 * RELS)
    classes, points, slots = taper.shape
    return pl.pallas_call(
        prepare_body,
        out_shape=(
            jax.ShapeDtypeStruct((RELS, members, 6 * owned), BF16),
            jax.ShapeDtypeStruct((RELS, 6 * owned, points), F32),
        ),
        in_specs=[SMEM] + [VMEM] * 4,
        out_specs=(VMEM, VMEM),
        scratch_shapes=[
            pltpu.VMEM((6 * owned, members), BF16),
            pltpu.VMEM((classes, slots, points), F32),
        ],
        cost_estimate=cost(3e9, 6e6),
        name="prepare",
    )(meta, low, mid, high, taper)


def analyse_body(rel, first, step, rows, cells, dual_t, scaled, *refs):
    out = refs[-1]
    before = refs[0] if len(refs) == 2 else None
    taper = scaled[rel]
    wide = jnp.concatenate([taper] * (step // taper.shape[1]), axis=1)
    for at in range(0, out.shape[1], step):
        covar = jnp.dot(rows[...], cells[:, first + at : first + at + step], preferred_element_type=F32)
        tapered = (covar * wide).astype(BF16)
        gained = jnp.dot(dual_t[rel], tapered, preferred_element_type=F32)
        if before is None:
            out[:, at : at + step] = gained
        else:
            out[:, at : at + step] = before[:, at : at + step] + gained


def analyse(rel, first, width, rows, cells, dual_t, scaled, before=None):
    members = cells.shape[0]
    inputs = [rows, cells, dual_t, scaled] + ([] if before is None else [before])
    return pl.pallas_call(
        functools.partial(analyse_body, rel, first, 256),
        out_shape=jax.ShapeDtypeStruct((members, width), F32),
        in_specs=[VMEM] * len(inputs),
        out_specs=VMEM,
        input_output_aliases={} if before is None else {4: 0},
        cost_estimate=cost(4 * rows.shape[0] * members * width, 4e6),
        name="analyse",
    )(*inputs)


def finish_body(mine, theirs, out):
    members = mine.shape[0]
    levels = out.shape[0] // members
    points = out.shape[1]
    for l in range(levels):
        at = slice(l * points, (l + 1) * points)
        out[pl.ds(l, members, stride=levels), :] = mine[:, at] + theirs[:, at]


def finish(mine, theirs, points):
    return pl.pallas_call(
        finish_body,
        out_shape=jax.ShapeDtypeStruct((mine.size // points, points), F32),
        in_specs=[VMEM] * 2,
        out_specs=VMEM,
        cost_estimate=cost(1e8, 3e6),
        name="finish",
    )(mine, theirs)


def shards(
    anomalies, footprint, weighting, dual_rows, taper_blocks, obs_count, near_tiles, taper_class
):
    members, levels, points = anomalies.shape
    owned = dual_rows.shape[0]
    tile = ("z", "y")
    tile_id = lax.axis_index(tile)
    tile_count = lax.axis_size("z") * lax.axis_size("y")
    x, c = lax.axis_index("x"), lax.axis_index("c")

    own = anomalies.reshape(members * levels, points)
    w_own = weighting.reshape(levels, RELS, 2 * owned).transpose(1, 0, 2)
    w_flat = w_own.reshape(RELS * levels, 2 * owned)
    w_high = w_flat.astype(BF16)
    w_low = (w_flat - w_high.astype(F32)).astype(BF16)
    other = move(jnp.concatenate([own, w_high, w_low], axis=0), "c", 1)

    sources = lax.dynamic_index_in_dim(near_tiles, tile_id, 0, keepdims=False)
    places = (sources - tile_id + REACH) % tile_count
    meta = jnp.concatenate([places, taper_class[0], jnp.stack([x, c])]).astype(jnp.int32)
    slot_ids = (x * 2 + c) * owned + jnp.arange(owned, dtype=jnp.int32)
    present = slot_ids < obs_count[tile_id]

    mine, pay1, pay2, pay3, cells = project(meta, footprint, own, other, w_own, dual_rows)
    got1, got3, got2 = move(pay1, "x", 1), move(pay3, "x", -1), move(pay2, "x", 2)
    observed = (
        mine + got1[:owned].astype(F32) + got3[:owned].astype(F32) + got2[:owned].astype(F32)
    )
    rows_y = jnp.where(present[:, None], observed, 0.0).astype(BF16)
    rows_w = jnp.concatenate([dual_rows, got3[owned:], got2[owned:], got1[owned:]], axis=0)

    y_low, y_high = move(rows_y, tile, 1), move(rows_y, tile, -1)
    w_low, w_high = move(rows_w, tile, 1), move(rows_w, tile, -1)
    y_mid = jnp.concatenate([y_low, rows_y, y_high], axis=0)
    w_mid = jnp.concatenate([w_low, rows_w, w_high], axis=0)
    y_far_low, y_far_high = move(y_mid, tile, 3), move(y_mid, tile, -3)
    w_far_low, w_far_high = move(w_mid, tile, 3), move(w_mid, tile, -3)

    y0 = pick(meta, y_far_low, y_mid, y_far_high)
    y3, y1, y2 = move(y0, "x", 1), move(y0, "x", -1), move(y0, "x", 2)
    dual_t, scaled = prepare(meta, w_far_low, w_mid, w_far_high, taper_blocks)

    width = levels * points
    sums = [None, None]
    for rel, rows in ((0, y0), (3, y3), (1, y1), (2, y2)):
        for h in (1, 0):
            sums[h] = analyse(rel, h * width, width, rows, cells, dual_t, scaled, sums[h])
    theirs = move(sums[1], "c", 1)
    return finish(sums[0], theirs, points).reshape(members, levels, points)


def solution(mesh):
    fine = Mesh(mesh.devices.reshape(16, 4, 4, 2), ("z", "y", "x", "c"))
    tile, level = ("z", "y"), ("x", "c")
    return jax.shard_map(
        shards,
        mesh=fine,
        in_specs=(
            P(None, level, tile),
            P(tile, None),
            P(level, tile),
            P((*tile, *level), None),
            P(),
            P(),
            P(),
            P(tile, None),
        ),
        out_specs=P(None, level, tile),
        check_vma=False,
    )
```

time: 175 us -> 153 us (0.87)
  Pallas kernels: 0 us -> 47.6 us
  between operations: 25.1 us -> 0.34 us
  matrix products: 23.3 us -> 0 us
  local copies, waits for them, and re-layouts: 22.4 us -> 7.18 us
  waiting for transfers between devices: 33.2 us -> 26.1 us
    pallas_call x0 -> x12, Pallas kernels: none -> 47.6 us  [the longest x8 34.9 us: analyse(): pl.pallas_call(functools.partial(analyse_body, rel, first, 256), out_shap...]
    all_gather x1 -> x0, waiting for transfers between devices: 30.9 us -> none  [side_by_side(): whole = lax.all_gather(both, axis, axis=dim, tiled=True)]
    ppermute x16, waiting for transfers between devices: 1.66 us -> 26.1 us  [move(): lax.ppermute(value, axis, [(i, (i + steps) % count) for i in range(count)])]
    dot_general x16 -> x0, matrix products: 23.3 us -> none  [the longest x12 21.1 us: add_block(): lax.dot_general(block_w, tapered, (((0,), (1,)), ((), ())), preferred_ele...]
    mul x12 -> x0, local copies, waits for them, and re-layouts: 8.33 us -> none  [add_block(): covar.reshape(lev_dev, points, block_size) * scaled[None]]
    unnamed x29 -> x37, local copies, waits for them, and re-layouts: 0.13 us -> 6.56 us
    div x12 -> x0, local copies, waits for them, and re-layouts: 6.33 us -> none  [add_block(): scaled = taper.astype(jnp.float32) / jnp.float32(members - 1)]
    all_to_all x1 -> x0, starting transfers between devices: 5.65 us -> none  [sum_at_owner(): lax.all_to_all(blocks, axis, split_axis=0, concat_axis=0, tiled=True)]
  transfers between devices with their start and end apart: 18 -> 16, of which waited for: 4 -> 9; matrix products, arithmetic and copies ran while one was open for 9% -> 1% of each run, Pallas kernels for 0% -> 24%
where the time goes in v1:
time: 153 us; the launch traced here: 151 us
  starting transfers between devices  66.8 us (44%)
  Pallas kernels  47.6 us (31%)
  waiting for transfers between devices  26.1 us (17%)
  local copies, waits for them, and re-layouts  7.18 us (5%)
  other arithmetic  3.41 us (2%)
    ppermute x16, starting transfers between devices, move(): lax.ppermute(value, axis, [(i, (i + steps) % count) for i in range(count)])  66.8 us
    pallas_call x8, Pallas kernels, analyse(): pl.pallas_call(functools.partial(analyse_body, rel, first, 256), out_shap...  34.9 us
    ppermute x16, waiting for transfers between devices, move(): lax.ppermute(value, axis, [(i, (i + steps) % count) for i in range(count)])  26.1 us
    unnamed x37, local copies, waits for them, and re-layouts  6.56 us
    pallas_call x1, Pallas kernels, prepare(): pl.pallas_call(prepare_body, out_shape=(jax.ShapeDtypeStruct((RELS, membe...  4.59 us
    pallas_call x1, Pallas kernels, project(): pl.pallas_call(project_body, out_shape=(jax.ShapeDtypeStruct((owned, memb...  3.36 us
  transfers between devices with their start and end apart: 16, of which 9 were waited for; matrix products, arithmetic and copies ran while one was open for 1% of the time, Pallas kernels for 24%

profile of v1, /device:TPU:1, one launch (start us, length us, event | category | flops | bytes accessed | tf_op | source)
XLA Modules:
  0.0 151.5 jit_solution(2451575887578116443)
XLA Ops:
  0.0 0.8 subtract_convert_fusion
  0.8 1.1 pad_maximum_fusion
  1.9 8.9 %collective-permute-start = (bf16[2080,128]{1,0:T(8,128)(2,1)S(1)}, bf16[2080,128]{1,0:T(8,128)(2,1)S(1)}, u32[]{:S(2)}, u32[]{:S(2)}) collective-permute-start(bf16[2080,128]{1,0:T(8,128)(2,1)S(1)} %pad_maximum_fusion), channel_id=1, source_target_pairs={{0,1},{1,0},{2,3},{3,2},{4,5},{5,4},{6,7},{7,6},{8,9},{9,8},{10,11... | collective-permute-start | bytes 1597448 | tf_op jit(solution)/shard_map/ppermute | solution.py:26
  11.0 0.7 pad_add_fusion.meta
  11.7 0.6 collective-permute-done.other
  12.3 0.8 copy-done.6
  13.1 3.4 %project.1 = (f32[64,512]{1,0:T(8,128)}, bf16[128,512]{1,0:T(8,128)(2,1)}, bf16[128,512]{1,0:T(8,128)(2,1)}, bf16[128,512]{1,0:T(8,128)(2,1)}, bf16[512,1024]{1,0:T(8,128)(2,1)}) custom-call(s32[14]{0:T(128)} %pad_add_fusion.meta, bf16[512,128]{1,0:T(8,128)(2,1)} %foot.1, bf16[2048,128]{1,0:T(8,128)(2,1)} %bitcast.12, bf16[2080,128]{1,0:T(8,128)(2,1)} %copy-done.6, ...), custom_call_target="tpu_custom_call" | custom-call | flops 268435456 | bytes 3000000 | tf_op jit(solution)/shard_map/project/pallas_call | solution.py:75
  16.5 1.9 %collective-permute-start.1 = (bf16[128,512]{1,0:T(8,128)(2,1)}, bf16[128,512]{1,0:T(8,128)(2,1)S(1)}, u32[]{:S(2)}, u32[]{:S(2)}) collective-permute-start(bf16[128,512]{1,0:T(8,128)(2,1)} %get-tuple-element.13), channel_id=1, source_target_pairs={{0,2},{2,4},{4,6},{6,0},{1,3},{3,5},{5,7},{7,1},{8,10},{10,12},{12... | collective-permute-start | bytes 393224 | tf_op jit(solution)/shard_map/ppermute | solution.py:26
  18.4 4.6 %collective-permute-start.2 = (bf16[128,512]{1,0:T(8,128)(2,1)}, bf16[128,512]{1,0:T(8,128)(2,1)S(1)}, u32[]{:S(2)}, u32[]{:S(2)}) collective-permute-start(bf16[128,512]{1,0:T(8,128)(2,1)} %get-tuple-element.14), channel_id=1, source_target_pairs={{0,6},{2,0},{4,2},{6,4},{1,7},{3,1},{5,3},{7,5},{8,14},{10,8},{12,... | collective-permute-start | bytes 393224 | tf_op jit(solution)/shard_map/ppermute | solution.py:26
  23.0 1.9 %collective-permute-start.3 = (bf16[128,512]{1,0:T(8,128)(2,1)}, bf16[128,512]{1,0:T(8,128)(2,1)S(1)}, u32[]{:S(2)}, u32[]{:S(2)}) collective-permute-start(bf16[128,512]{1,0:T(8,128)(2,1)} %get-tuple-element.15), channel_id=1, source_target_pairs={{0,4},{2,6},{4,0},{6,2},{1,5},{3,7},{5,1},{7,3},{8,12},{10,14},{12... | collective-permute-start | bytes 393224 | tf_op jit(solution)/shard_map/ppermute | solution.py:26
  25.5 5.2 %collective-permute-done.3 = bf16[128,512]{1,0:T(8,128)(2,1)S(1)} collective-permute-done((bf16[128,512]{1,0:T(8,128)(2,1)}, bf16[128,512]{1,0:T(8,128)(2,1)S(1)}, u32[]{:S(2)}, u32[]{:S(2)}) %collective-permute-start.3) | collective-permute-done | bytes 131104 | tf_op jit(solution)/shard_map/ppermute | solution.py:26
  30.7 2.1 %collective-permute-start.9 = (bf16[256,512]{1,0:T(8,128)(2,1)S(1)}, bf16[256,512]{1,0:T(8,128)(2,1)S(1)}, u32[]{:S(2)}, u32[]{:S(2)}) collective-permute-start(bf16[256,512]{1,0:T(8,128)(2,1)S(1)} %pad_maximum_fusion.1), channel_id=1, source_target_pairs={{0,8},{8,16},{16,24},{24,32},{32,40},{40,48},{48,56},{56,64},{64,7... | collective-permute-start | bytes 786440 | tf_op jit(solution)/shard_map/ppermute | solution.py:26
  32.8 0.6 dynamic_slice.8
  33.4 8.2 %collective-permute-start.10 = (bf16[256,512]{1,0:T(8,128)(2,1)S(1)}, bf16[256,512]{1,0:T(8,128)(2,1)S(1)}, u32[]{:S(2)}, u32[]{:S(2)}) collective-permute-start(bf16[256,512]{1,0:T(8,128)(2,1)S(1)} %pad_maximum_fusion.1), channel_id=1, source_target_pairs={{0,504},{8,0},{16,8},{24,16},{32,24},{40,32},{48,40},{56,48},{64,5... | collective-permute-start | bytes 786440 | tf_op jit(solution)/shard_map/ppermute | solution.py:26
  41.6 2.4 %collective-permute-done.9 = bf16[256,512]{1,0:T(8,128)(2,1)S(1)} collective-permute-done((bf16[256,512]{1,0:T(8,128)(2,1)S(1)}, bf16[256,512]{1,0:T(8,128)(2,1)S(1)}, u32[]{:S(2)}, u32[]{:S(2)}) %collective-permute-start.9) | collective-permute-done | bytes 262176 | tf_op jit(solution)/shard_map/ppermute | solution.py:26
  44.1 1.4 collective-permute-done.10
  45.5 3.7 %collective-permute-start.12 = (bf16[768,512]{1,0:T(8,128)(2,1)S(1)}, bf16[768,512]{1,0:T(8,128)(2,1)S(1)}, u32[]{:S(2)}, u32[]{:S(2)}) collective-permute-start(bf16[768,512]{1,0:T(8,128)(2,1)S(1)} %constant_dynamic-update-slice_fusion.mid), channel_id=1, source_target_pairs={{0,488},{8,496},{16,504},{24,0},{32,8},{40,16},{48,24},{56,32},{64... | collective-permute-start | bytes 2359304 | tf_op jit(solution)/shard_map/ppermute | solution.py:26
  49.2 2.8 %collective-permute-start.11 = (bf16[768,512]{1,0:T(8,128)(2,1)S(1)}, bf16[768,512]{1,0:T(8,128)(2,1)S(1)}, u32[]{:S(2)}, u32[]{:S(2)}) collective-permute-start(bf16[768,512]{1,0:T(8,128)(2,1)S(1)} %constant_dynamic-update-slice_fusion.mid), channel_id=1, source_target_pairs={{0,24},{8,32},{16,40},{24,48},{32,56},{40,64},{48,72},{56,80},{64,... | collective-permute-start | bytes 2359304 | tf_op jit(solution)/shard_map/ppermute | solution.py:26
  52.0 0.6 add_compare_fusion
  52.7 8.3 %collective-permute-start.5 = (bf16[64,512]{1,0:T(8,128)(2,1)S(1)}, bf16[64,512]{1,0:T(8,128)(2,1)S(1)}, u32[]{:S(2)}, u32[]{:S(2)}) collective-permute-start(bf16[64,512]{1,0:T(8,128)(2,1)S(1)} %select_convert_fusion), channel_id=1, source_target_pairs={{0,504},{8,0},{16,8},{24,16},{32,24},{40,32},{48,40},{56,48},{64,5... | collective-permute-start | bytes 196616 | tf_op jit(solution)/shard_map/ppermute | solution.py:26
  61.0 1.9 %collective-permute-start.4 = (bf16[64,512]{1,0:T(8,128)(2,1)S(1)}, bf16[64,512]{1,0:T(8,128)(2,1)S(1)}, u32[]{:S(2)}, u32[]{:S(2)}) collective-permute-start(bf16[64,512]{1,0:T(8,128)(2,1)S(1)} %select_convert_fusion), channel_id=1, source_target_pairs={{0,8},{8,16},{16,24},{24,32},{32,40},{40,48},{48,56},{56,64},{64,7... | collective-permute-start | bytes 196616 | tf_op jit(solution)/shard_map/ppermute | solution.py:26
  62.9 11.1 %collective-permute-done.5 = bf16[64,512]{1,0:T(8,128)(2,1)S(1)} collective-permute-done((bf16[64,512]{1,0:T(8,128)(2,1)S(1)}, bf16[64,512]{1,0:T(8,128)(2,1)S(1)}, u32[]{:S(2)}, u32[]{:S(2)}) %collective-permute-start.5) | collective-permute-done | bytes 65568 | tf_op jit(solution)/shard_map/ppermute | solution.py:26
  74.3 2.5 %collective-permute-start.7 = (bf16[192,512]{1,0:T(8,128)(2,1)S(1)}, bf16[192,512]{1,0:T(8,128)(2,1)S(1)}, u32[]{:S(2)}, u32[]{:S(2)}) collective-permute-start(bf16[192,512]{1,0:T(8,128)(2,1)S(1)} %pad_maximum_fusion.2.mid), channel_id=1, source_target_pairs={{0,488},{8,496},{16,504},{24,0},{32,8},{40,16},{48,24},{56,32},{64... | collective-permute-start | bytes 589832 | tf_op jit(solution)/shard_map/ppermute | solution.py:26
  76.8 4.0 %collective-permute-start.6 = (bf16[192,512]{1,0:T(8,128)(2,1)S(1)}, bf16[192,512]{1,0:T(8,128)(2,1)S(1)}, u32[]{:S(2)}, u32[]{:S(2)}) collective-permute-start(bf16[192,512]{1,0:T(8,128)(2,1)S(1)} %pad_maximum_fusion.2.mid), channel_id=1, source_target_pairs={{0,24},{8,32},{16,40},{24,48},{32,56},{40,64},{48,72},{56,80},{64,... | collective-permute-start | bytes 589832 | tf_op jit(solution)/shard_map/ppermute | solution.py:26
  80.8 1.1 collective-permute-done.7.high
  81.9 3.4 %collective-permute-done.6.low = bf16[192,512]{1,0:T(8,128)(2,1)S(1)} collective-permute-done((bf16[192,512]{1,0:T(8,128)(2,1)S(1)}, bf16[192,512]{1,0:T(8,128)(2,1)S(1)}, u32[]{:S(2)}, u32[]{:S(2)}) %collective-permute-start.6) | collective-permute-done | bytes 196640 | tf_op jit(solution)/shard_map/ppermute | solution.py:26
  85.4 0.7 copy-done.8
  86.0 2.1 %pick.1.rows = bf16[384,512]{1,0:T(8,128)(2,1)} custom-call(s32[14]{0:T(128)} %pad_add_fusion.meta, bf16[192,512]{1,0:T(8,128)(2,1)} %copy-done.8, bf16[192,512]{1,0:T(8,128)(2,1)} %copy-done.4, bf16[192,512]{1,0:T(8,128)(2,1)} %copy-done.7), custom_call_target="tpu_custom_call" | custom-call | flops 100000000 | bytes 800000 | tf_op jit(solution)/shard_map/pick/pallas_call | solution.py:111
  88.1 1.9 %collective-permute-start.14 = (bf16[384,512]{1,0:T(8,128)(2,1)}, bf16[384,512]{1,0:T(8,128)(2,1)S(1)}, u32[]{:S(2)}, u32[]{:S(2)}) collective-permute-start(bf16[384,512]{1,0:T(8,128)(2,1)} %pick.1.rows), channel_id=1, source_target_pairs={{0,2},{2,4},{4,6},{6,0},{1,3},{3,5},{5,7},{7,1},{8,10},{10,12},{12... | collective-permute-start | bytes 1179656 | tf_op jit(solution)/shard_map/ppermute | solution.py:26
  90.0 4.6 %collective-permute-start.13 = (bf16[384,512]{1,0:T(8,128)(2,1)}, bf16[384,512]{1,0:T(8,128)(2,1)S(1)}, u32[]{:S(2)}, u32[]{:S(2)}) collective-permute-start(bf16[384,512]{1,0:T(8,128)(2,1)} %pick.1.rows), channel_id=1, source_target_pairs={{0,6},{2,0},{4,2},{6,4},{1,7},{3,1},{5,3},{7,5},{8,14},{10,8},{12,... | collective-permute-start | bytes 1179656 | tf_op jit(solution)/shard_map/ppermute | solution.py:26
  94.6 2.2 %collective-permute-start.8 = (bf16[384,512]{1,0:T(8,128)(2,1)}, bf16[384,512]{1,0:T(8,128)(2,1)S(1)}, u32[]{:S(2)}, u32[]{:S(2)}) collective-permute-start(bf16[384,512]{1,0:T(8,128)(2,1)} %pick.1.rows), channel_id=1, source_target_pairs={{0,4},{2,6},{4,0},{6,2},{1,5},{3,7},{5,1},{7,3},{8,12},{10,14},{12... | collective-permute-start | bytes 1179656 | tf_op jit(solution)/shard_map/ppermute | solution.py:26
  96.9 0.9 copy-done.13
  97.8 0.9 copy-done.14
  98.6 4.6 %prepare.1 = (bf16[4,512,384]{2,1,0:T(8,128)(2,1)}, f32[4,384,128]{2,1,0:T(8,128)}) custom-call(s32[14]{0:T(128)} %pad_add_fusion.meta, bf16[768,512]{1,0:T(8,128)(2,1)} %copy-done.14, bf16[768,512]{1,0:T(8,128)(2,1)} %copy-done.10, bf16[768,512]{1,0:T(8,128)(2,1)} %copy-done.13, bf16[4,128,512]{2,1,0:T(8,128)(2,1)} %taper.1), custom_call_target="tpu_custom_call" | custom-call | flops 3000000000 | bytes 6000000 | tf_op jit(solution)/shard_map/prepare/pallas_call | solution.py:149
  103.2 4.1 %analyse.12.refs_0_ = f32[512,512]{1,0:T(8,128)} custom-call(bf16[384,512]{1,0:T(8,128)(2,1)} %pick.1.rows, bf16[512,1024]{1,0:T(8,128)(2,1)} %get-tuple-element.16.cells, bf16[4,512,384]{2,1,0:T(8,128)(2,1)} %get-tuple-element.17.dual_t, f32[4,384,128]{2,1,0:T(8,128)} %get-tuple-element.18.scaled), custom_call_target="tpu_custom_call" | custom-call | flops 402653184 | bytes 4000000 | tf_op jit(solution)/shard_map/analyse/pallas_call | solution.py:184
  107.3 0.8 copy-done
  108.1 4.4 %analyse.13.refs_0_ = f32[512,512]{1,0:T(8,128)} custom-call(bf16[384,512]{1,0:T(8,128)(2,1)} %copy-done, bf16[512,1024]{1,0:T(8,128)(2,1)} %get-tuple-element.16.cells, bf16[4,512,384]{2,1,0:T(8,128)(2,1)} %get-tuple-element.17.dual_t, f32[4,384,128]{2,1,0:T(8,128)} %get-tuple-element.18.scaled, ...), custom_call_target="tpu_custom_call", output_to_operand_aliasing={{}: (4, {})} | custom-call | flops 402653184 | bytes 4000000 | tf_op jit(solution)/shard_map/analyse/pallas_call | solution.py:184
  112.5 0.8 copy-done.1
  113.3 4.4 %analyse.14.refs_0_ = f32[512,512]{1,0:T(8,128)} custom-call(bf16[384,512]{1,0:T(8,128)(2,1)} %copy-done.1, bf16[512,1024]{1,0:T(8,128)(2,1)} %get-tuple-element.16.cells, bf16[4,512,384]{2,1,0:T(8,128)(2,1)} %get-tuple-element.17.dual_t, f32[4,384,128]{2,1,0:T(8,128)} %get-tuple-element.18.scaled, ...), custom_call_target="tpu_custom_call", output_to_operand_aliasing={{}: (4, {})} | custom-call | flops 402653184 | bytes 4000000 | tf_op jit(solution)/shard_map/analyse/pallas_call | solution.py:184
  117.7 0.7 copy-done.2
  118.5 4.4 %analyse.15 = f32[512,512]{1,0:T(8,128)} custom-call(bf16[384,512]{1,0:T(8,128)(2,1)} %copy-done.2, bf16[512,1024]{1,0:T(8,128)(2,1)} %get-tuple-element.16.cells, bf16[4,512,384]{2,1,0:T(8,128)(2,1)} %get-tuple-element.17.dual_t, f32[4,384,128]{2,1,0:T(8,128)} %get-tuple-element.18.scaled, f32[512,512]{1,0:T(8,128)} %analyse.14.refs_0_), custom_call_target="tpu_custom_call", output_to_operand_aliasing={{}: (4, {})} | custom-call | flops 402653184 | bytes 4000000 | tf_op jit(solution)/shard_map/analyse/pallas_call | solution.py:184
  122.9 7.4 %collective-permute-start.15 = (f32[512,512]{1,0:T(8,128)}, f32[512,512]{1,0:T(8,128)S(1)}, u32[]{:S(2)}, u32[]{:S(2)}) collective-permute-start(f32[512,512]{1,0:T(8,128)} %analyse.15), channel_id=1, source_target_pairs={{0,1},{1,0},{2,3},{3,2},{4,5},{5,4},{6,7},{7,6},{8,9},{9,8},{10,11... | collective-permute-start | bytes 3145736 | tf_op jit(solution)/shard_map/ppermute | solution.py:26
  130.3 4.1 %analyse.8.refs_0_ = f32[512,512]{1,0:T(8,128)} custom-call(bf16[384,512]{1,0:T(8,128)(2,1)} %pick.1.rows, bf16[512,1024]{1,0:T(8,128)(2,1)} %get-tuple-element.16.cells, bf16[4,512,384]{2,1,0:T(8,128)(2,1)} %get-tuple-element.17.dual_t, f32[4,384,128]{2,1,0:T(8,128)} %get-tuple-element.18.scaled), custom_call_target="tpu_custom_call" | custom-call | flops 402653184 | bytes 4000000 | tf_op jit(solution)/shard_map/analyse/pallas_call | solution.py:184
  134.4 4.5 %analyse.9.refs_0_ = f32[512,512]{1,0:T(8,128)} custom-call(bf16[384,512]{1,0:T(8,128)(2,1)} %copy-done, bf16[512,1024]{1,0:T(8,128)(2,1)} %get-tuple-element.16.cells, bf16[4,512,384]{2,1,0:T(8,128)(2,1)} %get-tuple-element.17.dual_t, f32[4,384,128]{2,1,0:T(8,128)} %get-tuple-element.18.scaled, ...), custom_call_target="tpu_custom_call", output_to_operand_aliasing={{}: (4, {})} | custom-call | flops 402653184 | bytes 4000000 | tf_op jit(solution)/shard_map/analyse/pallas_call | solution.py:184
  138.9 4.5 %analyse.10.refs_0_ = f32[512,512]{1,0:T(8,128)} custom-call(bf16[384,512]{1,0:T(8,128)(2,1)} %copy-done.1, bf16[512,1024]{1,0:T(8,128)(2,1)} %get-tuple-element.16.cells, bf16[4,512,384]{2,1,0:T(8,128)(2,1)} %get-tuple-element.17.dual_t, f32[4,384,128]{2,1,0:T(8,128)} %get-tuple-element.18.scaled, ...), custom_call_target="tpu_custom_call", output_to_operand_aliasing={{}: (4, {})} | custom-call | flops 402653184 | bytes 4000000 | tf_op jit(solution)/shard_map/analyse/pallas_call | solution.py:184
  143.3 4.5 %analyse.11.mine = f32[512,512]{1,0:T(8,128)} custom-call(bf16[384,512]{1,0:T(8,128)(2,1)} %copy-done.2, bf16[512,1024]{1,0:T(8,128)(2,1)} %get-tuple-element.16.cells, bf16[4,512,384]{2,1,0:T(8,128)(2,1)} %get-tuple-element.17.dual_t, f32[4,384,128]{2,1,0:T(8,128)} %get-tuple-element.18.scaled, ...), custom_call_target="tpu_custom_call", output_to_operand_aliasing={{}: (4, {})} | custom-call | flops 402653184 | bytes 4000000 | tf_op jit(solution)/shard_map/analyse/pallas_call | solution.py:184
  147.8 1.0 copy-done.3
  148.8 2.7 %finish.1 = f32[2048,128]{1,0:T(8,128)} custom-call(f32[512,512]{1,0:T(8,128)} %analyse.11.mine, f32[512,512]{1,0:T(8,128)} %copy-done.3), custom_call_target="tpu_custom_call" | custom-call | flops 100000000 | bytes 3000000 | tf_op jit(solution)/shard_map/finish/pallas_call | solution.py:205
  (47 shorter events, 1.2 us)
Async XLA Ops:
  0.0 10.8 %copy-start.11 = (s32[64,6]{0,1:T(8,128)S(1)}, s32[64,6]{0,1:T(8,128)}, u32[]{:S(2)}) copy-start(s32[64,6]{0,1:T(8,128)} %param.14) | copy-start | bytes 4612
  0.0 11.0 %copy-start.12 = (s32[1,6]{1,0:T(1,128)S(1)}, s32[1,6]{1,0:T(1,128)}, u32[]{:S(2)}) copy-start(s32[1,6]{1,0:T(1,128)} %param.15) | copy-start | bytes 76
  1.9 28.8 %copy-start.5 = (bf16[64,512]{1,0:T(8,128)(2,1)S(1)}, bf16[64,512]{1,0:T(8,128)(2,1)}, u32[]{:S(2)}) copy-start(bf16[64,512]{1,0:T(8,128)(2,1)} %duals.1) | copy-start | bytes 196612
  1.9 10.4 %collective-permute-start = (bf16[2080,128]{1,0:T(8,128)(2,1)S(1)}, bf16[2080,128]{1,0:T(8,128)(2,1)S(1)}, u32[]{:S(2)}, u32[]{:S(2)}) collective-permute-start(bf16[2080,128]{1,0:T(8,128)(2,1)S(1)} %pad_maximum_fusion), channel_id=1, source_target_pairs={{0,1},{1,0},{2,3},{3,2},{4,5},{5,4},{6,7},{7,6},{8,9},{9,8},{10,11... | collective-permute-start | bytes 1597448 | tf_op jit(solution)/shard_map/ppermute | solution.py:26
  12.3 0.8 copy-start.6
  13.1 19.7 %copy-start.15 = (s32[64]{0:T(128)S(1)}, s32[64]{0:T(128)}, u32[]{:S(2)}) copy-start(s32[64]{0:T(128)} %param.13) | copy-start | bytes 772
  16.5 8.4 %collective-permute-start.1 = (bf16[128,512]{1,0:T(8,128)(2,1)}, bf16[128,512]{1,0:T(8,128)(2,1)S(1)}, u32[]{:S(2)}, u32[]{:S(2)}) collective-permute-start(bf16[128,512]{1,0:T(8,128)(2,1)} %get-tuple-element.13), channel_id=1, source_target_pairs={{0,2},{2,4},{4,6},{6,0},{1,3},{3,5},{5,7},{7,1},{8,10},{10,12},{12... | collective-permute-start | bytes 393224 | tf_op jit(solution)/shard_map/ppermute | solution.py:26
  18.4 7.1 %collective-permute-start.2 = (bf16[128,512]{1,0:T(8,128)(2,1)}, bf16[128,512]{1,0:T(8,128)(2,1)S(1)}, u32[]{:S(2)}, u32[]{:S(2)}) collective-permute-start(bf16[128,512]{1,0:T(8,128)(2,1)} %get-tuple-element.14), channel_id=1, source_target_pairs={{0,6},{2,0},{4,2},{6,4},{1,7},{3,1},{5,3},{7,5},{8,14},{10,8},{12,... | collective-permute-start | bytes 393224 | tf_op jit(solution)/shard_map/ppermute | solution.py:26
  23.0 7.7 %collective-permute-start.3 = (bf16[128,512]{1,0:T(8,128)(2,1)}, bf16[128,512]{1,0:T(8,128)(2,1)S(1)}, u32[]{:S(2)}, u32[]{:S(2)}) collective-permute-start(bf16[128,512]{1,0:T(8,128)(2,1)} %get-tuple-element.15), channel_id=1, source_target_pairs={{0,4},{2,6},{4,0},{6,2},{1,5},{3,7},{5,1},{7,3},{8,12},{10,14},{12... | collective-permute-start | bytes 393224 | tf_op jit(solution)/shard_map/ppermute | solution.py:26
  30.7 21.9 %copy-start.9 = (f32[64,512]{1,0:T(8,128)S(1)}, f32[64,512]{1,0:T(8,128)}, u32[]{:S(2)}) copy-start(f32[64,512]{1,0:T(8,128)} %get-tuple-element.12) | copy-start | bytes 393220
  30.7 13.2 %collective-permute-start.9 = (bf16[256,512]{1,0:T(8,128)(2,1)S(1)}, bf16[256,512]{1,0:T(8,128)(2,1)S(1)}, u32[]{:S(2)}, u32[]{:S(2)}) collective-permute-start(bf16[256,512]{1,0:T(8,128)(2,1)S(1)} %pad_maximum_fusion.1), channel_id=1, source_target_pairs={{0,8},{8,16},{16,24},{24,32},{32,40},{40,48},{48,56},{56,64},{64,7... | collective-permute-start | bytes 786440 | tf_op jit(solution)/shard_map/ppermute | solution.py:26
  33.4 12.1 %collective-permute-start.10 = (bf16[256,512]{1,0:T(8,128)(2,1)S(1)}, bf16[256,512]{1,0:T(8,128)(2,1)S(1)}, u32[]{:S(2)}, u32[]{:S(2)}) collective-permute-start(bf16[256,512]{1,0:T(8,128)(2,1)S(1)} %pad_maximum_fusion.1), channel_id=1, source_target_pairs={{0,504},{8,0},{16,8},{24,16},{32,24},{40,32},{48,40},{56,48},{64,5... | collective-permute-start | bytes 786440 | tf_op jit(solution)/shard_map/ppermute | solution.py:26
  45.5 51.4 %copy-start.10 = (bf16[768,512]{1,0:T(8,128)(2,1)}, bf16[768,512]{1,0:T(8,128)(2,1)S(1)}, u32[]{:S(2)}) copy-start(bf16[768,512]{1,0:T(8,128)(2,1)S(1)} %constant_dynamic-update-slice_fusion.mid) | copy-start | bytes 2359300
  45.5 51.3 %collective-permute-start.12 = (bf16[768,512]{1,0:T(8,128)(2,1)S(1)}, bf16[768,512]{1,0:T(8,128)(2,1)S(1)}, u32[]{:S(2)}, u32[]{:S(2)}) collective-permute-start(bf16[768,512]{1,0:T(8,128)(2,1)S(1)} %constant_dynamic-update-slice_fusion.mid), channel_id=1, source_target_pairs={{0,488},{8,496},{16,504},{24,0},{32,8},{40,16},{48,24},{56,32},{64... | collective-permute-start | bytes 2359304 | tf_op jit(solution)/shard_map/ppermute | solution.py:26
  49.2 47.7 %collective-permute-start.11 = (bf16[768,512]{1,0:T(8,128)(2,1)S(1)}, bf16[768,512]{1,0:T(8,128)(2,1)S(1)}, u32[]{:S(2)}, u32[]{:S(2)}) collective-permute-start(bf16[768,512]{1,0:T(8,128)(2,1)S(1)} %constant_dynamic-update-slice_fusion.mid), channel_id=1, source_target_pairs={{0,24},{8,32},{16,40},{24,48},{32,56},{40,64},{48,72},{56,80},{64,... | collective-permute-start | bytes 2359304 | tf_op jit(solution)/shard_map/ppermute | solution.py:26
  52.7 21.4 %collective-permute-start.5 = (bf16[64,512]{1,0:T(8,128)(2,1)S(1)}, bf16[64,512]{1,0:T(8,128)(2,1)S(1)}, u32[]{:S(2)}, u32[]{:S(2)}) collective-permute-start(bf16[64,512]{1,0:T(8,128)(2,1)S(1)} %select_convert_fusion), channel_id=1, source_target_pairs={{0,504},{8,0},{16,8},{24,16},{32,24},{40,32},{48,40},{56,48},{64,5... | collective-permute-start | bytes 196616 | tf_op jit(solution)/shard_map/ppermute | solution.py:26
  61.0 13.3 %collective-permute-start.4 = (bf16[64,512]{1,0:T(8,128)(2,1)S(1)}, bf16[64,512]{1,0:T(8,128)(2,1)S(1)}, u32[]{:S(2)}, u32[]{:S(2)}) collective-permute-start(bf16[64,512]{1,0:T(8,128)(2,1)S(1)} %select_convert_fusion), channel_id=1, source_target_pairs={{0,8},{8,16},{16,24},{24,32},{32,40},{40,48},{48,56},{56,64},{64,7... | collective-permute-start | bytes 196616 | tf_op jit(solution)/shard_map/ppermute | solution.py:26
  74.3 11.1 %copy-start.4 = (bf16[192,512]{1,0:T(8,128)(2,1)}, bf16[192,512]{1,0:T(8,128)(2,1)S(1)}, u32[]{:S(2)}) copy-start(bf16[192,512]{1,0:T(8,128)(2,1)S(1)} %pad_maximum_fusion.2.mid) | copy-start | bytes 589828
  74.3 7.6 %collective-permute-start.7 = (bf16[192,512]{1,0:T(8,128)(2,1)S(1)}, bf16[192,512]{1,0:T(8,128)(2,1)S(1)}, u32[]{:S(2)}, u32[]{:S(2)}) collective-permute-start(bf16[192,512]{1,0:T(8,128)(2,1)S(1)} %pad_maximum_fusion.2.mid), channel_id=1, source_target_pairs={{0,488},{8,496},{16,504},{24,0},{32,8},{40,16},{48,24},{56,32},{64... | collective-permute-start | bytes 589832 | tf_op jit(solution)/shard_map/ppermute | solution.py:26
  76.8 8.5 %collective-permute-start.6 = (bf16[192,512]{1,0:T(8,128)(2,1)S(1)}, bf16[192,512]{1,0:T(8,128)(2,1)S(1)}, u32[]{:S(2)}, u32[]{:S(2)}) collective-permute-start(bf16[192,512]{1,0:T(8,128)(2,1)S(1)} %pad_maximum_fusion.2.mid), channel_id=1, source_target_pairs={{0,24},{8,32},{16,40},{24,48},{32,56},{40,64},{48,72},{56,80},{64,... | collective-permute-start | bytes 589832 | tf_op jit(solution)/shard_map/ppermute | solution.py:26
  81.9 3.4 %copy-start.7 = (bf16[192,512]{1,0:T(8,128)(2,1)}, bf16[192,512]{1,0:T(8,128)(2,1)S(1)}, u32[]{:S(2)}) copy-start(bf16[192,512]{1,0:T(8,128)(2,1)S(1)} %collective-permute-done.7.high) | copy-start | bytes 589828
  85.4 0.7 copy-start.8
  88.1 19.2 %collective-permute-start.14 = (bf16[384,512]{1,0:T(8,128)(2,1)}, bf16[384,512]{1,0:T(8,128)(2,1)S(1)}, u32[]{:S(2)}, u32[]{:S(2)}) collective-permute-start(bf16[384,512]{1,0:T(8,128)(2,1)} %pick.1.rows), channel_id=1, source_target_pairs={{0,2},{2,4},{4,6},{6,0},{1,3},{3,5},{5,7},{7,1},{8,10},{10,12},{12... | collective-permute-start | bytes 1179656 | tf_op jit(solution)/shard_map/ppermute | solution.py:26
  90.0 22.5 %collective-permute-start.13 = (bf16[384,512]{1,0:T(8,128)(2,1)}, bf16[384,512]{1,0:T(8,128)(2,1)S(1)}, u32[]{:S(2)}, u32[]{:S(2)}) collective-permute-start(bf16[384,512]{1,0:T(8,128)(2,1)} %pick.1.rows), channel_id=1, source_target_pairs={{0,6},{2,0},{4,2},{6,4},{1,7},{3,1},{5,3},{7,5},{8,14},{10,8},{12,... | collective-permute-start | bytes 1179656 | tf_op jit(solution)/shard_map/ppermute | solution.py:26
  94.6 23.1 %collective-permute-start.8 = (bf16[384,512]{1,0:T(8,128)(2,1)}, bf16[384,512]{1,0:T(8,128)(2,1)S(1)}, u32[]{:S(2)}, u32[]{:S(2)}) collective-permute-start(bf16[384,512]{1,0:T(8,128)(2,1)} %pick.1.rows), channel_id=1, source_target_pairs={{0,4},{2,6},{4,0},{6,2},{1,5},{3,7},{5,1},{7,3},{8,12},{10,14},{12... | collective-permute-start | bytes 1179656 | tf_op jit(solution)/shard_map/ppermute | solution.py:26
  96.8 0.9 copy-start.13
  97.7 0.9 copy-start.14
  107.3 0.8 copy-start
  112.5 0.8 copy-start.1
  117.7 0.7 copy-start.2
  122.9 24.9 %collective-permute-start.15 = (f32[512,512]{1,0:T(8,128)}, f32[512,512]{1,0:T(8,128)S(1)}, u32[]{:S(2)}, u32[]{:S(2)}) collective-permute-start(f32[512,512]{1,0:T(8,128)} %analyse.15), channel_id=1, source_target_pairs={{0,1},{1,0},{2,3},{3,2},{4,5},{5,4},{6,7},{7,6},{8,9},{9,8},{10,11... | collective-permute-start | bytes 3145736 | tf_op jit(solution)/shard_map/ppermute | solution.py:26
  147.8 1.0 copy-start.3

commit v2 on v0

v2 whole, which is shorter than its diff:
```python
import functools

import jax
import jax.numpy as jnp
from jax import lax
from jax.experimental import pallas as pl
from jax.experimental.pallas import tpu as pltpu
from jax.sharding import Mesh
from jax.sharding import PartitionSpec as P

REACH = 4
NEAR = 6
RELS = 4
F32 = jnp.float32
BF16 = jnp.bfloat16
VMEM = pl.BlockSpec(memory_space=pltpu.VMEM)
SMEM = pl.BlockSpec(memory_space=pltpu.SMEM)
NT = (((1,), (1,)), ((), ()))
CLASS, CHIP, CORE, LEFT = 6, 12, 13, 14


def kernel(body, out, inputs, flops, scalars=True, scratch=(), aliases=None, final=False):
    kept = [pltpu.with_memory_space_constraint(a, pltpu.VMEM) for a in inputs[scalars:]]
    shapes = [o if final else pltpu.VMEM(o.shape, o.dtype) for o in out]
    return pl.pallas_call(
        body,
        out_shape=shapes,
        in_specs=[SMEM] * scalars + [VMEM] * len(kept),
        out_specs=[VMEM] * len(out),
        scratch_shapes=list(scratch),
        input_output_aliases=aliases or {},
        cost_estimate=pl.CostEstimate(flops=int(flops), bytes_accessed=int(1e6), transcendentals=0),
        compiler_params=pltpu.CompilerParams(vmem_limit_bytes=16 << 20),
    )(*inputs[:scalars], *kept)


def array(shape, kind):
    return jax.ShapeDtypeStruct(shape, kind)


def move(value, axis, steps):
    count = lax.axis_size(axis)
    return lax.ppermute(value, axis, [(i, (i + steps) % count) for i in range(count)])


def pack_body(raw, weights, out, wide):
    members = out.shape[0] - 16
    levels, slots = weights.shape
    points = raw.shape[1]
    wide[...] = raw[...].astype(F32)
    for l in range(levels):
        plane = wide[pl.ds(l, members, stride=levels), :].astype(BF16)
        out[:members, l * points : (l + 1) * points] = plane
    high = weights[...].astype(BF16).astype(F32)
    low = weights[...] - high
    pad = jnp.zeros((16 - 2 * levels, slots), F32)
    out[members:, :] = jnp.concatenate([high, low, pad], axis=0).astype(BF16)


def columns(meta, weights, owned):
    parts = []
    for r in range(RELS):
        chip = lax.rem(meta[CHIP] + r, RELS)
        block = weights(pl.ds(pl.multiple_of(chip * 2 * owned, 2 * owned), 2 * owned))
        flipped = jnp.concatenate([block, block], axis=0).T
        parts.append(jnp.where(meta[CORE] == 0, flipped[:owned], flipped[owned:]))
    return jnp.concatenate(parts, axis=0)


def rows_of(meta, foot, owned):
    parts = []
    for r in range(RELS):
        chip = lax.rem(meta[CHIP] + r, RELS)
        start = pl.multiple_of(chip * 2 * owned + meta[CORE] * owned, owned)
        parts.append(foot[pl.ds(start, owned), :])
    return jnp.concatenate(parts, axis=0)


def project(picked, column, cells, acc, fresh):
    members = acc.shape[1]
    points = picked.shape[1]
    for l in range(cells.shape[1] // points):
        plane = cells[:members, l * points : (l + 1) * points]
        got = lax.dot_general(picked, plane, NT, preferred_element_type=F32)
        term = column[:, l : l + 1] * got
        if l == 0 and fresh:
            acc[...] = term
        else:
            acc[...] += term


def own_body(meta, foot, cells, weights, out):
    owned = out.shape[0] // RELS
    column = columns(meta, lambda at: weights[:, at], owned)
    project(rows_of(meta, foot, owned), column, cells, out, True)


def other_body(meta, foot, cells, before, duals, mine, pay1, pay2, pay3, acc):
    owned, members = duals.shape

    def weights(at):
        terms = cells[members:, at].astype(F32)
        return terms[:4] + terms[4:8]

    acc[...] = before[...]
    project(rows_of(meta, foot, owned), columns(meta, weights, owned), cells, acc, False)
    mine[...] = acc[:owned]
    for r, pay in ((1, pay1), (2, pay2), (3, pay3)):
        part = acc[r * owned : (r + 1) * owned]
        high = part.astype(BF16)
        pay[:owned] = high
        pay[owned : 2 * owned] = (part - high.astype(F32)).astype(BF16)
        pay[2 * owned :] = duals[...]


def fold_body(meta, mine, *refs):
    out = refs[-1]
    owned = out.shape[0]
    total = mine[...]
    for got in refs[:-1]:
        total = total + (got[:owned].astype(F32) + got[owned : 2 * owned].astype(F32))
    slot = lax.broadcasted_iota(jnp.int32, total.shape, 0)
    out[...] = jnp.where(slot < meta[LEFT], total, 0.0).astype(BF16)


def flip_body(duals, after, across, before, out):
    owned = duals.shape[0]
    rows = [duals[...]] + [got[2 * owned :] for got in (after, across, before)]
    out[...] = jnp.concatenate(rows, axis=0).T


def choose(meta, k, sources, size, store):
    group = meta[k] // 3
    start = pl.multiple_of(lax.rem(meta[k], 3) * size, size)
    for g, source in enumerate(sources):

        @pl.when(group == g)
        def _(source=source):
            store(source[pl.ds(start, size), :])


def pick_body(meta, low, mid, high, out):
    size = out.shape[0] // NEAR
    for k in range(NEAR):

        def store(value, k=k):
            out[k * size : (k + 1) * size] = value

        choose(meta, k, (low, mid, high), size, store)


def pick_dual_body(meta, low, mid, high, out):
    size = out.shape[0]
    wide = out.shape[1] // NEAR
    for k in range(NEAR):

        def store(value, k=k):
            out[:, k * wide : (k + 1) * wide] = value

        choose(meta, k, (low, mid, high), size, store)


def taper_body(meta, taper, out, tall):
    classes = taper.shape[0]
    owned = out.shape[1] // NEAR
    for q in range(classes):
        tall[q] = taper[q].astype(F32).T / F32(511)
    for r in range(RELS):
        chip = lax.rem(meta[CHIP] + r, RELS)
        start = pl.multiple_of(chip * 2 * owned + meta[CORE] * owned, owned)
        for k in range(NEAR):
            out[r, k * owned : (k + 1) * owned] = tall[meta[CLASS + k], pl.ds(start, owned), :]


def covary_body(rel, rows, own, other, scaled, *refs):
    out = refs[-1]
    members = rows.shape[1]
    size = rows.shape[0] // NEAR
    half = own.shape[1]
    step = 256
    taper = scaled[rel]
    wide = jnp.concatenate([taper] * (step // taper.shape[1]), axis=1)
    for h, cells in enumerate((own, other)):
        for at in range(0, half, step):
            covar = jnp.dot(rows[...], cells[:members, at : at + step], preferred_element_type=F32)
            tapered = (covar * wide).astype(BF16)
            for k in range(NEAR):
                first = (k * RELS + rel) * size
                out[first : first + size, h * half + at : h * half + at + step] = tapered[
                    k * size : (k + 1) * size
                ]


def gain_body(h, duals, tapered, out):
    half = out.shape[1]
    step = 256
    for at in range(0, half, step):
        out[:, at : at + step] = jnp.dot(
            duals[...], tapered[:, h * half + at : h * half + at + step], preferred_element_type=F32
        )


def finish_body(mine, theirs, out):
    members = mine.shape[0]
    levels = out.shape[0] // members
    points = out.shape[1]
    for l in range(levels):
        at = slice(l * points, (l + 1) * points)
        out[pl.ds(l, members, stride=levels), :] = mine[:, at] + theirs[:, at]


def shards(
    anomalies, footprint, weighting, dual_rows, taper_blocks, obs_count, near_tiles, taper_class
):
    members, levels, points = anomalies.shape
    owned = dual_rows.shape[0]
    tile = ("z", "y")
    tile_id = lax.axis_index(tile)
    tile_count = lax.axis_size("z") * lax.axis_size("y")
    x, c = lax.axis_index("x"), lax.axis_index("c")

    raw = anomalies.reshape(members * levels, points)
    (own,) = kernel(
        pack_body,
        [array((members + 16, levels * points), BF16)],
        [raw, weighting],
        1e8,
        scalars=False,
        scratch=[pltpu.VMEM(raw.shape, F32)],
    )
    other = move(own, "c", 1)

    sources = lax.dynamic_index_in_dim(near_tiles, tile_id, 0, keepdims=False)
    places = (sources - tile_id + REACH) % tile_count
    left = obs_count[tile_id] - (x * 2 + c) * owned
    meta = jnp.concatenate([places, taper_class[0], jnp.stack([x, c, left, left])]).astype(jnp.int32)

    rows = RELS * owned
    work = 2 * rows * points * members * levels
    (begun,) = kernel(
        own_body, [array((rows, members), F32)], [meta, footprint, own, weighting], work
    )
    pay = array((3 * owned, members), BF16)
    mine, pay1, pay2, pay3 = kernel(
        other_body,
        [array((owned, members), F32), pay, pay, pay],
        [meta, footprint, other, begun, dual_rows],
        work,
        scratch=[pltpu.VMEM((rows, members), F32)],
    )
    got1, got3, got2 = move(pay1, "x", 1), move(pay3, "x", -1), move(pay2, "x", 2)
    (rows_y,) = kernel(
        fold_body, [array((owned, members), BF16)], [meta, mine, got1, got3, got2], 1e8
    )
    y_low, y_high = move(rows_y, tile, 1), move(rows_y, tile, -1)
    (dual_t,) = kernel(
        flip_body, [array((members, rows), BF16)], [dual_rows, got3, got2, got1], 1e8, scalars=False
    )
    y_mid = jnp.concatenate([y_low, rows_y, y_high], axis=0)
    y_far_low, y_far_high = move(y_mid, tile, 3), move(y_mid, tile, -3)
    w_low, w_high = move(dual_t, tile, 1), move(dual_t, tile, -1)
    (y0,) = kernel(
        pick_body, [array((NEAR * owned, members), BF16)], [meta, y_far_low, y_mid, y_far_high], 1e8
    )
    y3, y1, y2 = move(y0, "x", 1), move(y0, "x", -1), move(y0, "x", 2)
    w_mid = jnp.concatenate([w_low, dual_t, w_high], axis=0)
    w_far_low, w_far_high = move(w_mid, tile, 3), move(w_mid, tile, -3)

    meta_late, _ = lax.optimization_barrier((meta, y0))
    (scaled,) = kernel(
        taper_body,
        [array((RELS, NEAR * owned, points), F32)],
        [meta_late, taper_blocks],
        1e9,
        scratch=[pltpu.VMEM((taper_blocks.shape[0], taper_blocks.shape[2], points), F32)],
    )
    width = levels * points
    tapered = None
    for rel, got in ((0, y0), (3, y3), (1, y1), (2, y2)):
        inputs = [got, own, other, scaled] + ([] if tapered is None else [tapered])
        (tapered,) = kernel(
            functools.partial(covary_body, rel),
            [array((NEAR * rows, 2 * width), BF16)],
            inputs,
            4 * NEAR * owned * members * width,
            scalars=False,
            aliases={} if tapered is None else {4: 0},
        )
    (duals,) = kernel(
        pick_dual_body,
        [array((members, NEAR * rows), BF16)],
        [meta, w_far_low, w_mid, w_far_high],
        1e8,
    )
    sums = [
        kernel(
            functools.partial(gain_body, h),
            [array((members, width), F32)],
            [duals, tapered],
            2 * NEAR * rows * members * width,
            scalars=False,
        )[0]
        for h in (0, 1)
    ]
    theirs = move(sums[1], "c", 1)
    (out,) = kernel(
        finish_body,
        [array((members * levels, points), F32)],
        [sums[0], theirs],
        1e8,
        scalars=False,
        final=True,
    )
    return out.reshape(members, levels, points)


def solution(mesh):
    fine = Mesh(mesh.devices.reshape(16, 4, 4, 2), ("z", "y", "x", "c"))
    tile, level = ("z", "y"), ("x", "c")
    return jax.shard_map(
        shards,
        mesh=fine,
        in_specs=(
            P(None, level, tile),
            P(tile, None),
            P(level, tile),
            P((*tile, *level), None),
            P(),
            P(),
            P(),
            P(tile, None),
        ),
        out_specs=P(None, level, tile),
        check_vma=False,
    )
```

time: 175 us -> 118 us (0.67)
  between operations: 25.1 us -> 0.97 us
  matrix products: 23.3 us -> 0 us
  local copies, waits for them, and re-layouts: 22.4 us -> 5.36 us
  Pallas kernels: 0 us -> 10.8 us
  waiting for transfers between devices: 33.2 us -> 29.4 us
  starting transfers between devices: 67.6 us -> 69.4 us
    all_gather x1 -> x0, waiting for transfers between devices: 30.9 us -> none  [side_by_side(): whole = lax.all_gather(both, axis, axis=dim, tiled=True)]
    ppermute x16, waiting for transfers between devices: 1.66 us -> 29.4 us  [move(): lax.ppermute(value, axis, [(i, (i + steps) % count) for i in range(count)])]
    dot_general x16 -> x0, matrix products: 23.3 us -> none  [the longest x12 21.1 us: add_block(): lax.dot_general(block_w, tapered, (((0,), (1,)), ((), ())), preferred_ele...]
    pallas_call x0 -> x15, Pallas kernels: none -> 10.8 us  [kernel(): pl.pallas_call(body, out_shape=shapes, in_specs=[SMEM] * scalars + [VMEM]...]
    mul x12 -> x0, local copies, waits for them, and re-layouts: 8.33 us -> none  [add_block(): covar.reshape(lev_dev, points, block_size) * scaled[None]]
    ppermute x16, starting transfers between devices: 61.9 us -> 69.4 us  [move(): lax.ppermute(value, axis, [(i, (i + steps) % count) for i in range(count)])]
    div x12 -> x0, local copies, waits for them, and re-layouts: 6.33 us -> none  [add_block(): scaled = taper.astype(jnp.float32) / jnp.float32(members - 1)]
    all_to_all x1 -> x0, starting transfers between devices: 5.65 us -> none  [sum_at_owner(): lax.all_to_all(blocks, axis, split_axis=0, concat_axis=0, tiled=True)]
  transfers between devices with their start and end apart: 18 -> 16, of which waited for: 4 -> 9; matrix products, arithmetic and copies ran while one was open for 9% -> 3% of each run, Pallas kernels for 0% -> 6%
where the time goes in v2:
time: 118 us; the launch traced here: 117 us
  starting transfers between devices  69.4 us (59%)
  waiting for transfers between devices  29.4 us (25%)
  Pallas kernels  10.8 us (9%)
  local copies, waits for them, and re-layouts  5.36 us (5%)
    ppermute x16, starting transfers between devices, move(): lax.ppermute(value, axis, [(i, (i + steps) % count) for i in range(count)])  69.4 us
    ppermute x16, waiting for transfers between devices, move(): lax.ppermute(value, axis, [(i, (i + steps) % count) for i in range(count)])  29.4 us
    pallas_call x15, Pallas kernels, kernel(): pl.pallas_call(body, out_shape=shapes, in_specs=[SMEM] * scalars + [VMEM]...  10.8 us
    unnamed x12, local copies, waits for them, and re-layouts  3.35 us
  transfers between devices with their start and end apart: 16, of which 9 were waited for; matrix products, arithmetic and copies ran while one was open for 3% of the time, Pallas kernels for 6%

profile of v2, /device:TPU:1, one launch (start us, length us, event | category | flops | bytes accessed | tf_op | source)
XLA Modules:
  0.0 116.9 jit_solution(801837374043501020)
XLA Ops:
  0.0 1.0 copy-done.1
  1.0 0.7 copy-done.3
  1.7 0.2 shard_map.82.cells.own
  1.9 8.7 %collective-permute-start = (bf16[528,512]{1,0:T(8,128)(2,1)S(1)}, bf16[528,512]{1,0:T(8,128)(2,1)S(1)}, u32[]{:S(2)}, u32[]{:S(2)}) collective-permute-start(bf16[528,512]{1,0:T(8,128)(2,1)S(1)} %shard_map.82.cells.own), channel_id=1, source_target_pairs={{0,1},{1,0},{2,3},{3,2},{4,5},{5,4},{6,7},{7,6},{8,9},{9,8},{10,11... | collective-permute-start | bytes 1622024 | tf_op jit(solution)/shard_map/ppermute | solution.py:43
  10.7 1.3 %dynamic_slice.8 = s32[1]{0:T(128)} dynamic-slice(s32[64]{0:T(128)} %param.13, s32[]{:T(128)S(6)} %select_n.12), dynamic_slice_sizes={1} | dynamic-slice | bytes 12 | tf_op jit(solution)/shard_map/dynamic_slice | solution.py:235
  12.6 0.9 add_reduce_fusion
  13.5 0.7 concatenate.9.meta
  14.2 0.9 copy-done
  15.1 0.7 copy-done.4
  15.8 1.0 shard_map.83.before
  16.9 1.1 shard_map.84
  18.0 1.9 %collective-permute-start.1 = (bf16[192,512]{1,0:T(8,128)(2,1)S(1)}, bf16[192,512]{1,0:T(8,128)(2,1)S(1)}, u32[]{:S(2)}, u32[]{:S(2)}) collective-permute-start(bf16[192,512]{1,0:T(8,128)(2,1)S(1)} %get-tuple-element.10), channel_id=1, source_target_pairs={{0,6},{2,0},{4,2},{6,4},{1,7},{3,1},{5,3},{7,5},{8,14},{10,8},{12,... | collective-permute-start | bytes 589832 | tf_op jit(solution)/shard_map/ppermute | solution.py:43
  19.9 1.9 %collective-permute-start.2 = (bf16[192,512]{1,0:T(8,128)(2,1)S(1)}, bf16[192,512]{1,0:T(8,128)(2,1)S(1)}, u32[]{:S(2)}, u32[]{:S(2)}) collective-permute-start(bf16[192,512]{1,0:T(8,128)(2,1)S(1)} %get-tuple-element.11), channel_id=1, source_target_pairs={{0,4},{2,6},{4,0},{6,2},{1,5},{3,7},{5,1},{7,3},{8,12},{10,14},{12... | collective-permute-start | bytes 589832 | tf_op jit(solution)/shard_map/ppermute | solution.py:43
  21.8 3.4 %collective-permute-start.3 = (bf16[192,512]{1,0:T(8,128)(2,1)S(1)}, bf16[192,512]{1,0:T(8,128)(2,1)S(1)}, u32[]{:S(2)}, u32[]{:S(2)}) collective-permute-start(bf16[192,512]{1,0:T(8,128)(2,1)S(1)} %get-tuple-element.12), channel_id=1, source_target_pairs={{0,2},{2,4},{4,6},{6,0},{1,3},{3,5},{5,7},{7,1},{8,10},{10,12},{12... | collective-permute-start | bytes 589832 | tf_op jit(solution)/shard_map/ppermute | solution.py:43
  25.2 1.1 collective-permute-done.1.after.refs_1_
  26.3 3.4 %collective-permute-done.2.across.refs_2_ = bf16[192,512]{1,0:T(8,128)(2,1)S(1)} collective-permute-done((bf16[192,512]{1,0:T(8,128)(2,1)S(1)}, bf16[192,512]{1,0:T(8,128)(2,1)S(1)}, u32[]{:S(2)}, u32[]{:S(2)}) %collective-permute-start.2) | collective-permute-done | bytes 196640 | tf_op jit(solution)/shard_map/ppermute | solution.py:43
  29.8 4.6 %collective-permute-done.3.before.refs_0_ = bf16[192,512]{1,0:T(8,128)(2,1)S(1)} collective-permute-done((bf16[192,512]{1,0:T(8,128)(2,1)S(1)}, bf16[192,512]{1,0:T(8,128)(2,1)S(1)}, u32[]{:S(2)}, u32[]{:S(2)}) %collective-permute-start.3) | collective-permute-done | bytes 196640 | tf_op jit(solution)/shard_map/ppermute | solution.py:43
  34.4 0.1 shard_map.85
  34.5 1.9 %collective-permute-start.4 = (bf16[512,256]{1,0:T(8,128)(2,1)S(1)}, bf16[512,256]{1,0:T(8,128)(2,1)S(1)}, u32[]{:S(2)}, u32[]{:S(2)}) collective-permute-start(bf16[512,256]{1,0:T(8,128)(2,1)S(1)} %shard_map.85), channel_id=1, source_target_pairs={{0,8},{8,16},{16,24},{24,32},{32,40},{40,48},{48,56},{56,64},{64,7... | collective-permute-start | bytes 786440 | tf_op jit(solution)/shard_map/ppermute | solution.py:43
  36.4 10.7 %collective-permute-start.5 = (bf16[512,256]{1,0:T(8,128)(2,1)S(1)}, bf16[512,256]{1,0:T(8,128)(2,1)S(1)}, u32[]{:S(2)}, u32[]{:S(2)}) collective-permute-start(bf16[512,256]{1,0:T(8,128)(2,1)S(1)} %shard_map.85), channel_id=1, source_target_pairs={{0,504},{8,0},{16,8},{24,16},{32,24},{40,32},{48,40},{56,48},{64,5... | collective-permute-start | bytes 786440 | tf_op jit(solution)/shard_map/ppermute | solution.py:43
  47.1 0.6 shard_map.87
  47.7 2.1 %collective-permute-start.8 = (bf16[64,512]{1,0:T(8,128)(2,1)S(1)}, bf16[64,512]{1,0:T(8,128)(2,1)S(1)}, u32[]{:S(2)}, u32[]{:S(2)}) collective-permute-start(bf16[64,512]{1,0:T(8,128)(2,1)S(1)} %shard_map.87), channel_id=1, source_target_pairs={{0,8},{8,16},{16,24},{24,32},{32,40},{40,48},{48,56},{56,64},{64,7... | collective-permute-start | bytes 196616 | tf_op jit(solution)/shard_map/ppermute | solution.py:43
  49.8 6.7 %collective-permute-start.9 = (bf16[64,512]{1,0:T(8,128)(2,1)S(1)}, bf16[64,512]{1,0:T(8,128)(2,1)S(1)}, u32[]{:S(2)}, u32[]{:S(2)}) collective-permute-start(bf16[64,512]{1,0:T(8,128)(2,1)S(1)} %shard_map.87), channel_id=1, source_target_pairs={{0,504},{8,0},{16,8},{24,16},{32,24},{40,32},{48,40},{56,48},{64,5... | collective-permute-start | bytes 196616 | tf_op jit(solution)/shard_map/ppermute | solution.py:43
  56.5 0.1 pad_maximum_fusion.mid
  56.6 1.9 %collective-permute-start.6 = (bf16[1536,256]{1,0:T(8,128)(2,1)S(1)}, bf16[1536,256]{1,0:T(8,128)(2,1)S(1)}, u32[]{:S(2)}, u32[]{:S(2)}) collective-permute-start(bf16[1536,256]{1,0:T(8,128)(2,1)S(1)} %pad_maximum_fusion.mid), channel_id=1, source_target_pairs={{0,24},{8,32},{16,40},{24,48},{32,56},{40,64},{48,72},{56,80},{64,... | collective-permute-start | bytes 2359304 | tf_op jit(solution)/shard_map/ppermute | solution.py:43
  58.5 5.5 %collective-permute-start.7 = (bf16[1536,256]{1,0:T(8,128)(2,1)S(1)}, bf16[1536,256]{1,0:T(8,128)(2,1)S(1)}, u32[]{:S(2)}, u32[]{:S(2)}) collective-permute-start(bf16[1536,256]{1,0:T(8,128)(2,1)S(1)} %pad_maximum_fusion.mid), channel_id=1, source_target_pairs={{0,488},{8,496},{16,504},{24,0},{32,8},{40,16},{48,24},{56,32},{64... | collective-permute-start | bytes 2359304 | tf_op jit(solution)/shard_map/ppermute | solution.py:43
  64.0 1.9 %collective-permute-start.10 = (bf16[192,512]{1,0:T(8,128)(2,1)S(1)}, bf16[192,512]{1,0:T(8,128)(2,1)S(1)}, u32[]{:S(2)}, u32[]{:S(2)}) collective-permute-start(bf16[192,512]{1,0:T(8,128)(2,1)S(1)} %pad_maximum_fusion.1.mid), channel_id=1, source_target_pairs={{0,24},{8,32},{16,40},{24,48},{32,56},{40,64},{48,72},{56,80},{64,... | collective-permute-start | bytes 589832 | tf_op jit(solution)/shard_map/ppermute | solution.py:43
  65.9 5.5 %collective-permute-start.11 = (bf16[192,512]{1,0:T(8,128)(2,1)S(1)}, bf16[192,512]{1,0:T(8,128)(2,1)S(1)}, u32[]{:S(2)}, u32[]{:S(2)}) collective-permute-start(bf16[192,512]{1,0:T(8,128)(2,1)S(1)} %pad_maximum_fusion.1.mid), channel_id=1, source_target_pairs={{0,488},{8,496},{16,504},{24,0},{32,8},{40,16},{48,24},{56,32},{64... | collective-permute-start | bytes 589832 | tf_op jit(solution)/shard_map/ppermute | solution.py:43
  71.4 11.1 %collective-permute-done.10.low = bf16[192,512]{1,0:T(8,128)(2,1)S(1)} collective-permute-done((bf16[192,512]{1,0:T(8,128)(2,1)S(1)}, bf16[192,512]{1,0:T(8,128)(2,1)S(1)}, u32[]{:S(2)}, u32[]{:S(2)}) %collective-permute-start.10) | collective-permute-done | bytes 196640 | tf_op jit(solution)/shard_map/ppermute | solution.py:43
  82.5 1.0 collective-permute-done.11.high
  83.6 0.7 shard_map.88.rows
  84.3 1.9 %collective-permute-start.14 = (bf16[384,512]{1,0:T(8,128)(2,1)S(1)}, bf16[384,512]{1,0:T(8,128)(2,1)S(1)}, u32[]{:S(2)}, u32[]{:S(2)}) collective-permute-start(bf16[384,512]{1,0:T(8,128)(2,1)S(1)} %shard_map.88.rows), channel_id=1, source_target_pairs={{0,2},{2,4},{4,6},{6,0},{1,3},{3,5},{5,7},{7,1},{8,10},{10,12},{12... | collective-permute-start | bytes 1179656 | tf_op jit(solution)/shard_map/ppermute | solution.py:43
  86.2 4.6 %collective-permute-start.13 = (bf16[384,512]{1,0:T(8,128)(2,1)S(1)}, bf16[384,512]{1,0:T(8,128)(2,1)S(1)}, u32[]{:S(2)}, u32[]{:S(2)}) collective-permute-start(bf16[384,512]{1,0:T(8,128)(2,1)S(1)} %shard_map.88.rows), channel_id=1, source_target_pairs={{0,6},{2,0},{4,2},{6,4},{1,7},{3,1},{5,3},{7,5},{8,14},{10,8},{12,... | collective-permute-start | bytes 1179656 | tf_op jit(solution)/shard_map/ppermute | solution.py:43
  90.8 1.9 %collective-permute-start.12 = (bf16[384,512]{1,0:T(8,128)(2,1)S(1)}, bf16[384,512]{1,0:T(8,128)(2,1)S(1)}, u32[]{:S(2)}, u32[]{:S(2)}) collective-permute-start(bf16[384,512]{1,0:T(8,128)(2,1)S(1)} %shard_map.88.rows), channel_id=1, source_target_pairs={{0,4},{2,6},{4,0},{6,2},{1,5},{3,7},{5,1},{7,3},{8,12},{10,14},{12... | collective-permute-start | bytes 1179656 | tf_op jit(solution)/shard_map/ppermute | solution.py:43
  92.8 0.8 shard_map.89.scaled
  93.6 0.6 shard_map.90.refs_0_
  94.1 1.6 %collective-permute-done.14.rows = bf16[384,512]{1,0:T(8,128)(2,1)S(1)} collective-permute-done((bf16[384,512]{1,0:T(8,128)(2,1)S(1)}, bf16[384,512]{1,0:T(8,128)(2,1)S(1)}, u32[]{:S(2)}, u32[]{:S(2)}) %collective-permute-start.14) | collective-permute-done | bytes 393248 | tf_op jit(solution)/shard_map/ppermute | solution.py:43
  95.7 0.6 shard_map.91.refs_0_
  96.3 1.0 collective-permute-done.13.rows
  97.4 0.6 shard_map.92.refs_0_
  97.9 4.2 %collective-permute-done.12.rows = bf16[384,512]{1,0:T(8,128)(2,1)S(1)} collective-permute-done((bf16[384,512]{1,0:T(8,128)(2,1)S(1)}, bf16[384,512]{1,0:T(8,128)(2,1)S(1)}, u32[]{:S(2)}, u32[]{:S(2)}) %collective-permute-start.12) | collective-permute-done | bytes 393248 | tf_op jit(solution)/shard_map/ppermute | solution.py:43
  102.1 0.6 shard_map.93.tapered
  102.7 0.8 shard_map.86.duals
  103.5 1.0 shard_map.95
  104.5 9.0 %collective-permute-start.15 = (f32[512,512]{1,0:T(8,128)S(1)}, f32[512,512]{1,0:T(8,128)S(1)}, u32[]{:S(2)}, u32[]{:S(2)}) collective-permute-start(f32[512,512]{1,0:T(8,128)S(1)} %shard_map.95), channel_id=1, source_target_pairs={{0,1},{1,0},{2,3},{3,2},{4,5},{5,4},{6,7},{7,6},{8,9},{9,8},{10,11... | collective-permute-start | bytes 3145736 | tf_op jit(solution)/shard_map/ppermute | solution.py:43
  113.5 1.0 shard_map.94.mine
  114.4 1.3 %collective-permute-done.15.theirs = f32[512,512]{1,0:T(8,128)S(1)} collective-permute-done((f32[512,512]{1,0:T(8,128)S(1)}, f32[512,512]{1,0:T(8,128)S(1)}, u32[]{:S(2)}, u32[]{:S(2)}) %collective-permute-start.15) | collective-permute-done | bytes 1048608 | tf_op jit(solution)/shard_map/ppermute | solution.py:43
  115.7 1.2 %shard_map.96 = f32[2048,128]{1,0:T(8,128)} custom-call(f32[512,512]{1,0:T(8,128)S(1)} %shard_map.94.mine, f32[512,512]{1,0:T(8,128)S(1)} %collective-permute-done.15.theirs), custom_call_target="tpu_custom_call" | custom-call | flops 100000000 | bytes 1000000 | tf_op jit(solution)/shard_map/pallas_call | solution.py:25
  (17 shorter events, 0.1 us)
Async XLA Ops:
  0.0 1.0 copy-start.1
  1.0 0.7 copy-start.3
  1.7 15.1 %copy-start.2 = (bf16[64,512]{1,0:T(8,128)(2,1)S(1)}, bf16[64,512]{1,0:T(8,128)(2,1)}, u32[]{:S(2)}) copy-start(bf16[64,512]{1,0:T(8,128)(2,1)} %duals.3) | copy-start | bytes 196612
  1.9 15.0 %collective-permute-start = (bf16[528,512]{1,0:T(8,128)(2,1)S(1)}, bf16[528,512]{1,0:T(8,128)(2,1)S(1)}, u32[]{:S(2)}, u32[]{:S(2)}) collective-permute-start(bf16[528,512]{1,0:T(8,128)(2,1)S(1)} %shard_map.82.cells.own), channel_id=1, source_target_pairs={{0,1},{1,0},{2,3},{3,2},{4,5},{5,4},{6,7},{7,6},{8,9},{9,8},{10,11... | collective-permute-start | bytes 1622024 | tf_op jit(solution)/shard_map/ppermute | solution.py:43
  14.2 0.9 copy-start
  15.1 0.7 copy-start.4
  18.0 8.3 %collective-permute-start.1 = (bf16[192,512]{1,0:T(8,128)(2,1)S(1)}, bf16[192,512]{1,0:T(8,128)(2,1)S(1)}, u32[]{:S(2)}, u32[]{:S(2)}) collective-permute-start(bf16[192,512]{1,0:T(8,128)(2,1)S(1)} %get-tuple-element.10), channel_id=1, source_target_pairs={{0,6},{2,0},{4,2},{6,4},{1,7},{3,1},{5,3},{7,5},{8,14},{10,8},{12,... | collective-permute-start | bytes 589832 | tf_op jit(solution)/shard_map/ppermute | solution.py:43
  19.9 9.8 %collective-permute-start.2 = (bf16[192,512]{1,0:T(8,128)(2,1)S(1)}, bf16[192,512]{1,0:T(8,128)(2,1)S(1)}, u32[]{:S(2)}, u32[]{:S(2)}) collective-permute-start(bf16[192,512]{1,0:T(8,128)(2,1)S(1)} %get-tuple-element.11), channel_id=1, source_target_pairs={{0,4},{2,6},{4,0},{6,2},{1,5},{3,7},{5,1},{7,3},{8,12},{10,14},{12... | collective-permute-start | bytes 589832 | tf_op jit(solution)/shard_map/ppermute | solution.py:43
  21.8 12.5 %collective-permute-start.3 = (bf16[192,512]{1,0:T(8,128)(2,1)S(1)}, bf16[192,512]{1,0:T(8,128)(2,1)S(1)}, u32[]{:S(2)}, u32[]{:S(2)}) collective-permute-start(bf16[192,512]{1,0:T(8,128)(2,1)S(1)} %get-tuple-element.12), channel_id=1, source_target_pairs={{0,2},{2,4},{4,6},{6,0},{1,3},{3,5},{5,7},{7,1},{8,10},{10,12},{12... | collective-permute-start | bytes 589832 | tf_op jit(solution)/shard_map/ppermute | solution.py:43
  34.5 22.0 %collective-permute-start.4 = (bf16[512,256]{1,0:T(8,128)(2,1)S(1)}, bf16[512,256]{1,0:T(8,128)(2,1)S(1)}, u32[]{:S(2)}, u32[]{:S(2)}) collective-permute-start(bf16[512,256]{1,0:T(8,128)(2,1)S(1)} %shard_map.85), channel_id=1, source_target_pairs={{0,8},{8,16},{16,24},{24,32},{32,40},{40,48},{48,56},{56,64},{64,7... | collective-permute-start | bytes 786440 | tf_op jit(solution)/shard_map/ppermute | solution.py:43
  36.4 20.1 %collective-permute-start.5 = (bf16[512,256]{1,0:T(8,128)(2,1)S(1)}, bf16[512,256]{1,0:T(8,128)(2,1)S(1)}, u32[]{:S(2)}, u32[]{:S(2)}) collective-permute-start(bf16[512,256]{1,0:T(8,128)(2,1)S(1)} %shard_map.85), channel_id=1, source_target_pairs={{0,504},{8,0},{16,8},{24,16},{32,24},{40,32},{48,40},{56,48},{64,5... | collective-permute-start | bytes 786440 | tf_op jit(solution)/shard_map/ppermute | solution.py:43
  47.7 45.0 %copy-start.5 = (bf16[4,128,512]{2,1,0:T(8,128)(2,1)S(1)}, bf16[4,128,512]{2,1,0:T(8,128)(2,1)}, u32[]{:S(2)}) copy-start(bf16[4,128,512]{2,1,0:T(8,128)(2,1)} %taper.1) | copy-start | bytes 1572868
  47.7 16.2 %collective-permute-start.8 = (bf16[64,512]{1,0:T(8,128)(2,1)S(1)}, bf16[64,512]{1,0:T(8,128)(2,1)S(1)}, u32[]{:S(2)}, u32[]{:S(2)}) collective-permute-start(bf16[64,512]{1,0:T(8,128)(2,1)S(1)} %shard_map.87), channel_id=1, source_target_pairs={{0,8},{8,16},{16,24},{24,32},{32,40},{40,48},{48,56},{56,64},{64,7... | collective-permute-start | bytes 196616 | tf_op jit(solution)/shard_map/ppermute | solution.py:43
  49.8 14.2 %collective-permute-start.9 = (bf16[64,512]{1,0:T(8,128)(2,1)S(1)}, bf16[64,512]{1,0:T(8,128)(2,1)S(1)}, u32[]{:S(2)}, u32[]{:S(2)}) collective-permute-start(bf16[64,512]{1,0:T(8,128)(2,1)S(1)} %shard_map.87), channel_id=1, source_target_pairs={{0,504},{8,0},{16,8},{24,16},{32,24},{40,32},{48,40},{56,48},{64,5... | collective-permute-start | bytes 196616 | tf_op jit(solution)/shard_map/ppermute | solution.py:43
  56.6 46.1 %collective-permute-start.6 = (bf16[1536,256]{1,0:T(8,128)(2,1)S(1)}, bf16[1536,256]{1,0:T(8,128)(2,1)S(1)}, u32[]{:S(2)}, u32[]{:S(2)}) collective-permute-start(bf16[1536,256]{1,0:T(8,128)(2,1)S(1)} %pad_maximum_fusion.mid), channel_id=1, source_target_pairs={{0,24},{8,32},{16,40},{24,48},{32,56},{40,64},{48,72},{56,80},{64,... | collective-permute-start | bytes 2359304 | tf_op jit(solution)/shard_map/ppermute | solution.py:43
  58.5 44.2 %collective-permute-start.7 = (bf16[1536,256]{1,0:T(8,128)(2,1)S(1)}, bf16[1536,256]{1,0:T(8,128)(2,1)S(1)}, u32[]{:S(2)}, u32[]{:S(2)}) collective-permute-start(bf16[1536,256]{1,0:T(8,128)(2,1)S(1)} %pad_maximum_fusion.mid), channel_id=1, source_target_pairs={{0,488},{8,496},{16,504},{24,0},{32,8},{40,16},{48,24},{56,32},{64... | collective-permute-start | bytes 2359304 | tf_op jit(solution)/shard_map/ppermute | solution.py:43
  64.0 18.5 %collective-permute-start.10 = (bf16[192,512]{1,0:T(8,128)(2,1)S(1)}, bf16[192,512]{1,0:T(8,128)(2,1)S(1)}, u32[]{:S(2)}, u32[]{:S(2)}) collective-permute-start(bf16[192,512]{1,0:T(8,128)(2,1)S(1)} %pad_maximum_fusion.1.mid), channel_id=1, source_target_pairs={{0,24},{8,32},{16,40},{24,48},{32,56},{40,64},{48,72},{56,80},{64,... | collective-permute-start | bytes 589832 | tf_op jit(solution)/shard_map/ppermute | solution.py:43
  65.9 17.6 %collective-permute-start.11 = (bf16[192,512]{1,0:T(8,128)(2,1)S(1)}, bf16[192,512]{1,0:T(8,128)(2,1)S(1)}, u32[]{:S(2)}, u32[]{:S(2)}) collective-permute-start(bf16[192,512]{1,0:T(8,128)(2,1)S(1)} %pad_maximum_fusion.1.mid), channel_id=1, source_target_pairs={{0,488},{8,496},{16,504},{24,0},{32,8},{40,16},{48,24},{56,32},{64... | collective-permute-start | bytes 589832 | tf_op jit(solution)/shard_map/ppermute | solution.py:43
  84.3 11.4 %collective-permute-start.14 = (bf16[384,512]{1,0:T(8,128)(2,1)S(1)}, bf16[384,512]{1,0:T(8,128)(2,1)S(1)}, u32[]{:S(2)}, u32[]{:S(2)}) collective-permute-start(bf16[384,512]{1,0:T(8,128)(2,1)S(1)} %shard_map.88.rows), channel_id=1, source_target_pairs={{0,2},{2,4},{4,6},{6,0},{1,3},{3,5},{5,7},{7,1},{8,10},{10,12},{12... | collective-permute-start | bytes 1179656 | tf_op jit(solution)/shard_map/ppermute | solution.py:43
  86.2 11.1 %collective-permute-start.13 = (bf16[384,512]{1,0:T(8,128)(2,1)S(1)}, bf16[384,512]{1,0:T(8,128)(2,1)S(1)}, u32[]{:S(2)}, u32[]{:S(2)}) collective-permute-start(bf16[384,512]{1,0:T(8,128)(2,1)S(1)} %shard_map.88.rows), channel_id=1, source_target_pairs={{0,6},{2,0},{4,2},{6,4},{1,7},{3,1},{5,3},{7,5},{8,14},{10,8},{12,... | collective-permute-start | bytes 1179656 | tf_op jit(solution)/shard_map/ppermute | solution.py:43
  90.8 11.3 %collective-permute-start.12 = (bf16[384,512]{1,0:T(8,128)(2,1)S(1)}, bf16[384,512]{1,0:T(8,128)(2,1)S(1)}, u32[]{:S(2)}, u32[]{:S(2)}) collective-permute-start(bf16[384,512]{1,0:T(8,128)(2,1)S(1)} %shard_map.88.rows), channel_id=1, source_target_pairs={{0,4},{2,6},{4,0},{6,2},{1,5},{3,7},{5,1},{7,3},{8,12},{10,14},{12... | collective-permute-start | bytes 1179656 | tf_op jit(solution)/shard_map/ppermute | solution.py:43
  104.5 11.2 %collective-permute-start.15 = (f32[512,512]{1,0:T(8,128)S(1)}, f32[512,512]{1,0:T(8,128)S(1)}, u32[]{:S(2)}, u32[]{:S(2)}) collective-permute-start(f32[512,512]{1,0:T(8,128)S(1)} %shard_map.95), channel_id=1, source_target_pairs={{0,1},{1,0},{2,3},{3,2},{4,5},{5,4},{6,7},{7,6},{8,9},{9,8},{10,11... | collective-permute-start | bytes 3145736 | tf_op jit(solution)/shard_map/ppermute | solution.py:43

commit v3 on v2

v3 whole, which is shorter than its diff:
```python
import functools

import jax
import jax.numpy as jnp
from jax import lax
from jax.experimental import pallas as pl
from jax.experimental.pallas import tpu as pltpu
from jax.sharding import Mesh
from jax.sharding import PartitionSpec as P

REACH = 4
NEAR = 6
RELS = 4
F32 = jnp.float32
BF16 = jnp.bfloat16
NT = (((1,), (1,)), ((), ()))
CLASS, CHIP, CORE, COUNT = 6, 12, 13, 14


def kernel(body, out, inputs, flops, scalars=0, scratch=(), aliases=None, given=None, spaces=None):
    spaces = spaces or [pltpu.VMEM] * len(out)
    given = given or [pltpu.SMEM] * scalars + [pltpu.VMEM] * (len(inputs) - scalars)
    inputs = [pltpu.with_memory_space_constraint(a, m) for a, m in zip(inputs, given)]
    return pl.pallas_call(
        body,
        out_shape=[o if m is None else m(o.shape, o.dtype) for o, m in zip(out, spaces)],
        in_specs=[pl.BlockSpec(memory_space=m) for m in given],
        out_specs=[pl.BlockSpec(memory_space=m or pl.ANY) for m in spaces],
        scratch_shapes=list(scratch),
        input_output_aliases=aliases or {},
        cost_estimate=pl.CostEstimate(flops=int(flops), bytes_accessed=int(1e6), transcendentals=0),
        compiler_params=pltpu.CompilerParams(vmem_limit_bytes=16 << 20),
    )(*inputs)


def array(shape, kind):
    return jax.ShapeDtypeStruct(shape, kind)


def move(value, axis, steps):
    count = lax.axis_size(axis)
    return lax.ppermute(value, axis, [(i, (i + steps) % count) for i in range(count)])


def pack_body(*refs):
    given, (meta, out, weights, foot), held = refs[:6], refs[6:10], refs[10:]
    near, count, classes, raw, wide, done = held
    copies = []
    for q, kept in enumerate((near, count, classes, raw, weights, foot)):
        copies.append(pltpu.make_async_copy(given[q], kept, done.at[q]))
    for q in (3, 4, 0, 1, 2, 5):
        copies[q].start()
    copies[3].wait()
    members = out.shape[0] - 16
    levels, slots = weights.shape
    points = raw.shape[1]
    wide[...] = raw[...].astype(F32)
    for l in range(levels):
        plane = wide[pl.ds(l, members, stride=levels), :].astype(BF16)
        out[:members, l * points : (l + 1) * points] = plane
    for q in (4, 0, 1, 2, 5):
        copies[q].wait()
    high = weights[...].astype(BF16).astype(F32)
    low = weights[...] - high
    pad = jnp.zeros((16 - 2 * levels, slots), F32)
    out[members:, :] = jnp.concatenate([high, low, pad], axis=0).astype(BF16)
    tile = lax.axis_index("z") * lax.axis_size("y") + lax.axis_index("y")
    tiles = lax.axis_size("z") * lax.axis_size("y")
    for k in range(NEAR):
        meta[k] = lax.rem(near[k, tile] - tile + REACH + tiles, tiles)
        meta[CLASS + k] = classes[0, k]
    meta[CHIP] = lax.axis_index("x")
    meta[CORE] = lax.axis_index("c")
    meta[COUNT] = count[tile]


def columns(meta, weights, owned):
    parts = []
    for r in range(RELS):
        chip = lax.rem(meta[CHIP] + r, RELS)
        block = weights(pl.ds(pl.multiple_of(chip * 2 * owned, 2 * owned), 2 * owned))
        flipped = jnp.concatenate([block, block], axis=0).T
        parts.append(jnp.where(meta[CORE] == 0, flipped[:owned], flipped[owned:]))
    return jnp.concatenate(parts, axis=0)


def rows_of(meta, foot, owned):
    parts = []
    for r in range(RELS):
        chip = lax.rem(meta[CHIP] + r, RELS)
        start = pl.multiple_of(chip * 2 * owned + meta[CORE] * owned, owned)
        parts.append(foot[pl.ds(start, owned), :])
    return jnp.concatenate(parts, axis=0)


def project(picked, column, cells, acc, fresh):
    members = acc.shape[1]
    points = picked.shape[1]
    for l in range(cells.shape[1] // points):
        plane = cells[:members, l * points : (l + 1) * points]
        got = lax.dot_general(picked, plane, NT, preferred_element_type=F32)
        term = column[:, l : l + 1] * got
        if l == 0 and fresh:
            acc[...] = term
        else:
            acc[...] += term


def own_body(meta, foot, cells, weights, out):
    owned = out.shape[0] // RELS
    column = columns(meta, lambda at: weights[:, at], owned)
    project(rows_of(meta, foot, owned), column, cells, out, True)


def other_body(meta, foot, cells, before, mine, pay1, pay2, pay3, acc):
    owned, members = mine.shape

    def weights(at):
        terms = cells[members:, at].astype(F32)
        return terms[:4] + terms[4:8]

    acc[...] = before[...]
    project(rows_of(meta, foot, owned), columns(meta, weights, owned), cells, acc, False)
    slot = lax.broadcasted_iota(jnp.int32, mine.shape, 0) + meta[CORE] * owned
    for r, pay in enumerate((mine, pay1, pay2, pay3)):
        chip = lax.rem(meta[CHIP] + r, RELS)
        present = slot + chip * 2 * owned < meta[COUNT]
        part = jnp.where(present, acc[r * owned : (r + 1) * owned], 0.0)
        if r == 0:
            mine[...] = part
        else:
            high = part.astype(BF16)
            pay[:owned] = high
            pay[owned:] = (part - high.astype(F32)).astype(BF16)


def fold_body(mine, *refs):
    out = refs[-1]
    owned = out.shape[0]
    total = mine[...]
    for got in refs[:-1]:
        total = total + (got[:owned].astype(F32) + got[owned:].astype(F32))
    out[...] = total.astype(BF16)


def flip_body(*refs):
    out = refs[-1]
    wide = refs[0].shape[0]
    for r, rows in enumerate(refs[:-1]):
        out[:, r * wide : (r + 1) * wide] = rows[...].T


def choose(meta, k, sources, size, store):
    group = meta[k] // 3
    start = pl.multiple_of(lax.rem(meta[k], 3) * size, size)
    for g, source in enumerate(sources):

        @pl.when(group == g)
        def _(source=source):
            store(source[pl.ds(start, size), :])


def pick_body(meta, low, mid, high, out):
    size = out.shape[0] // NEAR
    for k in range(NEAR):

        def store(value, k=k):
            out[k * size : (k + 1) * size] = value

        choose(meta, k, (low, mid, high), size, store)


def taper_body(meta, taper, out, tall):
    classes = taper.shape[0]
    owned = out.shape[1] // NEAR
    for q in range(classes):
        tall[q] = taper[q].astype(F32).T / F32(511)
    for r in range(RELS):
        chip = lax.rem(meta[CHIP] + r, RELS)
        start = pl.multiple_of(chip * 2 * owned + meta[CORE] * owned, owned)
        for k in range(NEAR):
            out[r, k * owned : (k + 1) * owned] = tall[meta[CLASS + k], pl.ds(start, owned), :]


def covary_body(rel, rows, own, other, scaled, *refs):
    out = refs[-1]
    members = rows.shape[1]
    size = rows.shape[0]
    half = own.shape[1]
    step = 256
    taper = scaled[rel]
    wide = jnp.concatenate([taper] * (step // taper.shape[1]), axis=1)
    for h, cells in enumerate((own, other)):
        for at in range(0, half, step):
            covar = jnp.dot(rows[...], cells[:members, at : at + step], preferred_element_type=F32)
            tapered = (covar * wide).astype(BF16)
            out[rel * size : (rel + 1) * size, h * half + at : h * half + at + step] = tapered


def gain_body(h, duals, tapered, out):
    half = out.shape[1]
    step = 256
    for at in range(0, half, step):
        out[:, at : at + step] = jnp.dot(
            duals[...], tapered[:, h * half + at : h * half + at + step], preferred_element_type=F32
        )


def finish_body(mine, theirs, out, held, done):
    members = mine.shape[0]
    levels = out.shape[0] // members
    points = out.shape[1]
    parts = done.shape[0]
    size = members // parts
    copies = []
    for q in range(parts):
        for l in range(levels):
            at = (slice(q * size, (q + 1) * size), slice(l * points, (l + 1) * points))
            held[pl.ds(q * size * levels + l, size, stride=levels), :] = mine[at] + theirs[at]
        span = pl.ds(q * size * levels, size * levels)
        copies.append(pltpu.make_async_copy(held.at[span], out.at[span], done.at[q]))
        copies[-1].start()
    for copy in copies:
        copy.wait()


def shards(
    anomalies, footprint, weighting, dual_rows, taper_blocks, obs_count, near_tiles, taper_class
):
    members, levels, points = anomalies.shape
    owned = dual_rows.shape[0]
    tile = ("z", "y")
    w_low, w_high = move(dual_rows, tile, 1), move(dual_rows, tile, -1)
    raw = anomalies.reshape(members * levels, points)
    meta, own, weights, foot = kernel(
        pack_body,
        [
            array((16,), jnp.int32),
            array((members + 16, levels * points), BF16),
            array(weighting.shape, F32),
            array(footprint.shape, BF16),
        ],
        [near_tiles.T, obs_count, taper_class, raw, weighting, footprint],
        1e8,
        scratch=[
            pltpu.SMEM(near_tiles.T.shape, jnp.int32),
            pltpu.SMEM(obs_count.shape, jnp.int32),
            pltpu.SMEM(taper_class.shape, jnp.int32),
            pltpu.VMEM(raw.shape, BF16),
            pltpu.VMEM(raw.shape, F32),
            pltpu.SemaphoreType.DMA((6,)),
        ],
        given=[pltpu.HBM] * 6,
        spaces=[pltpu.SMEM, pltpu.VMEM, pltpu.VMEM, pltpu.VMEM],
    )
    other = move(own, "c", 1)

    rows = RELS * owned
    work = 2 * rows * points * members * levels
    (begun,) = kernel(
        own_body, [array((rows, members), F32)], [meta, foot, own, weights], work, scalars=1
    )
    pay = array((2 * owned, members), BF16)
    mine, pay1, pay2, pay3 = kernel(
        other_body,
        [array((owned, members), F32), pay, pay, pay],
        [meta, foot, other, begun],
        work,
        scalars=1,
        scratch=[pltpu.VMEM((rows, members), F32)],
    )
    got1, got3, got2 = move(pay1, "x", 1), move(pay3, "x", -1), move(pay2, "x", 2)
    w_mid = jnp.concatenate([w_low, dual_rows, w_high], axis=0)
    w_far_low, w_far_high = move(w_mid, tile, 3), move(w_mid, tile, -3)
    (rows_y,) = kernel(fold_body, [array((owned, members), BF16)], [mine, got1, got3, got2], 1e8)
    y_low, y_high = move(rows_y, tile, 1), move(rows_y, tile, -1)
    chosen = [array((NEAR * owned, members), BF16)]
    (w0,) = kernel(pick_body, chosen, [meta, w_far_low, w_mid, w_far_high], 1e8, scalars=1)
    w3, w1, w2 = move(w0, "x", 1), move(w0, "x", -1), move(w0, "x", 2)
    y_mid = jnp.concatenate([y_low, rows_y, y_high], axis=0)
    y_far_low, y_far_high = move(y_mid, tile, 3), move(y_mid, tile, -3)
    (y0,) = kernel(pick_body, chosen, [meta, y_far_low, y_mid, y_far_high], 1e8, scalars=1)
    y3, y1, y2 = move(y0, "x", 1), move(y0, "x", -1), move(y0, "x", 2)

    taper_late, _ = lax.optimization_barrier((taper_blocks, y0))
    (scaled,) = kernel(
        taper_body,
        [array((RELS, NEAR * owned, points), F32)],
        [meta, taper_late],
        1e9,
        scalars=1,
        scratch=[pltpu.VMEM((taper_blocks.shape[0], taper_blocks.shape[2], points), F32)],
    )
    width = levels * points
    tapered = None
    for rel, got in ((0, y0), (3, y3), (1, y1), (2, y2)):
        inputs = [got, own, other, scaled] + ([] if tapered is None else [tapered])
        (tapered,) = kernel(
            functools.partial(covary_body, rel),
            [array((NEAR * rows, 2 * width), BF16)],
            inputs,
            4 * NEAR * owned * members * width,
            aliases={} if tapered is None else {4: 0},
        )
    (duals,) = kernel(flip_body, [array((members, NEAR * rows), BF16)], [w0, w1, w2, w3], 1e9)
    sums = [
        kernel(
            functools.partial(gain_body, h),
            [array((members, width), F32)],
            [duals, tapered],
            2 * NEAR * rows * members * width,
        )[0]
        for h in (0, 1)
    ]
    theirs = move(sums[1], "c", 1)
    (out,) = kernel(
        finish_body,
        [array((members * levels, points), F32)],
        [sums[0], theirs],
        1e8,
        scratch=[pltpu.VMEM((members * levels, points), F32), pltpu.SemaphoreType.DMA((4,))],
        spaces=[None],
    )
    return out.reshape(members, levels, points)


def solution(mesh):
    fine = Mesh(mesh.devices.reshape(16, 4, 4, 2), ("z", "y", "x", "c"))
    tile, level = ("z", "y"), ("x", "c")
    return jax.shard_map(
        shards,
        mesh=fine,
        in_specs=(
            P(None, level, tile),
            P(tile, None),
            P(level, tile),
            P((*tile, *level), None),
            P(),
            P(),
            P(),
            P(tile, None),
        ),
        out_specs=P(None, level, tile),
        check_vma=False,
    )
```

time: 118 us -> 105 us (0.89)
  waiting for transfers between devices: 29.4 us -> 15.4 us
  starting transfers between devices: 69.4 us -> 78.7 us
  local copies, waits for them, and re-layouts: 5.36 us -> 0.86 us
  Pallas kernels: 10.8 us -> 8.71 us
    ppermute x16 -> x19, waiting for transfers between devices: 29.4 us -> 15.4 us  [move(): lax.ppermute(value, axis, [(i, (i + steps) % count) for i in range(count)])]
    ppermute x16 -> x19, starting transfers between devices: 69.4 us -> 78.7 us  [move(): lax.ppermute(value, axis, [(i, (i + steps) % count) for i in range(count)])]
    unnamed x12 -> x4, local copies, waits for them, and re-layouts: 3.35 us -> 0.86 us
    pallas_call x15, Pallas kernels: 10.8 us -> 8.71 us  [kernel(): pl.pallas_call(body, out_shape=[o if m is None else m(o.shape, o.dtype) f...]
    dynamic_slice x1 -> x0, local copies, waits for them, and re-layouts: 1.28 us -> none  [shards(): left = obs_count[tile_id] - (x * 2 + c) * owned]
  transfers between devices with their start and end apart: 16 -> 19, of which waited for: 9 -> 9; matrix products, arithmetic and copies ran while one was open for 3% -> 1% of each run, Pallas kernels for 6% -> 5%
where the time goes in v3:
time: 105 us; the launch traced here: 104 us
  starting transfers between devices  78.7 us (75%)
  waiting for transfers between devices  15.4 us (15%)
  Pallas kernels  8.71 us (8%)
    ppermute x19, starting transfers between devices, move(): lax.ppermute(value, axis, [(i, (i + steps) % count) for i in range(count)])  78.7 us
    ppermute x19, waiting for transfers between devices, move(): lax.ppermute(value, axis, [(i, (i + steps) % count) for i in range(count)])  15.4 us
    pallas_call x15, Pallas kernels, kernel(): pl.pallas_call(body, out_shape=[o if m is None else m(o.shape, o.dtype) f...  8.71 us
  transfers between devices with their start and end apart: 19, of which 9 were waited for; matrix products, arithmetic and copies ran while one was open for 1% of the time, Pallas kernels for 5%

profile of v3, /device:TPU:1, one launch (start us, length us, event | category | flops | bytes accessed | tf_op | source)
XLA Modules:
  0.0 104.1 jit_solution(15777643073811095583)
XLA Ops:
  0.0 1.3 %shard_map.82 = (s32[16]{0:T(128)S(4)}, bf16[528,512]{1,0:T(8,128)(2,1)S(1)}, f32[4,512]{1,0:T(4,128)S(1)}, bf16[512,128]{1,0:T(8,128)(2,1)S(1)}) custom-call(s32[6,64]{1,0:T(8,128)} %bitcast.4, s32[64]{0:T(128)} %refs_1_.1, s32[1,6]{1,0:T(1,128)} %refs_2_.1, bf16[2048,128]{1,0:T(8,128)(2,1)} %bitcast.3, f32[4,512]{1,0:T(4,128)} %refs_4_.1, ...), custom_call_target="tpu_custom_call" | custom-call | flops 100000000 | bytes 1000000 | tf_op jit(solution)/shard_map/pallas_call | solution.py:24
  1.3 8.7 %collective-permute-start.7 = (bf16[528,512]{1,0:T(8,128)(2,1)S(1)}, bf16[528,512]{1,0:T(8,128)(2,1)S(1)}, u32[]{:S(2)}, u32[]{:S(2)}) collective-permute-start(bf16[528,512]{1,0:T(8,128)(2,1)S(1)} %get-tuple-element.16.cells.own), channel_id=1, source_target_pairs={{0,1},{1,0},{2,3},{3,2},{4,5},{5,4},{6,7},{7,6},{8,9},{9,8},{10,11... | collective-permute-start | bytes 1622024 | tf_op jit(solution)/shard_map/ppermute | solution.py:42
  10.1 1.9 %collective-permute-start = (bf16[64,512]{1,0:T(8,128)(2,1)}, bf16[64,512]{1,0:T(8,128)(2,1)S(1)}, u32[]{:S(2)}, u32[]{:S(2)}) collective-permute-start(bf16[64,512]{1,0:T(8,128)(2,1)} %param.11), channel_id=1, source_target_pairs={{0,8},{8,16},{16,24},{24,32},{32,40},{40,48},{48,56},{56,64},{64,7... | collective-permute-start | bytes 196616 | tf_op jit(solution)/shard_map/ppermute | solution.py:42
  12.0 8.2 %collective-permute-start.1 = (bf16[64,512]{1,0:T(8,128)(2,1)}, bf16[64,512]{1,0:T(8,128)(2,1)S(1)}, u32[]{:S(2)}, u32[]{:S(2)}) collective-permute-start(bf16[64,512]{1,0:T(8,128)(2,1)} %param.11), channel_id=1, source_target_pairs={{0,504},{8,0},{16,8},{24,16},{32,24},{40,32},{48,40},{56,48},{64,5... | collective-permute-start | bytes 196616 | tf_op jit(solution)/shard_map/ppermute | solution.py:42
  20.2 0.5 shard_map.85.before
  20.7 0.2 collective-permute-done
  21.0 0.8 constant_dynamic-update-slice_fusion.1
  21.8 0.2 collective-permute-done.1
  22.0 1.9 %collective-permute-start.2 = (bf16[192,512]{1,0:T(8,128)(2,1)S(1)}, bf16[192,512]{1,0:T(8,128)(2,1)S(1)}, u32[]{:S(2)}, u32[]{:S(2)}) collective-permute-start(bf16[192,512]{1,0:T(8,128)(2,1)S(1)} %constant_dynamic-update-slice_fusion.mid), channel_id=1, source_target_pairs={{0,24},{8,32},{16,40},{24,48},{32,56},{40,64},{48,72},{56,80},{64,... | collective-permute-start | bytes 589832 | tf_op jit(solution)/shard_map/ppermute | solution.py:42
  23.9 5.5 %collective-permute-start.3 = (bf16[192,512]{1,0:T(8,128)(2,1)S(1)}, bf16[192,512]{1,0:T(8,128)(2,1)S(1)}, u32[]{:S(2)}, u32[]{:S(2)}) collective-permute-start(bf16[192,512]{1,0:T(8,128)(2,1)S(1)} %constant_dynamic-update-slice_fusion.mid), channel_id=1, source_target_pairs={{0,488},{8,496},{16,504},{24,0},{32,8},{40,16},{48,24},{56,32},{64... | collective-permute-start | bytes 589832 | tf_op jit(solution)/shard_map/ppermute | solution.py:42
  29.4 0.0 collective-permute-done.7.cells.other
  29.4 0.5 shard_map.86
  29.9 4.7 %collective-permute-start.10 = (bf16[128,512]{1,0:T(8,128)(2,1)S(1)}, bf16[128,512]{1,0:T(8,128)(2,1)S(1)}, u32[]{:S(2)}, u32[]{:S(2)}) collective-permute-start(bf16[128,512]{1,0:T(8,128)(2,1)S(1)} %get-tuple-element.21), channel_id=1, source_target_pairs={{0,4},{2,6},{4,0},{6,2},{1,5},{3,7},{5,1},{7,3},{8,12},{10,14},{12... | collective-permute-start | bytes 393224 | tf_op jit(solution)/shard_map/ppermute | solution.py:42
  34.6 2.2 %collective-permute-start.8 = (bf16[128,512]{1,0:T(8,128)(2,1)S(1)}, bf16[128,512]{1,0:T(8,128)(2,1)S(1)}, u32[]{:S(2)}, u32[]{:S(2)}) collective-permute-start(bf16[128,512]{1,0:T(8,128)(2,1)S(1)} %get-tuple-element.19), channel_id=1, source_target_pairs={{0,2},{2,4},{4,6},{6,0},{1,3},{3,5},{5,7},{7,1},{8,10},{10,12},{12... | collective-permute-start | bytes 393224 | tf_op jit(solution)/shard_map/ppermute | solution.py:42
  36.8 4.3 %collective-permute-start.9 = (bf16[128,512]{1,0:T(8,128)(2,1)S(1)}, bf16[128,512]{1,0:T(8,128)(2,1)S(1)}, u32[]{:S(2)}, u32[]{:S(2)}) collective-permute-start(bf16[128,512]{1,0:T(8,128)(2,1)S(1)} %get-tuple-element.20), channel_id=1, source_target_pairs={{0,6},{2,0},{4,2},{6,4},{1,7},{3,1},{5,3},{7,5},{8,14},{10,8},{12,... | collective-permute-start | bytes 393224 | tf_op jit(solution)/shard_map/ppermute | solution.py:42
  41.1 0.0 collective-permute-done.10.refs_2_
  41.1 0.4 collective-permute-done.8.refs_0_
  41.5 1.5 %collective-permute-done.9.refs_1_ = bf16[128,512]{1,0:T(8,128)(2,1)S(1)} collective-permute-done((bf16[128,512]{1,0:T(8,128)(2,1)S(1)}, bf16[128,512]{1,0:T(8,128)(2,1)S(1)}, u32[]{:S(2)}, u32[]{:S(2)}) %collective-permute-start.9) | collective-permute-done | bytes 131104 | tf_op jit(solution)/shard_map/ppermute | solution.py:42
  43.0 0.1 shard_map.87
  43.1 0.0 copy-start
  43.1 2.1 %collective-permute-start.11 = (bf16[64,512]{1,0:T(8,128)(2,1)S(1)}, bf16[64,512]{1,0:T(8,128)(2,1)S(1)}, u32[]{:S(2)}, u32[]{:S(2)}) collective-permute-start(bf16[64,512]{1,0:T(8,128)(2,1)S(1)} %shard_map.87), channel_id=1, source_target_pairs={{0,8},{8,16},{16,24},{24,32},{32,40},{40,48},{48,56},{56,64},{64,7... | collective-permute-start | bytes 196616 | tf_op jit(solution)/shard_map/ppermute | solution.py:42
  45.2 6.7 %collective-permute-start.12 = (bf16[64,512]{1,0:T(8,128)(2,1)S(1)}, bf16[64,512]{1,0:T(8,128)(2,1)S(1)}, u32[]{:S(2)}, u32[]{:S(2)}) collective-permute-start(bf16[64,512]{1,0:T(8,128)(2,1)S(1)} %shard_map.87), channel_id=1, source_target_pairs={{0,504},{8,0},{16,8},{24,16},{32,24},{40,32},{48,40},{56,48},{64,5... | collective-permute-start | bytes 196616 | tf_op jit(solution)/shard_map/ppermute | solution.py:42
  51.9 0.0 collective-permute-done.3.high
  51.9 0.2 shard_map.83.refs_0_
  52.1 5.0 %collective-permute-start.4 = (bf16[384,512]{1,0:T(8,128)(2,1)S(1)}, bf16[384,512]{1,0:T(8,128)(2,1)S(1)}, u32[]{:S(2)}, u32[]{:S(2)}) collective-permute-start(bf16[384,512]{1,0:T(8,128)(2,1)S(1)} %shard_map.83.refs_0_), channel_id=1, source_target_pairs={{0,6},{2,0},{4,2},{6,4},{1,7},{3,1},{5,3},{7,5},{8,14},{10,8},{12,... | collective-permute-start | bytes 1179656 | tf_op jit(solution)/shard_map/ppermute | solution.py:42
  57.1 1.9 %collective-permute-start.5 = (bf16[384,512]{1,0:T(8,128)(2,1)S(1)}, bf16[384,512]{1,0:T(8,128)(2,1)S(1)}, u32[]{:S(2)}, u32[]{:S(2)}) collective-permute-start(bf16[384,512]{1,0:T(8,128)(2,1)S(1)} %shard_map.83.refs_0_), channel_id=1, source_target_pairs={{0,4},{2,6},{4,0},{6,2},{1,5},{3,7},{5,1},{7,3},{8,12},{10,14},{12... | collective-permute-start | bytes 1179656 | tf_op jit(solution)/shard_map/ppermute | solution.py:42
  59.0 2.5 %collective-permute-start.6 = (bf16[384,512]{1,0:T(8,128)(2,1)S(1)}, bf16[384,512]{1,0:T(8,128)(2,1)S(1)}, u32[]{:S(2)}, u32[]{:S(2)}) collective-permute-start(bf16[384,512]{1,0:T(8,128)(2,1)S(1)} %shard_map.83.refs_0_), channel_id=1, source_target_pairs={{0,2},{2,4},{4,6},{6,0},{1,3},{3,5},{5,7},{7,1},{8,10},{10,12},{12... | collective-permute-start | bytes 1179656 | tf_op jit(solution)/shard_map/ppermute | solution.py:42
  61.5 1.9 %collective-permute-start.13 = (bf16[192,512]{1,0:T(8,128)(2,1)S(1)}, bf16[192,512]{1,0:T(8,128)(2,1)S(1)}, u32[]{:S(2)}, u32[]{:S(2)}) collective-permute-start(bf16[192,512]{1,0:T(8,128)(2,1)S(1)} %pad_maximum_fusion.mid), channel_id=1, source_target_pairs={{0,24},{8,32},{16,40},{24,48},{32,56},{40,64},{48,72},{56,80},{64,... | collective-permute-start | bytes 589832 | tf_op jit(solution)/shard_map/ppermute | solution.py:42
  63.5 5.5 %collective-permute-start.14 = (bf16[192,512]{1,0:T(8,128)(2,1)S(1)}, bf16[192,512]{1,0:T(8,128)(2,1)S(1)}, u32[]{:S(2)}, u32[]{:S(2)}) collective-permute-start(bf16[192,512]{1,0:T(8,128)(2,1)S(1)} %pad_maximum_fusion.mid), channel_id=1, source_target_pairs={{0,488},{8,496},{16,504},{24,0},{32,8},{40,16},{48,24},{56,32},{64... | collective-permute-start | bytes 589832 | tf_op jit(solution)/shard_map/ppermute | solution.py:42
  69.0 1.4 %collective-permute-done.13.low = bf16[192,512]{1,0:T(8,128)(2,1)S(1)} collective-permute-done((bf16[192,512]{1,0:T(8,128)(2,1)S(1)}, bf16[192,512]{1,0:T(8,128)(2,1)S(1)}, u32[]{:S(2)}, u32[]{:S(2)}) %collective-permute-start.13) | collective-permute-done | bytes 196640 | tf_op jit(solution)/shard_map/ppermute | solution.py:42
  70.4 1.2 %collective-permute-done.14.high = bf16[192,512]{1,0:T(8,128)(2,1)S(1)} collective-permute-done((bf16[192,512]{1,0:T(8,128)(2,1)S(1)}, bf16[192,512]{1,0:T(8,128)(2,1)S(1)}, u32[]{:S(2)}, u32[]{:S(2)}) %collective-permute-start.14) | collective-permute-done | bytes 196640 | tf_op jit(solution)/shard_map/ppermute | solution.py:42
  71.5 0.1 shard_map.88.rows
  71.7 4.0 %collective-permute-start.17 = (bf16[384,512]{1,0:T(8,128)(2,1)S(1)}, bf16[384,512]{1,0:T(8,128)(2,1)S(1)}, u32[]{:S(2)}, u32[]{:S(2)}) collective-permute-start(bf16[384,512]{1,0:T(8,128)(2,1)S(1)} %shard_map.88.rows), channel_id=1, source_target_pairs={{0,2},{2,4},{4,6},{6,0},{1,3},{3,5},{5,7},{7,1},{8,10},{10,12},{12... | collective-permute-start | bytes 1179656 | tf_op jit(solution)/shard_map/ppermute | solution.py:42
  75.7 2.5 %collective-permute-start.16 = (bf16[384,512]{1,0:T(8,128)(2,1)S(1)}, bf16[384,512]{1,0:T(8,128)(2,1)S(1)}, u32[]{:S(2)}, u32[]{:S(2)}) collective-permute-start(bf16[384,512]{1,0:T(8,128)(2,1)S(1)} %shard_map.88.rows), channel_id=1, source_target_pairs={{0,6},{2,0},{4,2},{6,4},{1,7},{3,1},{5,3},{7,5},{8,14},{10,8},{12,... | collective-permute-start | bytes 1179656 | tf_op jit(solution)/shard_map/ppermute | solution.py:42
  78.2 3.1 %collective-permute-start.15 = (bf16[384,512]{1,0:T(8,128)(2,1)S(1)}, bf16[384,512]{1,0:T(8,128)(2,1)S(1)}, u32[]{:S(2)}, u32[]{:S(2)}) collective-permute-start(bf16[384,512]{1,0:T(8,128)(2,1)S(1)} %shard_map.88.rows), channel_id=1, source_target_pairs={{0,4},{2,6},{4,0},{6,2},{1,5},{3,7},{5,1},{7,3},{8,12},{10,14},{12... | collective-permute-start | bytes 1179656 | tf_op jit(solution)/shard_map/ppermute | solution.py:42
  81.3 0.5 shard_map.84.duals
  81.8 0.3 shard_map.89.scaled
  82.1 0.6 shard_map.90.refs_0_
  82.7 3.0 %collective-permute-done.17.rows = bf16[384,512]{1,0:T(8,128)(2,1)S(1)} collective-permute-done((bf16[384,512]{1,0:T(8,128)(2,1)S(1)}, bf16[384,512]{1,0:T(8,128)(2,1)S(1)}, u32[]{:S(2)}, u32[]{:S(2)}) %collective-permute-start.17) | collective-permute-done | bytes 393248 | tf_op jit(solution)/shard_map/ppermute | solution.py:42
  85.7 0.6 shard_map.91.refs_0_
  86.2 0.6 shard_map.92.refs_0_
  86.8 6.2 %collective-permute-done.15.rows = bf16[384,512]{1,0:T(8,128)(2,1)S(1)} collective-permute-done((bf16[384,512]{1,0:T(8,128)(2,1)S(1)}, bf16[384,512]{1,0:T(8,128)(2,1)S(1)}, u32[]{:S(2)}, u32[]{:S(2)}) %collective-permute-start.15) | collective-permute-done | bytes 393248 | tf_op jit(solution)/shard_map/ppermute | solution.py:42
  93.1 0.6 shard_map.93.tapered
  93.6 1.0 shard_map.95
  94.6 6.2 %collective-permute-start.18 = (f32[512,512]{1,0:T(8,128)S(1)}, f32[512,512]{1,0:T(8,128)S(1)}, u32[]{:S(2)}, u32[]{:S(2)}) collective-permute-start(f32[512,512]{1,0:T(8,128)S(1)} %shard_map.95), channel_id=1, source_target_pairs={{0,1},{1,0},{2,3},{3,2},{4,5},{5,4},{6,7},{7,6},{8,9},{9,8},{10,11... | collective-permute-start | bytes 3145736 | tf_op jit(solution)/shard_map/ppermute | solution.py:42
  100.8 1.0 shard_map.94.mine
  101.8 1.3 %collective-permute-done.18.theirs = f32[512,512]{1,0:T(8,128)S(1)} collective-permute-done((f32[512,512]{1,0:T(8,128)S(1)}, f32[512,512]{1,0:T(8,128)S(1)}, u32[]{:S(2)}, u32[]{:S(2)}) %collective-permute-start.18) | collective-permute-done | bytes 1048608 | tf_op jit(solution)/shard_map/ppermute | solution.py:42
  103.1 1.0 shard_map.96
  (11 shorter events, 0.0 us)
Async XLA Ops:
  1.3 28.1 %collective-permute-start.7 = (bf16[528,512]{1,0:T(8,128)(2,1)S(1)}, bf16[528,512]{1,0:T(8,128)(2,1)S(1)}, u32[]{:S(2)}, u32[]{:S(2)}) collective-permute-start(bf16[528,512]{1,0:T(8,128)(2,1)S(1)} %get-tuple-element.16.cells.own), channel_id=1, source_target_pairs={{0,1},{1,0},{2,3},{3,2},{4,5},{5,4},{6,7},{7,6},{8,9},{9,8},{10,11... | collective-permute-start | bytes 1622024 | tf_op jit(solution)/shard_map/ppermute | solution.py:42
  10.1 10.9 %collective-permute-start = (bf16[64,512]{1,0:T(8,128)(2,1)}, bf16[64,512]{1,0:T(8,128)(2,1)S(1)}, u32[]{:S(2)}, u32[]{:S(2)}) collective-permute-start(bf16[64,512]{1,0:T(8,128)(2,1)} %param.11), channel_id=1, source_target_pairs={{0,8},{8,16},{16,24},{24,32},{32,40},{40,48},{48,56},{56,64},{64,7... | collective-permute-start | bytes 196616 | tf_op jit(solution)/shard_map/ppermute | solution.py:42
  12.0 10.0 %collective-permute-start.1 = (bf16[64,512]{1,0:T(8,128)(2,1)}, bf16[64,512]{1,0:T(8,128)(2,1)S(1)}, u32[]{:S(2)}, u32[]{:S(2)}) collective-permute-start(bf16[64,512]{1,0:T(8,128)(2,1)} %param.11), channel_id=1, source_target_pairs={{0,504},{8,0},{16,8},{24,16},{32,24},{40,32},{48,40},{56,48},{64,5... | collective-permute-start | bytes 196616 | tf_op jit(solution)/shard_map/ppermute | solution.py:42
  22.0 29.9 %collective-permute-start.2 = (bf16[192,512]{1,0:T(8,128)(2,1)S(1)}, bf16[192,512]{1,0:T(8,128)(2,1)S(1)}, u32[]{:S(2)}, u32[]{:S(2)}) collective-permute-start(bf16[192,512]{1,0:T(8,128)(2,1)S(1)} %constant_dynamic-update-slice_fusion.mid), channel_id=1, source_target_pairs={{0,24},{8,32},{16,40},{24,48},{32,56},{40,64},{48,72},{56,80},{64,... | collective-permute-start | bytes 589832 | tf_op jit(solution)/shard_map/ppermute | solution.py:42
  23.9 28.0 %collective-permute-start.3 = (bf16[192,512]{1,0:T(8,128)(2,1)S(1)}, bf16[192,512]{1,0:T(8,128)(2,1)S(1)}, u32[]{:S(2)}, u32[]{:S(2)}) collective-permute-start(bf16[192,512]{1,0:T(8,128)(2,1)S(1)} %constant_dynamic-update-slice_fusion.mid), channel_id=1, source_target_pairs={{0,488},{8,496},{16,504},{24,0},{32,8},{40,16},{48,24},{56,32},{64... | collective-permute-start | bytes 589832 | tf_op jit(solution)/shard_map/ppermute | solution.py:42
  29.9 11.2 %collective-permute-start.10 = (bf16[128,512]{1,0:T(8,128)(2,1)S(1)}, bf16[128,512]{1,0:T(8,128)(2,1)S(1)}, u32[]{:S(2)}, u32[]{:S(2)}) collective-permute-start(bf16[128,512]{1,0:T(8,128)(2,1)S(1)} %get-tuple-element.21), channel_id=1, source_target_pairs={{0,4},{2,6},{4,0},{6,2},{1,5},{3,7},{5,1},{7,3},{8,12},{10,14},{12... | collective-permute-start | bytes 393224 | tf_op jit(solution)/shard_map/ppermute | solution.py:42
  34.6 6.9 %collective-permute-start.8 = (bf16[128,512]{1,0:T(8,128)(2,1)S(1)}, bf16[128,512]{1,0:T(8,128)(2,1)S(1)}, u32[]{:S(2)}, u32[]{:S(2)}) collective-permute-start(bf16[128,512]{1,0:T(8,128)(2,1)S(1)} %get-tuple-element.19), channel_id=1, source_target_pairs={{0,2},{2,4},{4,6},{6,0},{1,3},{3,5},{5,7},{7,1},{8,10},{10,12},{12... | collective-permute-start | bytes 393224 | tf_op jit(solution)/shard_map/ppermute | solution.py:42
  36.8 6.2 %collective-permute-start.9 = (bf16[128,512]{1,0:T(8,128)(2,1)S(1)}, bf16[128,512]{1,0:T(8,128)(2,1)S(1)}, u32[]{:S(2)}, u32[]{:S(2)}) collective-permute-start(bf16[128,512]{1,0:T(8,128)(2,1)S(1)} %get-tuple-element.20), channel_id=1, source_target_pairs={{0,6},{2,0},{4,2},{6,4},{1,7},{3,1},{5,3},{7,5},{8,14},{10,8},{12,... | collective-permute-start | bytes 393224 | tf_op jit(solution)/shard_map/ppermute | solution.py:42
  43.1 38.7 %copy-start = (bf16[4,128,512]{2,1,0:T(8,128)(2,1)S(1)}, bf16[4,128,512]{2,1,0:T(8,128)(2,1)}, u32[]{:S(2)}) copy-start(bf16[4,128,512]{2,1,0:T(8,128)(2,1)} %taper) | copy-start | bytes 1572868
  43.1 18.4 %collective-permute-start.11 = (bf16[64,512]{1,0:T(8,128)(2,1)S(1)}, bf16[64,512]{1,0:T(8,128)(2,1)S(1)}, u32[]{:S(2)}, u32[]{:S(2)}) collective-permute-start(bf16[64,512]{1,0:T(8,128)(2,1)S(1)} %shard_map.87), channel_id=1, source_target_pairs={{0,8},{8,16},{16,24},{24,32},{32,40},{40,48},{48,56},{56,64},{64,7... | collective-permute-start | bytes 196616 | tf_op jit(solution)/shard_map/ppermute | solution.py:42
  45.2 16.3 %collective-permute-start.12 = (bf16[64,512]{1,0:T(8,128)(2,1)S(1)}, bf16[64,512]{1,0:T(8,128)(2,1)S(1)}, u32[]{:S(2)}, u32[]{:S(2)}) collective-permute-start(bf16[64,512]{1,0:T(8,128)(2,1)S(1)} %shard_map.87), channel_id=1, source_target_pairs={{0,504},{8,0},{16,8},{24,16},{32,24},{40,32},{48,40},{56,48},{64,5... | collective-permute-start | bytes 196616 | tf_op jit(solution)/shard_map/ppermute | solution.py:42
  52.1 26.1 %collective-permute-start.4 = (bf16[384,512]{1,0:T(8,128)(2,1)S(1)}, bf16[384,512]{1,0:T(8,128)(2,1)S(1)}, u32[]{:S(2)}, u32[]{:S(2)}) collective-permute-start(bf16[384,512]{1,0:T(8,128)(2,1)S(1)} %shard_map.83.refs_0_), channel_id=1, source_target_pairs={{0,6},{2,0},{4,2},{6,4},{1,7},{3,1},{5,3},{7,5},{8,14},{10,8},{12,... | collective-permute-start | bytes 1179656 | tf_op jit(solution)/shard_map/ppermute | solution.py:42
  57.1 24.2 %collective-permute-start.5 = (bf16[384,512]{1,0:T(8,128)(2,1)S(1)}, bf16[384,512]{1,0:T(8,128)(2,1)S(1)}, u32[]{:S(2)}, u32[]{:S(2)}) collective-permute-start(bf16[384,512]{1,0:T(8,128)(2,1)S(1)} %shard_map.83.refs_0_), channel_id=1, source_target_pairs={{0,4},{2,6},{4,0},{6,2},{1,5},{3,7},{5,1},{7,3},{8,12},{10,14},{12... | collective-permute-start | bytes 1179656 | tf_op jit(solution)/shard_map/ppermute | solution.py:42
  59.0 22.3 %collective-permute-start.6 = (bf16[384,512]{1,0:T(8,128)(2,1)S(1)}, bf16[384,512]{1,0:T(8,128)(2,1)S(1)}, u32[]{:S(2)}, u32[]{:S(2)}) collective-permute-start(bf16[384,512]{1,0:T(8,128)(2,1)S(1)} %shard_map.83.refs_0_), channel_id=1, source_target_pairs={{0,2},{2,4},{4,6},{6,0},{1,3},{3,5},{5,7},{7,1},{8,10},{10,12},{12... | collective-permute-start | bytes 1179656 | tf_op jit(solution)/shard_map/ppermute | solution.py:42
  61.5 8.8 %collective-permute-start.13 = (bf16[192,512]{1,0:T(8,128)(2,1)S(1)}, bf16[192,512]{1,0:T(8,128)(2,1)S(1)}, u32[]{:S(2)}, u32[]{:S(2)}) collective-permute-start(bf16[192,512]{1,0:T(8,128)(2,1)S(1)} %pad_maximum_fusion.mid), channel_id=1, source_target_pairs={{0,24},{8,32},{16,40},{24,48},{32,56},{40,64},{48,72},{56,80},{64,... | collective-permute-start | bytes 589832 | tf_op jit(solution)/shard_map/ppermute | solution.py:42
  63.5 8.1 %collective-permute-start.14 = (bf16[192,512]{1,0:T(8,128)(2,1)S(1)}, bf16[192,512]{1,0:T(8,128)(2,1)S(1)}, u32[]{:S(2)}, u32[]{:S(2)}) collective-permute-start(bf16[192,512]{1,0:T(8,128)(2,1)S(1)} %pad_maximum_fusion.mid), channel_id=1, source_target_pairs={{0,488},{8,496},{16,504},{24,0},{32,8},{40,16},{48,24},{56,32},{64... | collective-permute-start | bytes 589832 | tf_op jit(solution)/shard_map/ppermute | solution.py:42
  71.7 14.0 %collective-permute-start.17 = (bf16[384,512]{1,0:T(8,128)(2,1)S(1)}, bf16[384,512]{1,0:T(8,128)(2,1)S(1)}, u32[]{:S(2)}, u32[]{:S(2)}) collective-permute-start(bf16[384,512]{1,0:T(8,128)(2,1)S(1)} %shard_map.88.rows), channel_id=1, source_target_pairs={{0,2},{2,4},{4,6},{6,0},{1,3},{3,5},{5,7},{7,1},{8,10},{10,12},{12... | collective-permute-start | bytes 1179656 | tf_op jit(solution)/shard_map/ppermute | solution.py:42
  75.7 10.6 %collective-permute-start.16 = (bf16[384,512]{1,0:T(8,128)(2,1)S(1)}, bf16[384,512]{1,0:T(8,128)(2,1)S(1)}, u32[]{:S(2)}, u32[]{:S(2)}) collective-permute-start(bf16[384,512]{1,0:T(8,128)(2,1)S(1)} %shard_map.88.rows), channel_id=1, source_target_pairs={{0,6},{2,0},{4,2},{6,4},{1,7},{3,1},{5,3},{7,5},{8,14},{10,8},{12,... | collective-permute-start | bytes 1179656 | tf_op jit(solution)/shard_map/ppermute | solution.py:42
  78.2 14.8 %collective-permute-start.15 = (bf16[384,512]{1,0:T(8,128)(2,1)S(1)}, bf16[384,512]{1,0:T(8,128)(2,1)S(1)}, u32[]{:S(2)}, u32[]{:S(2)}) collective-permute-start(bf16[384,512]{1,0:T(8,128)(2,1)S(1)} %shard_map.88.rows), channel_id=1, source_target_pairs={{0,4},{2,6},{4,0},{6,2},{1,5},{3,7},{5,1},{7,3},{8,12},{10,14},{12... | collective-permute-start | bytes 1179656 | tf_op jit(solution)/shard_map/ppermute | solution.py:42
  94.6 8.5 %collective-permute-start.18 = (f32[512,512]{1,0:T(8,128)S(1)}, f32[512,512]{1,0:T(8,128)S(1)}, u32[]{:S(2)}, u32[]{:S(2)}) collective-permute-start(f32[512,512]{1,0:T(8,128)S(1)} %shard_map.95), channel_id=1, source_target_pairs={{0,1},{1,0},{2,3},{3,2},{4,5},{5,4},{6,7},{7,6},{8,9},{9,8},{10,11... | collective-permute-start | bytes 3145736 | tf_op jit(solution)/shard_map/ppermute | solution.py:42

commit v4 on v3

--- a/solution.py
+++ b/solution.py
@@ -76,9 +76,8 @@
 
 def columns(meta, weights, owned):
     parts = []
-    for r in range(RELS):
-        chip = lax.rem(meta[CHIP] + r, RELS)
-        block = weights(pl.ds(pl.multiple_of(chip * 2 * owned, 2 * owned), 2 * owned))
+    for chip in range(RELS):
+        block = weights(slice(chip * 2 * owned, (chip + 1) * 2 * owned))
         flipped = jnp.concatenate([block, block], axis=0).T
         parts.append(jnp.where(meta[CORE] == 0, flipped[:owned], flipped[owned:]))
     return jnp.concatenate(parts, axis=0)
@@ -86,8 +85,7 @@
 
 def rows_of(meta, foot, owned):
     parts = []
-    for r in range(RELS):
-        chip = lax.rem(meta[CHIP] + r, RELS)
+    for chip in range(RELS):
         start = pl.multiple_of(chip * 2 * owned + meta[CORE] * owned, owned)
         parts.append(foot[pl.ds(start, owned), :])
     return jnp.concatenate(parts, axis=0)
@@ -112,8 +110,9 @@
     project(rows_of(meta, foot, owned), column, cells, out, True)
 
 
-def other_body(meta, foot, cells, before, mine, pay1, pay2, pay3, acc):
-    owned, members = mine.shape
+def other_body(meta, foot, cells, before, pay, acc):
+    members = acc.shape[1]
+    owned = acc.shape[0] // RELS
 
     def weights(at):
         terms = cells[members:, at].astype(F32)
@@ -121,53 +120,36 @@
 
     acc[...] = before[...]
     project(rows_of(meta, foot, owned), columns(meta, weights, owned), cells, acc, False)
-    slot = lax.broadcasted_iota(jnp.int32, mine.shape, 0) + meta[CORE] * owned
-    for r, pay in enumerate((mine, pay1, pay2, pay3)):
-        chip = lax.rem(meta[CHIP] + r, RELS)
+    slot = lax.broadcasted_iota(jnp.int32, (owned, members), 0) + meta[CORE] * owned
+    for chip in range(RELS):
         present = slot + chip * 2 * owned < meta[COUNT]
-        part = jnp.where(present, acc[r * owned : (r + 1) * owned], 0.0)
-        if r == 0:
-            mine[...] = part
-        else:
-            high = part.astype(BF16)
-            pay[:owned] = high
-            pay[owned:] = (part - high.astype(F32)).astype(BF16)
-
-
-def fold_body(mine, *refs):
-    out = refs[-1]
-    owned = out.shape[0]
-    total = mine[...]
-    for got in refs[:-1]:
-        total = total + (got[:owned].astype(F32) + got[owned:].astype(F32))
-    out[...] = total.astype(BF16)
-
-
-def flip_body(*refs):
-    out = refs[-1]
-    wide = refs[0].shape[0]
-    for r, rows in enumerate(refs[:-1]):
-        out[:, r * wide : (r + 1) * wide] = rows[...].T
-
-
-def choose(meta, k, sources, size, store):
-    group = meta[k] // 3
-    start = pl.multiple_of(lax.rem(meta[k], 3) * size, size)
-    for g, source in enumerate(sources):
-
-        @pl.when(group == g)
-        def _(source=source):
-            store(source[pl.ds(start, size), :])
+        part = jnp.where(present, acc[chip * owned : (chip + 1) * owned], 0.0)
+        high = part.astype(BF16)
+        pay[chip, :owned] = high
+        pay[chip, owned:] = (part - high.astype(F32)).astype(BF16)
+
+
+def fold_body(got, duals, out):
+    owned = duals.shape[0]
+    total = got[0, :owned].astype(F32) + got[0, owned:].astype(F32)
+    for chip in range(1, RELS):
+        total = total + (got[chip, :owned].astype(F32) + got[chip, owned:].astype(F32))
+    out[:owned] = total.astype(BF16)
+    out[owned:] = duals[...]
 
 
 def pick_body(meta, low, mid, high, out):
-    size = out.shape[0] // NEAR
+    size = out.shape[0] // (2 * NEAR)
     for k in range(NEAR):
-
-        def store(value, k=k):
-            out[k * size : (k + 1) * size] = value
-
-        choose(meta, k, (low, mid, high), size, store)
+        group = meta[k] // 3
+        start = pl.multiple_of(lax.rem(meta[k], 3) * (2 * size), 2 * size)
+        for g, source in enumerate((low, mid, high)):
+
+            @pl.when(group == g)
+            def _(k=k, start=start, source=source):
+                out[k * size : (k + 1) * size] = source[pl.ds(start, size), :]
+                at = (NEAR + k) * size
+                out[at : at + size] = source[pl.ds(pl.multiple_of(start + size, size), size), :]
 
 
 def taper_body(meta, taper, out, tall):
@@ -182,28 +164,23 @@
             out[r, k * owned : (k + 1) * owned] = tall[meta[CLASS + k], pl.ds(start, owned), :]
 
 
-def covary_body(rel, rows, own, other, scaled, *refs):
-    out = refs[-1]
+def analyse_body(rel, halves, rows, scaled, *refs):
+    count = len(halves)
+    cells, before = refs[:count], refs[count:-count - 1]
+    outs, flipped = refs[-count - 1 : -1], refs[-1]
     members = rows.shape[1]
-    size = rows.shape[0]
-    half = own.shape[1]
+    size = rows.shape[0] // 2
     step = 256
     taper = scaled[rel]
     wide = jnp.concatenate([taper] * (step // taper.shape[1]), axis=1)
-    for h, cells in enumerate((own, other)):
-        for at in range(0, half, step):
-            covar = jnp.dot(rows[...], cells[:members, at : at + step], preferred_element_type=F32)
+    flipped[...] = rows[size:, :].T
+    for h in range(count):
+        for at in range(0, outs[h].shape[1], step):
+            span = slice(at, at + step)
+            covar = jnp.dot(rows[:size], cells[h][:members, span], preferred_element_type=F32)
             tapered = (covar * wide).astype(BF16)
-            out[rel * size : (rel + 1) * size, h * half + at : h * half + at + step] = tapered
-
-
-def gain_body(h, duals, tapered, out):
-    half = out.shape[1]
-    step = 256
-    for at in range(0, half, step):
-        out[:, at : at + step] = jnp.dot(
-            duals[...], tapered[:, h * half + at : h * half + at + step], preferred_element_type=F32
-        )
+            gained = jnp.dot(flipped[...], tapered, preferred_element_type=F32)
+            outs[h][:, span] = before[h][:, span] + gained if before else gained
 
 
 def finish_body(mine, theirs, out, held, done):
@@ -230,7 +207,6 @@
     members, levels, points = anomalies.shape
     owned = dual_rows.shape[0]
     tile = ("z", "y")
-    w_low, w_high = move(dual_rows, tile, 1), move(dual_rows, tile, -1)
     raw = anomalies.reshape(members * levels, points)
     meta, own, weights, foot = kernel(
         pack_body,
@@ -260,26 +236,26 @@
     (begun,) = kernel(
         own_body, [array((rows, members), F32)], [meta, foot, own, weights], work, scalars=1
     )
-    pay = array((2 * owned, members), BF16)
-    mine, pay1, pay2, pay3 = kernel(
+    (pay,) = kernel(
         other_body,
-        [array((owned, members), F32), pay, pay, pay],
+        [array((RELS, 2 * owned, members), BF16)],
         [meta, foot, other, begun],
         work,
         scalars=1,
         scratch=[pltpu.VMEM((rows, members), F32)],
     )
-    got1, got3, got2 = move(pay1, "x", 1), move(pay3, "x", -1), move(pay2, "x", 2)
-    w_mid = jnp.concatenate([w_low, dual_rows, w_high], axis=0)
-    w_far_low, w_far_high = move(w_mid, tile, 3), move(w_mid, tile, -3)
-    (rows_y,) = kernel(fold_body, [array((owned, members), BF16)], [mine, got1, got3, got2], 1e8)
-    y_low, y_high = move(rows_y, tile, 1), move(rows_y, tile, -1)
-    chosen = [array((NEAR * owned, members), BF16)]
-    (w0,) = kernel(pick_body, chosen, [meta, w_far_low, w_mid, w_far_high], 1e8, scalars=1)
-    w3, w1, w2 = move(w0, "x", 1), move(w0, "x", -1), move(w0, "x", 2)
-    y_mid = jnp.concatenate([y_low, rows_y, y_high], axis=0)
-    y_far_low, y_far_high = move(y_mid, tile, 3), move(y_mid, tile, -3)
-    (y0,) = kernel(pick_body, chosen, [meta, y_far_low, y_mid, y_far_high], 1e8, scalars=1)
+    got = lax.all_to_all(pay, "x", 0, 0, tiled=True)
+    (here,) = kernel(fold_body, [array((2 * owned, members), BF16)], [got, dual_rows], 1e8)
+    low, high = move(here, tile, 1), move(here, tile, -1)
+    mid = jnp.concatenate([low, here, high], axis=0)
+    far_low, far_high = move(mid, tile, 3), move(mid, tile, -3)
+    (y0,) = kernel(
+        pick_body,
+        [array((2 * NEAR * owned, members), BF16)],
+        [meta, far_low, mid, far_high],
+        1e8,
+        scalars=1,
+    )
     y3, y1, y2 = move(y0, "x", 1), move(y0, "x", -1), move(y0, "x", 2)
 
     taper_late, _ = lax.optimization_barrier((taper_blocks, y0))
@@ -292,26 +268,27 @@
         scratch=[pltpu.VMEM((taper_blocks.shape[0], taper_blocks.shape[2], points), F32)],
     )
     width = levels * points
-    tapered = None
-    for rel, got in ((0, y0), (3, y3), (1, y1), (2, y2)):
-        inputs = [got, own, other, scaled] + ([] if tapered is None else [tapered])
-        (tapered,) = kernel(
-            functools.partial(covary_body, rel),
-            [array((NEAR * rows, 2 * width), BF16)],
-            inputs,
-            4 * NEAR * owned * members * width,
-            aliases={} if tapered is None else {4: 0},
+    sums = [None, None]
+    planes = [own, other]
+    for rel, got, halves in (
+        (0, y0, (0, 1)),
+        (3, y3, (0, 1)),
+        (1, y1, (0, 1)),
+        (2, y2, (1,)),
+        (2, y2, (0,)),
+    ):
+        cells = [planes[h] for h in halves]
+        before = [sums[h] for h in halves if sums[h] is not None]
+        gained = kernel(
+            functools.partial(analyse_body, rel, halves),
+            [array((members, width), F32)] * len(halves),
+            [got, scaled, *cells, *before],
+            4 * NEAR * owned * members * width * len(halves),
+            scratch=[pltpu.VMEM((members, NEAR * owned), BF16)],
+            aliases={2 + len(halves) + i: i for i in range(len(before))},
         )
-    (duals,) = kernel(flip_body, [array((members, NEAR * rows), BF16)], [w0, w1, w2, w3], 1e9)
-    sums = [
-        kernel(
-            functools.partial(gain_body, h),
-            [array((members, width), F32)],
-            [duals, tapered],
-            2 * NEAR * rows * members * width,
-        )[0]
-        for h in (0, 1)
-    ]
+        for h, g in zip(halves, gained):
+            sums[h] = g
     theirs = move(sums[1], "c", 1)
     (out,) = kernel(
         finish_body,

time: 105 us -> 100 us (0.952)
  starting transfers between devices: 78.7 us -> 45.7 us
  waiting for transfers between devices: 15.4 us -> 31.5 us
  blocking collectives: 0 us -> 11.7 us
  Pallas kernels: 8.71 us -> 10.4 us
    ppermute x19 -> x9, starting transfers between devices: 78.7 us -> 45.7 us  [move(): lax.ppermute(value, axis, [(i, (i + steps) % count) for i in range(count)])]
    ppermute x19 -> x9, waiting for transfers between devices: 15.4 us -> 31.5 us  [move(): lax.ppermute(value, axis, [(i, (i + steps) % count) for i in range(count)])]
    all_to_all x0 -> x1, blocking collectives: none -> 11.7 us  [shards(): got = lax.all_to_all(pay, 'x', 0, 0, tiled=True)]
    pallas_call x15 -> x12, Pallas kernels: 8.71 us -> 10.4 us  [kernel(): pl.pallas_call(body, out_shape=[o if m is None else m(o.shape, o.dtype) f...]
  transfers between devices with their start and end apart: 19 -> 9, of which waited for: 9 -> 8; matrix products, arithmetic and copies ran while one was open for 1% -> 0% of each run, Pallas kernels for 5% -> 6%
where the time goes in v4:
time: 100 us; the launch traced here: 99.6 us
  starting transfers between devices  45.7 us (46%)
  waiting for transfers between devices  31.5 us (32%)
  blocking collectives  11.7 us (12%)
  Pallas kernels  10.4 us (10%)
    ppermute x9, starting transfers between devices, move(): lax.ppermute(value, axis, [(i, (i + steps) % count) for i in range(count)])  45.7 us
    ppermute x9, waiting for transfers between devices, move(): lax.ppermute(value, axis, [(i, (i + steps) % count) for i in range(count)])  31.5 us
    all_to_all x1, blocking collectives, shards(): got = lax.all_to_all(pay, 'x', 0, 0, tiled=True)  11.7 us
    pallas_call x12, Pallas kernels, kernel(): pl.pallas_call(body, out_shape=[o if m is None else m(o.shape, o.dtype) f...  10.4 us
  transfers between devices with their start and end apart: 9, of which 8 were waited for; matrix products, arithmetic and copies ran while one was open for 0% of the time, Pallas kernels for 6%

profile of v4, /device:TPU:1, one launch (start us, length us, event | category | flops | bytes accessed | tf_op | source)
XLA Modules:
  0.0 99.6 jit_solution(8833891372038537163)
XLA Ops:
  0.0 1.3 %shard_map.82 = (s32[16]{0:T(128)S(4)}, bf16[528,512]{1,0:T(8,128)(2,1)S(1)}, f32[4,512]{1,0:T(4,128)S(1)}, bf16[512,128]{1,0:T(8,128)(2,1)S(1)}) custom-call(s32[6,64]{1,0:T(8,128)} %bitcast.4, s32[64]{0:T(128)} %refs_1_.1, s32[1,6]{1,0:T(1,128)} %refs_2_.1, bf16[2048,128]{1,0:T(8,128)(2,1)} %bitcast.3, f32[4,512]{1,0:T(4,128)} %refs_4_.1, ...), custom_call_target="tpu_custom_call" | custom-call | flops 100000000 | bytes 1000000 | tf_op jit(solution)/shard_map/pallas_call | solution.py:24
  1.3 8.7 %collective-permute-start = (bf16[528,512]{1,0:T(8,128)(2,1)S(1)}, bf16[528,512]{1,0:T(8,128)(2,1)S(1)}, u32[]{:S(2)}, u32[]{:S(2)}) collective-permute-start(bf16[528,512]{1,0:T(8,128)(2,1)S(1)} %get-tuple-element.18.cells.refs_0_), channel_id=1, source_target_pairs={{0,1},{1,0},{2,3},{3,2},{4,5},{5,4},{6,7},{7,6},{8,9},{9,8},{10,11... | collective-permute-start | bytes 1622024 | tf_op jit(solution)/shard_map/ppermute | solution.py:42
  10.1 0.5 shard_map.83.before
  10.6 1.0 %collective-permute-done.cells.refs_1_.refs_0_ = bf16[528,512]{1,0:T(8,128)(2,1)S(1)} collective-permute-done((bf16[528,512]{1,0:T(8,128)(2,1)S(1)}, bf16[528,512]{1,0:T(8,128)(2,1)S(1)}, u32[]{:S(2)}, u32[]{:S(2)}) %collective-permute-start) | collective-permute-done | bytes 540704 | tf_op jit(solution)/shard_map/ppermute | solution.py:42
  11.6 0.5 shard_map.84
  12.2 0.0 copy-start
  12.2 11.7 %all_to_all.5.got = bf16[4,128,512]{2,1,0:T(8,128)(2,1)S(1)} all-to-all(bf16[4,128,512]{2,1,0:T(8,128)(2,1)S(1)} %shard_map.84), channel_id=1, replica_groups=mesh['z'=16,'y'=4,'x'=4,'c'=2] {'x'}, dimensions={0} | all-to-all | bytes 1048576 | tf_op jit(solution)/shard_map/all_to_all | solution.py:247
  23.9 0.0 copy-done
  23.9 0.1 shard_map.85
  24.0 1.9 %collective-permute-start.1 = (bf16[128,512]{1,0:T(8,128)(2,1)S(1)}, bf16[128,512]{1,0:T(8,128)(2,1)S(1)}, u32[]{:S(2)}, u32[]{:S(2)}) collective-permute-start(bf16[128,512]{1,0:T(8,128)(2,1)S(1)} %shard_map.85), channel_id=1, source_target_pairs={{0,8},{8,16},{16,24},{24,32},{32,40},{40,48},{48,56},{56,64},{64,7... | collective-permute-start | bytes 393224 | tf_op jit(solution)/shard_map/ppermute | solution.py:42
  25.9 9.1 %collective-permute-start.2 = (bf16[128,512]{1,0:T(8,128)(2,1)S(1)}, bf16[128,512]{1,0:T(8,128)(2,1)S(1)}, u32[]{:S(2)}, u32[]{:S(2)}) collective-permute-start(bf16[128,512]{1,0:T(8,128)(2,1)S(1)} %shard_map.85), channel_id=1, source_target_pairs={{0,504},{8,0},{16,8},{24,16},{32,24},{40,32},{48,40},{56,48},{64,5... | collective-permute-start | bytes 393224 | tf_op jit(solution)/shard_map/ppermute | solution.py:42
  35.0 0.4 collective-permute-done.1
  35.4 1.5 %collective-permute-done.2 = bf16[128,512]{1,0:T(8,128)(2,1)S(1)} collective-permute-done((bf16[128,512]{1,0:T(8,128)(2,1)S(1)}, bf16[128,512]{1,0:T(8,128)(2,1)S(1)}, u32[]{:S(2)}, u32[]{:S(2)}) %collective-permute-start.2) | collective-permute-done | bytes 131104 | tf_op jit(solution)/shard_map/ppermute | solution.py:42
  37.0 0.0 copy-start.1
  37.0 2.1 %collective-permute-start.3 = (bf16[384,512]{1,0:T(8,128)(2,1)S(1)}, bf16[384,512]{1,0:T(8,128)(2,1)S(1)}, u32[]{:S(2)}, u32[]{:S(2)}) collective-permute-start(bf16[384,512]{1,0:T(8,128)(2,1)S(1)} %pad_maximum_fusion.mid), channel_id=1, source_target_pairs={{0,24},{8,32},{16,40},{24,48},{32,56},{40,64},{48,72},{56,80},{64,... | collective-permute-start | bytes 1179656 | tf_op jit(solution)/shard_map/ppermute | solution.py:42
  39.0 5.5 %collective-permute-start.4 = (bf16[384,512]{1,0:T(8,128)(2,1)S(1)}, bf16[384,512]{1,0:T(8,128)(2,1)S(1)}, u32[]{:S(2)}, u32[]{:S(2)}) collective-permute-start(bf16[384,512]{1,0:T(8,128)(2,1)S(1)} %pad_maximum_fusion.mid), channel_id=1, source_target_pairs={{0,488},{8,496},{16,504},{24,0},{32,8},{40,16},{48,24},{56,32},{64... | collective-permute-start | bytes 1179656 | tf_op jit(solution)/shard_map/ppermute | solution.py:42
  44.5 4.6 %collective-permute-done.3.low = bf16[384,512]{1,0:T(8,128)(2,1)S(1)} collective-permute-done((bf16[384,512]{1,0:T(8,128)(2,1)S(1)}, bf16[384,512]{1,0:T(8,128)(2,1)S(1)}, u32[]{:S(2)}, u32[]{:S(2)}) %collective-permute-start.3) | collective-permute-done | bytes 393248 | tf_op jit(solution)/shard_map/ppermute | solution.py:42
  49.1 1.0 %collective-permute-done.4.high = bf16[384,512]{1,0:T(8,128)(2,1)S(1)} collective-permute-done((bf16[384,512]{1,0:T(8,128)(2,1)S(1)}, bf16[384,512]{1,0:T(8,128)(2,1)S(1)}, u32[]{:S(2)}, u32[]{:S(2)}) %collective-permute-start.4) | collective-permute-done | bytes 393248 | tf_op jit(solution)/shard_map/ppermute | solution.py:42
  50.2 0.2 shard_map.86.rows
  50.4 2.2 %collective-permute-start.7 = (bf16[768,512]{1,0:T(8,128)(2,1)S(1)}, bf16[768,512]{1,0:T(8,128)(2,1)S(1)}, u32[]{:S(2)}, u32[]{:S(2)}) collective-permute-start(bf16[768,512]{1,0:T(8,128)(2,1)S(1)} %shard_map.86.rows), channel_id=1, source_target_pairs={{0,2},{2,4},{4,6},{6,0},{1,3},{3,5},{5,7},{7,1},{8,10},{10,12},{12... | collective-permute-start | bytes 2359304 | tf_op jit(solution)/shard_map/ppermute | solution.py:42
  52.6 4.3 %collective-permute-start.6 = (bf16[768,512]{1,0:T(8,128)(2,1)S(1)}, bf16[768,512]{1,0:T(8,128)(2,1)S(1)}, u32[]{:S(2)}, u32[]{:S(2)}) collective-permute-start(bf16[768,512]{1,0:T(8,128)(2,1)S(1)} %shard_map.86.rows), channel_id=1, source_target_pairs={{0,6},{2,0},{4,2},{6,4},{1,7},{3,1},{5,3},{7,5},{8,14},{10,8},{12,... | collective-permute-start | bytes 2359304 | tf_op jit(solution)/shard_map/ppermute | solution.py:42
  56.9 1.9 %collective-permute-start.5 = (bf16[768,512]{1,0:T(8,128)(2,1)S(1)}, bf16[768,512]{1,0:T(8,128)(2,1)S(1)}, u32[]{:S(2)}, u32[]{:S(2)}) collective-permute-start(bf16[768,512]{1,0:T(8,128)(2,1)S(1)} %shard_map.86.rows), channel_id=1, source_target_pairs={{0,4},{2,6},{4,0},{6,2},{1,5},{3,7},{5,1},{7,3},{8,12},{10,14},{12... | collective-permute-start | bytes 2359304 | tf_op jit(solution)/shard_map/ppermute | solution.py:42
  58.8 0.0 copy-done.1
  58.8 0.3 shard_map.87.scaled
  59.1 1.4 %shard_map.88 = (f32[512,512]{1,0:T(8,128)S(1)}, f32[512,512]{1,0:T(8,128)S(1)}) custom-call(bf16[768,512]{1,0:T(8,128)(2,1)S(1)} %shard_map.86.rows, f32[4,384,128]{2,1,0:T(8,128)S(1)} %shard_map.87.scaled, bf16[528,512]{1,0:T(8,128)(2,1)S(1)} %get-tuple-element.18.cells.refs_0_, bf16[528,512]{1,0:T(8,128)(2,1)S(1)} %collective-permute-done.cells.refs_1_.refs_0_), custom_call_target="tpu_custom_call" | custom-call | flops 805306368 | bytes 1000000 | tf_op jit(solution)/shard_map/pallas_call | solution.py:24
  60.5 9.0 %collective-permute-done.7.rows = bf16[768,512]{1,0:T(8,128)(2,1)S(1)} collective-permute-done((bf16[768,512]{1,0:T(8,128)(2,1)S(1)}, bf16[768,512]{1,0:T(8,128)(2,1)S(1)}, u32[]{:S(2)}, u32[]{:S(2)}) %collective-permute-start.7) | collective-permute-done | bytes 786464 | tf_op jit(solution)/shard_map/ppermute | solution.py:42
  69.5 1.5 %shard_map.89 = (f32[512,512]{1,0:T(8,128)S(1)}, f32[512,512]{1,0:T(8,128)S(1)}) custom-call(bf16[768,512]{1,0:T(8,128)(2,1)S(1)} %collective-permute-done.7.rows, f32[4,384,128]{2,1,0:T(8,128)S(1)} %shard_map.87.scaled, bf16[528,512]{1,0:T(8,128)(2,1)S(1)} %get-tuple-element.18.cells.refs_0_, ...), custom_call_target="tpu_custom_call", output_to_operand_aliasing={{0}: (4, {}), {1}: (5, {})} | custom-call | flops 805306368 | bytes 1000000 | tf_op jit(solution)/shard_map/pallas_call | solution.py:24
  71.0 0.0 collective-permute-done.6.rows
  71.0 1.5 %shard_map.90 = (f32[512,512]{1,0:T(8,128)S(1)}, f32[512,512]{1,0:T(8,128)S(1)}) custom-call(bf16[768,512]{1,0:T(8,128)(2,1)S(1)} %collective-permute-done.6.rows, f32[4,384,128]{2,1,0:T(8,128)S(1)} %shard_map.87.scaled, bf16[528,512]{1,0:T(8,128)(2,1)S(1)} %get-tuple-element.18.cells.refs_0_, ...), custom_call_target="tpu_custom_call", output_to_operand_aliasing={{0}: (4, {}), {1}: (5, {})} | custom-call | flops 805306368 | bytes 1000000 | tf_op jit(solution)/shard_map/pallas_call | solution.py:24
  72.5 12.7 %collective-permute-done.5.rows = bf16[768,512]{1,0:T(8,128)(2,1)S(1)} collective-permute-done((bf16[768,512]{1,0:T(8,128)(2,1)S(1)}, bf16[768,512]{1,0:T(8,128)(2,1)S(1)}, u32[]{:S(2)}, u32[]{:S(2)}) %collective-permute-start.5) | collective-permute-done | bytes 786464 | tf_op jit(solution)/shard_map/ppermute | solution.py:42
  85.2 1.1 %shard_map.92 = f32[512,512]{1,0:T(8,128)S(1)} custom-call(bf16[768,512]{1,0:T(8,128)(2,1)S(1)} %collective-permute-done.5.rows, f32[4,384,128]{2,1,0:T(8,128)S(1)} %shard_map.87.scaled, bf16[528,512]{1,0:T(8,128)(2,1)S(1)} %collective-permute-done.cells.refs_1_.refs_0_, f32[512,512]{1,0:T(8,128)S(1)} %get-tuple-element.26.refs_1_), custom_call_target="tpu_custom_call", output_to_operand_aliasing={{}: (3, {})} | custom-call | flops 402653184 | bytes 1000000 | tf_op jit(solution)/shard_map/pallas_call | solution.py:24
  86.3 10.0 %collective-permute-start.8 = (f32[512,512]{1,0:T(8,128)S(1)}, f32[512,512]{1,0:T(8,128)S(1)}, u32[]{:S(2)}, u32[]{:S(2)}) collective-permute-start(f32[512,512]{1,0:T(8,128)S(1)} %shard_map.92), channel_id=1, source_target_pairs={{0,1},{1,0},{2,3},{3,2},{4,5},{5,4},{6,7},{7,6},{8,9},{9,8},{10,11... | collective-permute-start | bytes 3145736 | tf_op jit(solution)/shard_map/ppermute | solution.py:42
  96.3 1.1 %shard_map.91.mine = f32[512,512]{1,0:T(8,128)S(1)} custom-call(bf16[768,512]{1,0:T(8,128)(2,1)S(1)} %collective-permute-done.5.rows, f32[4,384,128]{2,1,0:T(8,128)S(1)} %shard_map.87.scaled, bf16[528,512]{1,0:T(8,128)(2,1)S(1)} %get-tuple-element.18.cells.refs_0_, f32[512,512]{1,0:T(8,128)S(1)} %get-tuple-element.25.refs_1_), custom_call_target="tpu_custom_call", output_to_operand_aliasing={{}: (3, {})} | custom-call | flops 402653184 | bytes 1000000 | tf_op jit(solution)/shard_map/pallas_call | solution.py:24
  97.4 1.1 %collective-permute-done.8.theirs = f32[512,512]{1,0:T(8,128)S(1)} collective-permute-done((f32[512,512]{1,0:T(8,128)S(1)}, f32[512,512]{1,0:T(8,128)S(1)}, u32[]{:S(2)}, u32[]{:S(2)}) %collective-permute-start.8) | collective-permute-done | bytes 1048608 | tf_op jit(solution)/shard_map/ppermute | solution.py:42
  98.5 1.0 %shard_map.93 = f32[2048,128]{1,0:T(8,128)} custom-call(f32[512,512]{1,0:T(8,128)S(1)} %shard_map.91.mine, f32[512,512]{1,0:T(8,128)S(1)} %collective-permute-done.8.theirs), custom_call_target="tpu_custom_call" | custom-call | flops 100000000 | bytes 1000000 | tf_op jit(solution)/shard_map/pallas_call | solution.py:24
  (1 shorter events, 0.0 us)
Async XLA Ops:
  1.3 10.3 %collective-permute-start = (bf16[528,512]{1,0:T(8,128)(2,1)S(1)}, bf16[528,512]{1,0:T(8,128)(2,1)S(1)}, u32[]{:S(2)}, u32[]{:S(2)}) collective-permute-start(bf16[528,512]{1,0:T(8,128)(2,1)S(1)} %get-tuple-element.18.cells.refs_0_), channel_id=1, source_target_pairs={{0,1},{1,0},{2,3},{3,2},{4,5},{5,4},{6,7},{7,6},{8,9},{9,8},{10,11... | collective-permute-start | bytes 1622024 | tf_op jit(solution)/shard_map/ppermute | solution.py:42
  12.2 11.7 %copy-start = (bf16[64,512]{1,0:T(8,128)(2,1)S(1)}, bf16[64,512]{1,0:T(8,128)(2,1)}, u32[]{:S(2)}) copy-start(bf16[64,512]{1,0:T(8,128)(2,1)} %duals.1) | copy-start | bytes 196612
  24.0 11.4 %collective-permute-start.1 = (bf16[128,512]{1,0:T(8,128)(2,1)S(1)}, bf16[128,512]{1,0:T(8,128)(2,1)S(1)}, u32[]{:S(2)}, u32[]{:S(2)}) collective-permute-start(bf16[128,512]{1,0:T(8,128)(2,1)S(1)} %shard_map.85), channel_id=1, source_target_pairs={{0,8},{8,16},{16,24},{24,32},{32,40},{40,48},{48,56},{56,64},{64,7... | collective-permute-start | bytes 393224 | tf_op jit(solution)/shard_map/ppermute | solution.py:42
  25.9 11.0 %collective-permute-start.2 = (bf16[128,512]{1,0:T(8,128)(2,1)S(1)}, bf16[128,512]{1,0:T(8,128)(2,1)S(1)}, u32[]{:S(2)}, u32[]{:S(2)}) collective-permute-start(bf16[128,512]{1,0:T(8,128)(2,1)S(1)} %shard_map.85), channel_id=1, source_target_pairs={{0,504},{8,0},{16,8},{24,16},{32,24},{40,32},{48,40},{56,48},{64,5... | collective-permute-start | bytes 393224 | tf_op jit(solution)/shard_map/ppermute | solution.py:42
  37.0 21.8 %copy-start.1 = (bf16[4,128,512]{2,1,0:T(8,128)(2,1)S(1)}, bf16[4,128,512]{2,1,0:T(8,128)(2,1)}, u32[]{:S(2)}) copy-start(bf16[4,128,512]{2,1,0:T(8,128)(2,1)} %taper) | copy-start | bytes 1572868
  37.0 12.2 %collective-permute-start.3 = (bf16[384,512]{1,0:T(8,128)(2,1)S(1)}, bf16[384,512]{1,0:T(8,128)(2,1)S(1)}, u32[]{:S(2)}, u32[]{:S(2)}) collective-permute-start(bf16[384,512]{1,0:T(8,128)(2,1)S(1)} %pad_maximum_fusion.mid), channel_id=1, source_target_pairs={{0,24},{8,32},{16,40},{24,48},{32,56},{40,64},{48,72},{56,80},{64,... | collective-permute-start | bytes 1179656 | tf_op jit(solution)/shard_map/ppermute | solution.py:42
  39.0 11.1 %collective-permute-start.4 = (bf16[384,512]{1,0:T(8,128)(2,1)S(1)}, bf16[384,512]{1,0:T(8,128)(2,1)S(1)}, u32[]{:S(2)}, u32[]{:S(2)}) collective-permute-start(bf16[384,512]{1,0:T(8,128)(2,1)S(1)} %pad_maximum_fusion.mid), channel_id=1, source_target_pairs={{0,488},{8,496},{16,504},{24,0},{32,8},{40,16},{48,24},{56,32},{64... | collective-permute-start | bytes 1179656 | tf_op jit(solution)/shard_map/ppermute | solution.py:42
  50.4 19.2 %collective-permute-start.7 = (bf16[768,512]{1,0:T(8,128)(2,1)S(1)}, bf16[768,512]{1,0:T(8,128)(2,1)S(1)}, u32[]{:S(2)}, u32[]{:S(2)}) collective-permute-start(bf16[768,512]{1,0:T(8,128)(2,1)S(1)} %shard_map.86.rows), channel_id=1, source_target_pairs={{0,2},{2,4},{4,6},{6,0},{1,3},{3,5},{5,7},{7,1},{8,10},{10,12},{12... | collective-permute-start | bytes 2359304 | tf_op jit(solution)/shard_map/ppermute | solution.py:42
  52.6 18.4 %collective-permute-start.6 = (bf16[768,512]{1,0:T(8,128)(2,1)S(1)}, bf16[768,512]{1,0:T(8,128)(2,1)S(1)}, u32[]{:S(2)}, u32[]{:S(2)}) collective-permute-start(bf16[768,512]{1,0:T(8,128)(2,1)S(1)} %shard_map.86.rows), channel_id=1, source_target_pairs={{0,6},{2,0},{4,2},{6,4},{1,7},{3,1},{5,3},{7,5},{8,14},{10,8},{12,... | collective-permute-start | bytes 2359304 | tf_op jit(solution)/shard_map/ppermute | solution.py:42
  56.9 28.3 %collective-permute-start.5 = (bf16[768,512]{1,0:T(8,128)(2,1)S(1)}, bf16[768,512]{1,0:T(8,128)(2,1)S(1)}, u32[]{:S(2)}, u32[]{:S(2)}) collective-permute-start(bf16[768,512]{1,0:T(8,128)(2,1)S(1)} %shard_map.86.rows), channel_id=1, source_target_pairs={{0,4},{2,6},{4,0},{6,2},{1,5},{3,7},{5,1},{7,3},{8,12},{10,14},{12... | collective-permute-start | bytes 2359304 | tf_op jit(solution)/shard_map/ppermute | solution.py:42
  86.3 12.2 %collective-permute-start.8 = (f32[512,512]{1,0:T(8,128)S(1)}, f32[512,512]{1,0:T(8,128)S(1)}, u32[]{:S(2)}, u32[]{:S(2)}) collective-permute-start(f32[512,512]{1,0:T(8,128)S(1)} %shard_map.92), channel_id=1, source_target_pairs={{0,1},{1,0},{2,3},{3,2},{4,5},{5,4},{6,7},{7,6},{8,9},{9,8},{10,11... | collective-permute-start | bytes 3145736 | tf_op jit(solution)/shard_map/ppermute | solution.py:42

commit v5 on v3

--- a/solution.py
+++ b/solution.py
@@ -43,12 +43,12 @@
 
 
 def pack_body(*refs):
-    given, (meta, out, weights, foot), held = refs[:6], refs[6:10], refs[10:]
+    given, (meta, out, weights, foot, duals), held = refs[:7], refs[7:12], refs[12:]
     near, count, classes, raw, wide, done = held
     copies = []
-    for q, kept in enumerate((near, count, classes, raw, weights, foot)):
+    for q, kept in enumerate((near, count, classes, raw, weights, foot, duals)):
         copies.append(pltpu.make_async_copy(given[q], kept, done.at[q]))
-    for q in (3, 4, 0, 1, 2, 5):
+    for q in (3, 4, 0, 1, 2, 5, 6):
         copies[q].start()
     copies[3].wait()
     members = out.shape[0] - 16
@@ -58,7 +58,7 @@
     for l in range(levels):
         plane = wide[pl.ds(l, members, stride=levels), :].astype(BF16)
         out[:members, l * points : (l + 1) * points] = plane
-    for q in (4, 0, 1, 2, 5):
+    for q in (4, 0, 1, 2, 5, 6):
         copies[q].wait()
     high = weights[...].astype(BF16).astype(F32)
     low = weights[...] - high
@@ -76,9 +76,8 @@
 
 def columns(meta, weights, owned):
     parts = []
-    for r in range(RELS):
-        chip = lax.rem(meta[CHIP] + r, RELS)
-        block = weights(pl.ds(pl.multiple_of(chip * 2 * owned, 2 * owned), 2 * owned))
+    for chip in range(RELS):
+        block = weights(slice(chip * 2 * owned, (chip + 1) * 2 * owned))
         flipped = jnp.concatenate([block, block], axis=0).T
         parts.append(jnp.where(meta[CORE] == 0, flipped[:owned], flipped[owned:]))
     return jnp.concatenate(parts, axis=0)
@@ -86,8 +85,7 @@
 
 def rows_of(meta, foot, owned):
     parts = []
-    for r in range(RELS):
-        chip = lax.rem(meta[CHIP] + r, RELS)
+    for chip in range(RELS):
         start = pl.multiple_of(chip * 2 * owned + meta[CORE] * owned, owned)
         parts.append(foot[pl.ds(start, owned), :])
     return jnp.concatenate(parts, axis=0)
@@ -112,8 +110,9 @@
     project(rows_of(meta, foot, owned), column, cells, out, True)
 
 
-def other_body(meta, foot, cells, before, mine, pay1, pay2, pay3, acc):
-    owned, members = mine.shape
+def other_body(meta, foot, cells, before, duals, pay, acc):
+    members = acc.shape[1]
+    owned = acc.shape[0] // RELS
 
     def weights(at):
         terms = cells[members:, at].astype(F32)
@@ -121,43 +120,34 @@
 
     acc[...] = before[...]
     project(rows_of(meta, foot, owned), columns(meta, weights, owned), cells, acc, False)
-    slot = lax.broadcasted_iota(jnp.int32, mine.shape, 0) + meta[CORE] * owned
-    for r, pay in enumerate((mine, pay1, pay2, pay3)):
-        chip = lax.rem(meta[CHIP] + r, RELS)
+    slot = lax.broadcasted_iota(jnp.int32, (owned, members), 0) + meta[CORE] * owned
+    for chip in range(RELS):
         present = slot + chip * 2 * owned < meta[COUNT]
-        part = jnp.where(present, acc[r * owned : (r + 1) * owned], 0.0)
-        if r == 0:
-            mine[...] = part
-        else:
-            high = part.astype(BF16)
-            pay[:owned] = high
-            pay[owned:] = (part - high.astype(F32)).astype(BF16)
-
-
-def fold_body(mine, *refs):
-    out = refs[-1]
-    owned = out.shape[0]
-    total = mine[...]
-    for got in refs[:-1]:
-        total = total + (got[:owned].astype(F32) + got[owned:].astype(F32))
-    out[...] = total.astype(BF16)
-
-
-def flip_body(*refs):
-    out = refs[-1]
-    wide = refs[0].shape[0]
-    for r, rows in enumerate(refs[:-1]):
-        out[:, r * wide : (r + 1) * wide] = rows[...].T
-
-
-def choose(meta, k, sources, size, store):
+        part = jnp.where(present, acc[chip * owned : (chip + 1) * owned], 0.0)
+        high = part.astype(BF16)
+        pay[chip, :owned] = high
+        pay[chip, owned : 2 * owned] = (part - high.astype(F32)).astype(BF16)
+        pay[chip, 2 * owned :] = duals[...]
+
+
+def fold_body(got, out):
+    owned = got.shape[1] // 3
+    total = got[0, :owned].astype(F32) + got[0, owned : 2 * owned].astype(F32)
+    for chip in range(1, RELS):
+        total = total + (got[chip, :owned].astype(F32) + got[chip, owned : 2 * owned].astype(F32))
+    out[:owned] = total.astype(BF16)
+    for chip in range(RELS):
+        out[(chip + 1) * owned : (chip + 2) * owned] = got[chip, 2 * owned :]
+
+
+def choose(meta, k, sources, size, first, length, store):
     group = meta[k] // 3
-    start = pl.multiple_of(lax.rem(meta[k], 3) * size, size)
+    start = pl.multiple_of(lax.rem(meta[k], 3) * size + first, length)
     for g, source in enumerate(sources):
 
         @pl.when(group == g)
         def _(source=source):
-            store(source[pl.ds(start, size), :])
+            store(source[pl.ds(start, length), :])
 
 
 def pick_body(meta, low, mid, high, out):
@@ -167,7 +157,20 @@
         def store(value, k=k):
             out[k * size : (k + 1) * size] = value
 
-        choose(meta, k, (low, mid, high), size, store)
+        choose(meta, k, (low, mid, high), size, 0, size, store)
+
+
+def flip_body(meta, low, mid, high, out, held):
+    size = held.shape[0] // NEAR
+    for r in range(RELS):
+        chip = lax.rem(meta[CHIP] + r, RELS)
+        for k in range(NEAR):
+
+            def store(value, k=k):
+                held[k * size : (k + 1) * size] = value
+
+            choose(meta, k, (low, mid, high), RELS * size, chip * size, size, store)
+        out[:, r * held.shape[0] : (r + 1) * held.shape[0]] = held[...].T
 
 
 def taper_body(meta, taper, out, tall):
@@ -230,17 +233,17 @@
     members, levels, points = anomalies.shape
     owned = dual_rows.shape[0]
     tile = ("z", "y")
-    w_low, w_high = move(dual_rows, tile, 1), move(dual_rows, tile, -1)
     raw = anomalies.reshape(members * levels, points)
-    meta, own, weights, foot = kernel(
+    meta, own, weights, foot, duals = kernel(
         pack_body,
         [
             array((16,), jnp.int32),
             array((members + 16, levels * points), BF16),
             array(weighting.shape, F32),
             array(footprint.shape, BF16),
+            array(dual_rows.shape, BF16),
         ],
-        [near_tiles.T, obs_count, taper_class, raw, weighting, footprint],
+        [near_tiles.T, obs_count, taper_class, raw, weighting, footprint, dual_rows],
         1e8,
         scratch=[
             pltpu.SMEM(near_tiles.T.shape, jnp.int32),
@@ -248,10 +251,10 @@
             pltpu.SMEM(taper_class.shape, jnp.int32),
             pltpu.VMEM(raw.shape, BF16),
             pltpu.VMEM(raw.shape, F32),
-            pltpu.SemaphoreType.DMA((6,)),
+            pltpu.SemaphoreType.DMA((7,)),
         ],
-        given=[pltpu.HBM] * 6,
-        spaces=[pltpu.SMEM, pltpu.VMEM, pltpu.VMEM, pltpu.VMEM],
+        given=[pltpu.HBM] * 7,
+        spaces=[pltpu.SMEM] + [pltpu.VMEM] * 4,
     )
     other = move(own, "c", 1)
 
@@ -260,26 +263,28 @@
     (begun,) = kernel(
         own_body, [array((rows, members), F32)], [meta, foot, own, weights], work, scalars=1
     )
-    pay = array((2 * owned, members), BF16)
-    mine, pay1, pay2, pay3 = kernel(
+    (pay,) = kernel(
         other_body,
-        [array((owned, members), F32), pay, pay, pay],
-        [meta, foot, other, begun],
+        [array((RELS, 3 * owned, members), BF16)],
+        [meta, foot, other, begun, duals],
         work,
         scalars=1,
         scratch=[pltpu.VMEM((rows, members), F32)],
     )
-    got1, got3, got2 = move(pay1, "x", 1), move(pay3, "x", -1), move(pay2, "x", 2)
-    w_mid = jnp.concatenate([w_low, dual_rows, w_high], axis=0)
-    w_far_low, w_far_high = move(w_mid, tile, 3), move(w_mid, tile, -3)
-    (rows_y,) = kernel(fold_body, [array((owned, members), BF16)], [mine, got1, got3, got2], 1e8)
-    y_low, y_high = move(rows_y, tile, 1), move(rows_y, tile, -1)
-    chosen = [array((NEAR * owned, members), BF16)]
-    (w0,) = kernel(pick_body, chosen, [meta, w_far_low, w_mid, w_far_high], 1e8, scalars=1)
-    w3, w1, w2 = move(w0, "x", 1), move(w0, "x", -1), move(w0, "x", 2)
-    y_mid = jnp.concatenate([y_low, rows_y, y_high], axis=0)
-    y_far_low, y_far_high = move(y_mid, tile, 3), move(y_mid, tile, -3)
-    (y0,) = kernel(pick_body, chosen, [meta, y_far_low, y_mid, y_far_high], 1e8, scalars=1)
+    got = lax.all_to_all(pay, "x", 0, 0, tiled=True)
+    (here,) = kernel(fold_body, [array((owned + rows, members), BF16)], [got], 1e8)
+    low, high = move(here, tile, 1), move(here, tile, -1)
+    y_mid = jnp.concatenate([a[:owned] for a in (low, here, high)], axis=0)
+    y_low, y_high = move(y_mid, tile, 3), move(y_mid, tile, -3)
+    w_mid = jnp.concatenate([a[owned:] for a in (low, here, high)], axis=0)
+    w_low, w_high = move(w_mid, tile, 3), move(w_mid, tile, -3)
+    (y0,) = kernel(
+        pick_body,
+        [array((NEAR * owned, members), BF16)],
+        [meta, y_low, y_mid, y_high],
+        1e8,
+        scalars=1,
+    )
     y3, y1, y2 = move(y0, "x", 1), move(y0, "x", -1), move(y0, "x", 2)
 
     taper_late, _ = lax.optimization_barrier((taper_blocks, y0))
@@ -302,12 +307,19 @@
             4 * NEAR * owned * members * width,
             aliases={} if tapered is None else {4: 0},
         )
-    (duals,) = kernel(flip_body, [array((members, NEAR * rows), BF16)], [w0, w1, w2, w3], 1e9)
+    (flipped,) = kernel(
+        flip_body,
+        [array((members, NEAR * rows), BF16)],
+        [meta, w_low, w_mid, w_high],
+        1e9,
+        scalars=1,
+        scratch=[pltpu.VMEM((NEAR * owned, members), BF16)],
+    )
     sums = [
         kernel(
             functools.partial(gain_body, h),
             [array((members, width), F32)],
-            [duals, tapered],
+            [flipped, tapered],
             2 * NEAR * rows * members * width,
         )[0]
         for h in (0, 1)

time: 105 us -> 103 us (0.981)
  starting transfers between devices: 78.7 us -> 51.3 us
  blocking collectives: 0 us -> 14.4 us
  waiting for transfers between devices: 15.4 us -> 26.4 us
    ppermute x19 -> x11, starting transfers between devices: 78.7 us -> 51.3 us  [move(): lax.ppermute(value, axis, [(i, (i + steps) % count) for i in range(count)])]
    all_to_all x0 -> x1, blocking collectives: none -> 14.4 us  [shards(): got = lax.all_to_all(pay, 'x', 0, 0, tiled=True)]
    ppermute x19 -> x11, waiting for transfers between devices: 15.4 us -> 26.4 us  [move(): lax.ppermute(value, axis, [(i, (i + steps) % count) for i in range(count)])]
    pallas_call x15 -> x14, Pallas kernels: 8.71 us -> 9.4 us  [kernel(): pl.pallas_call(body, out_shape=[o if m is None else m(o.shape, o.dtype) f...]
  transfers between devices with their start and end apart: 19 -> 11, of which waited for: 9 -> 9; matrix products, arithmetic and copies ran while one was open for 1% -> 0% of each run, Pallas kernels for 5% -> 4%
where the time goes in v5:
time: 103 us; the launch traced here: 102 us
  starting transfers between devices  51.3 us (50%)
  waiting for transfers between devices  26.4 us (26%)
  blocking collectives  14.4 us (14%)
  Pallas kernels  9.4 us (9%)
    ppermute x11, starting transfers between devices, move(): lax.ppermute(value, axis, [(i, (i + steps) % count) for i in range(count)])  51.3 us
    ppermute x11, waiting for transfers between devices, move(): lax.ppermute(value, axis, [(i, (i + steps) % count) for i in range(count)])  26.4 us
    all_to_all x1, blocking collectives, shards(): got = lax.all_to_all(pay, 'x', 0, 0, tiled=True)  14.4 us
    pallas_call x14, Pallas kernels, kernel(): pl.pallas_call(body, out_shape=[o if m is None else m(o.shape, o.dtype) f...  9.4 us
  transfers between devices with their start and end apart: 11, of which 9 were waited for; matrix products, arithmetic and copies ran while one was open for 0% of the time, Pallas kernels for 4%

profile of v5, /device:TPU:1, one launch (start us, length us, event | category | flops | bytes accessed | tf_op | source)
XLA Modules:
  0.0 101.9 jit_solution(17313203930608806019)
XLA Ops:
  0.0 1.3 %shard_map.82 = (s32[16]{0:T(128)S(4)}, bf16[528,512]{1,0:T(8,128)(2,1)S(1)}, f32[4,512]{1,0:T(4,128)S(1)}, bf16[512,128]{1,0:T(8,128)(2,1)S(1)}, bf16[64,512]{1,0:T(8,128)(2,1)S(1)}) custom-call(s32[6,64]{1,0:T(8,128)} %bitcast.4, s32[64]{0:T(128)} %refs_1_.1, s32[1,6]{1,0:T(1,128)} %refs_2_.1, bf16[2048,128]{1,0:T(8,128)(2,1)} %bitcast.3, ...), custom_call_target="tpu_custom_call" | custom-call | flops 100000000 | bytes 1000000 | tf_op jit(solution)/shard_map/pallas_call | solution.py:24
  1.3 8.7 %collective-permute-start = (bf16[528,512]{1,0:T(8,128)(2,1)S(1)}, bf16[528,512]{1,0:T(8,128)(2,1)S(1)}, u32[]{:S(2)}, u32[]{:S(2)}) collective-permute-start(bf16[528,512]{1,0:T(8,128)(2,1)S(1)} %get-tuple-element.13.cells.own), channel_id=1, source_target_pairs={{0,1},{1,0},{2,3},{3,2},{4,5},{5,4},{6,7},{7,6},{8,9},{9,8},{10,11... | collective-permute-start | bytes 1622024 | tf_op jit(solution)/shard_map/ppermute | solution.py:42
  10.1 0.5 shard_map.83.before
  10.6 1.0 %collective-permute-done.cells.other = bf16[528,512]{1,0:T(8,128)(2,1)S(1)} collective-permute-done((bf16[528,512]{1,0:T(8,128)(2,1)S(1)}, bf16[528,512]{1,0:T(8,128)(2,1)S(1)}, u32[]{:S(2)}, u32[]{:S(2)}) %collective-permute-start) | collective-permute-done | bytes 540704 | tf_op jit(solution)/shard_map/ppermute | solution.py:42
  11.6 0.6 shard_map.84
  12.2 14.4 %all_to_all.5.got = bf16[4,192,512]{2,1,0:T(8,128)(2,1)S(1)} all-to-all(bf16[4,192,512]{2,1,0:T(8,128)(2,1)S(1)} %shard_map.84), channel_id=1, replica_groups=mesh['z'=16,'y'=4,'x'=4,'c'=2] {'x'}, dimensions={0} | all-to-all | bytes 1572864 | tf_op jit(solution)/shard_map/all_to_all | solution.py:274
  26.6 0.1 shard_map.85
  26.7 1.9 %collective-permute-start.1 = (bf16[320,512]{1,0:T(8,128)(2,1)S(1)}, bf16[320,512]{1,0:T(8,128)(2,1)S(1)}, u32[]{:S(2)}, u32[]{:S(2)}) collective-permute-start(bf16[320,512]{1,0:T(8,128)(2,1)S(1)} %shard_map.85), channel_id=1, source_target_pairs={{0,8},{8,16},{16,24},{24,32},{32,40},{40,48},{48,56},{56,64},{64,7... | collective-permute-start | bytes 983048 | tf_op jit(solution)/shard_map/ppermute | solution.py:42
  28.6 9.0 %collective-permute-start.2 = (bf16[320,512]{1,0:T(8,128)(2,1)S(1)}, bf16[320,512]{1,0:T(8,128)(2,1)S(1)}, u32[]{:S(2)}, u32[]{:S(2)}) collective-permute-start(bf16[320,512]{1,0:T(8,128)(2,1)S(1)} %shard_map.85), channel_id=1, source_target_pairs={{0,504},{8,0},{16,8},{24,16},{32,24},{40,32},{48,40},{56,48},{64,5... | collective-permute-start | bytes 983048 | tf_op jit(solution)/shard_map/ppermute | solution.py:42
  37.7 4.3 %collective-permute-done.1 = bf16[320,512]{1,0:T(8,128)(2,1)S(1)} collective-permute-done((bf16[320,512]{1,0:T(8,128)(2,1)S(1)}, bf16[320,512]{1,0:T(8,128)(2,1)S(1)}, u32[]{:S(2)}, u32[]{:S(2)}) %collective-permute-start.1) | collective-permute-done | bytes 327712 | tf_op jit(solution)/shard_map/ppermute | solution.py:42
  42.0 0.9 collective-permute-done.2
  42.9 0.0 copy-start
  42.9 0.1 pad_maximum_fusion.mid
  43.0 2.1 %collective-permute-start.3 = (bf16[768,512]{1,0:T(8,128)(2,1)S(1)}, bf16[768,512]{1,0:T(8,128)(2,1)S(1)}, u32[]{:S(2)}, u32[]{:S(2)}) collective-permute-start(bf16[768,512]{1,0:T(8,128)(2,1)S(1)} %pad_maximum_fusion.mid), channel_id=1, source_target_pairs={{0,24},{8,32},{16,40},{24,48},{32,56},{40,64},{48,72},{56,80},{64,... | collective-permute-start | bytes 2359304 | tf_op jit(solution)/shard_map/ppermute | solution.py:42
  45.1 5.5 %collective-permute-start.4 = (bf16[768,512]{1,0:T(8,128)(2,1)S(1)}, bf16[768,512]{1,0:T(8,128)(2,1)S(1)}, u32[]{:S(2)}, u32[]{:S(2)}) collective-permute-start(bf16[768,512]{1,0:T(8,128)(2,1)S(1)} %pad_maximum_fusion.mid), channel_id=1, source_target_pairs={{0,488},{8,496},{16,504},{24,0},{32,8},{40,16},{48,24},{56,32},{64... | collective-permute-start | bytes 2359304 | tf_op jit(solution)/shard_map/ppermute | solution.py:42
  50.6 1.9 %collective-permute-start.5 = (bf16[192,512]{1,0:T(8,128)(2,1)S(1)}, bf16[192,512]{1,0:T(8,128)(2,1)S(1)}, u32[]{:S(2)}, u32[]{:S(2)}) collective-permute-start(bf16[192,512]{1,0:T(8,128)(2,1)S(1)} %pad_maximum_fusion.1.mid), channel_id=1, source_target_pairs={{0,24},{8,32},{16,40},{24,48},{32,56},{40,64},{48,72},{56,80},{64,... | collective-permute-start | bytes 589832 | tf_op jit(solution)/shard_map/ppermute | solution.py:42
  52.5 5.5 %collective-permute-start.6 = (bf16[192,512]{1,0:T(8,128)(2,1)S(1)}, bf16[192,512]{1,0:T(8,128)(2,1)S(1)}, u32[]{:S(2)}, u32[]{:S(2)}) collective-permute-start(bf16[192,512]{1,0:T(8,128)(2,1)S(1)} %pad_maximum_fusion.1.mid), channel_id=1, source_target_pairs={{0,488},{8,496},{16,504},{24,0},{32,8},{40,16},{48,24},{56,32},{64... | collective-permute-start | bytes 589832 | tf_op jit(solution)/shard_map/ppermute | solution.py:42
  58.0 9.8 %collective-permute-done.5.low = bf16[192,512]{1,0:T(8,128)(2,1)S(1)} collective-permute-done((bf16[192,512]{1,0:T(8,128)(2,1)S(1)}, bf16[192,512]{1,0:T(8,128)(2,1)S(1)}, u32[]{:S(2)}, u32[]{:S(2)}) %collective-permute-start.5) | collective-permute-done | bytes 196640 | tf_op jit(solution)/shard_map/ppermute | solution.py:42
  67.8 1.0 %collective-permute-done.6.high = bf16[192,512]{1,0:T(8,128)(2,1)S(1)} collective-permute-done((bf16[192,512]{1,0:T(8,128)(2,1)S(1)}, bf16[192,512]{1,0:T(8,128)(2,1)S(1)}, u32[]{:S(2)}, u32[]{:S(2)}) %collective-permute-start.6) | collective-permute-done | bytes 196640 | tf_op jit(solution)/shard_map/ppermute | solution.py:42
  68.8 0.1 shard_map.87.rows
  69.0 2.2 %collective-permute-start.9 = (bf16[384,512]{1,0:T(8,128)(2,1)S(1)}, bf16[384,512]{1,0:T(8,128)(2,1)S(1)}, u32[]{:S(2)}, u32[]{:S(2)}) collective-permute-start(bf16[384,512]{1,0:T(8,128)(2,1)S(1)} %shard_map.87.rows), channel_id=1, source_target_pairs={{0,2},{2,4},{4,6},{6,0},{1,3},{3,5},{5,7},{7,1},{8,10},{10,12},{12... | collective-permute-start | bytes 1179656 | tf_op jit(solution)/shard_map/ppermute | solution.py:42
  71.2 4.3 %collective-permute-start.8 = (bf16[384,512]{1,0:T(8,128)(2,1)S(1)}, bf16[384,512]{1,0:T(8,128)(2,1)S(1)}, u32[]{:S(2)}, u32[]{:S(2)}) collective-permute-start(bf16[384,512]{1,0:T(8,128)(2,1)S(1)} %shard_map.87.rows), channel_id=1, source_target_pairs={{0,6},{2,0},{4,2},{6,4},{1,7},{3,1},{5,3},{7,5},{8,14},{10,8},{12,... | collective-permute-start | bytes 1179656 | tf_op jit(solution)/shard_map/ppermute | solution.py:42
  75.5 1.9 %collective-permute-start.7 = (bf16[384,512]{1,0:T(8,128)(2,1)S(1)}, bf16[384,512]{1,0:T(8,128)(2,1)S(1)}, u32[]{:S(2)}, u32[]{:S(2)}) collective-permute-start(bf16[384,512]{1,0:T(8,128)(2,1)S(1)} %shard_map.87.rows), channel_id=1, source_target_pairs={{0,4},{2,6},{4,0},{6,2},{1,5},{3,7},{5,1},{7,3},{8,12},{10,14},{12... | collective-permute-start | bytes 1179656 | tf_op jit(solution)/shard_map/ppermute | solution.py:42
  77.4 0.0 copy-done
  77.4 0.3 shard_map.88.scaled
  77.7 0.6 shard_map.89.refs_0_
  78.3 0.8 collective-permute-done.9.rows
  79.1 0.6 shard_map.90.refs_0_
  79.7 2.6 %collective-permute-done.8.rows = bf16[384,512]{1,0:T(8,128)(2,1)S(1)} collective-permute-done((bf16[384,512]{1,0:T(8,128)(2,1)S(1)}, bf16[384,512]{1,0:T(8,128)(2,1)S(1)}, u32[]{:S(2)}, u32[]{:S(2)}) %collective-permute-start.8) | collective-permute-done | bytes 393248 | tf_op jit(solution)/shard_map/ppermute | solution.py:42
  82.3 0.6 shard_map.91.refs_0_
  82.9 4.6 %collective-permute-done.7.rows = bf16[384,512]{1,0:T(8,128)(2,1)S(1)} collective-permute-done((bf16[384,512]{1,0:T(8,128)(2,1)S(1)}, bf16[384,512]{1,0:T(8,128)(2,1)S(1)}, u32[]{:S(2)}, u32[]{:S(2)}) %collective-permute-start.7) | collective-permute-done | bytes 393248 | tf_op jit(solution)/shard_map/ppermute | solution.py:42
  87.4 0.6 shard_map.92.tapered
  88.0 0.0 collective-permute-done.3.low
  88.0 0.0 collective-permute-done.4.high
  88.0 1.3 %shard_map.86.duals = bf16[512,1536]{1,0:T(8,128)(2,1)S(1)} custom-call(s32[16]{0:T(128)S(4)} %get-tuple-element.11.meta, bf16[768,512]{1,0:T(8,128)(2,1)S(1)} %collective-permute-done.3.low, bf16[768,512]{1,0:T(8,128)(2,1)S(1)} %pad_maximum_fusion.mid, bf16[768,512]{1,0:T(8,128)(2,1)S(1)} %collective-permute-done.4.high), custom_call_target="tpu_custom_call" | custom-call | flops 1000000000 | bytes 1000000 | tf_op jit(solution)/shard_map/pallas_call | solution.py:24
  89.4 1.0 shard_map.94
  90.3 8.3 %collective-permute-start.10 = (f32[512,512]{1,0:T(8,128)S(1)}, f32[512,512]{1,0:T(8,128)S(1)}, u32[]{:S(2)}, u32[]{:S(2)}) collective-permute-start(f32[512,512]{1,0:T(8,128)S(1)} %shard_map.94), channel_id=1, source_target_pairs={{0,1},{1,0},{2,3},{3,2},{4,5},{5,4},{6,7},{7,6},{8,9},{9,8},{10,11... | collective-permute-start | bytes 3145736 | tf_op jit(solution)/shard_map/ppermute | solution.py:42
  98.6 1.0 shard_map.93.mine
  99.6 1.3 %collective-permute-done.10.theirs = f32[512,512]{1,0:T(8,128)S(1)} collective-permute-done((f32[512,512]{1,0:T(8,128)S(1)}, f32[512,512]{1,0:T(8,128)S(1)}, u32[]{:S(2)}, u32[]{:S(2)}) %collective-permute-start.10) | collective-permute-done | bytes 1048608 | tf_op jit(solution)/shard_map/ppermute | solution.py:42
  100.9 1.0 %shard_map.95 = f32[2048,128]{1,0:T(8,128)} custom-call(f32[512,512]{1,0:T(8,128)S(1)} %shard_map.93.mine, f32[512,512]{1,0:T(8,128)S(1)} %collective-permute-done.10.theirs), custom_call_target="tpu_custom_call" | custom-call | flops 100000000 | bytes 1000000 | tf_op jit(solution)/shard_map/pallas_call | solution.py:24
  (7 shorter events, 0.1 us)
Async XLA Ops:
  1.3 10.3 %collective-permute-start = (bf16[528,512]{1,0:T(8,128)(2,1)S(1)}, bf16[528,512]{1,0:T(8,128)(2,1)S(1)}, u32[]{:S(2)}, u32[]{:S(2)}) collective-permute-start(bf16[528,512]{1,0:T(8,128)(2,1)S(1)} %get-tuple-element.13.cells.own), channel_id=1, source_target_pairs={{0,1},{1,0},{2,3},{3,2},{4,5},{5,4},{6,7},{7,6},{8,9},{9,8},{10,11... | collective-permute-start | bytes 1622024 | tf_op jit(solution)/shard_map/ppermute | solution.py:42
  26.7 15.3 %collective-permute-start.1 = (bf16[320,512]{1,0:T(8,128)(2,1)S(1)}, bf16[320,512]{1,0:T(8,128)(2,1)S(1)}, u32[]{:S(2)}, u32[]{:S(2)}) collective-permute-start(bf16[320,512]{1,0:T(8,128)(2,1)S(1)} %shard_map.85), channel_id=1, source_target_pairs={{0,8},{8,16},{16,24},{24,32},{32,40},{40,48},{48,56},{56,64},{64,7... | collective-permute-start | bytes 983048 | tf_op jit(solution)/shard_map/ppermute | solution.py:42
  28.6 14.3 %collective-permute-start.2 = (bf16[320,512]{1,0:T(8,128)(2,1)S(1)}, bf16[320,512]{1,0:T(8,128)(2,1)S(1)}, u32[]{:S(2)}, u32[]{:S(2)}) collective-permute-start(bf16[320,512]{1,0:T(8,128)(2,1)S(1)} %shard_map.85), channel_id=1, source_target_pairs={{0,504},{8,0},{16,8},{24,16},{32,24},{40,32},{48,40},{56,48},{64,5... | collective-permute-start | bytes 983048 | tf_op jit(solution)/shard_map/ppermute | solution.py:42
  42.9 34.5 %copy-start = (bf16[4,128,512]{2,1,0:T(8,128)(2,1)S(1)}, bf16[4,128,512]{2,1,0:T(8,128)(2,1)}, u32[]{:S(2)}) copy-start(bf16[4,128,512]{2,1,0:T(8,128)(2,1)} %taper) | copy-start | bytes 1572868
  43.0 45.0 %collective-permute-start.3 = (bf16[768,512]{1,0:T(8,128)(2,1)S(1)}, bf16[768,512]{1,0:T(8,128)(2,1)S(1)}, u32[]{:S(2)}, u32[]{:S(2)}) collective-permute-start(bf16[768,512]{1,0:T(8,128)(2,1)S(1)} %pad_maximum_fusion.mid), channel_id=1, source_target_pairs={{0,24},{8,32},{16,40},{24,48},{32,56},{40,64},{48,72},{56,80},{64,... | collective-permute-start | bytes 2359304 | tf_op jit(solution)/shard_map/ppermute | solution.py:42
  45.1 43.0 %collective-permute-start.4 = (bf16[768,512]{1,0:T(8,128)(2,1)S(1)}, bf16[768,512]{1,0:T(8,128)(2,1)S(1)}, u32[]{:S(2)}, u32[]{:S(2)}) collective-permute-start(bf16[768,512]{1,0:T(8,128)(2,1)S(1)} %pad_maximum_fusion.mid), channel_id=1, source_target_pairs={{0,488},{8,496},{16,504},{24,0},{32,8},{40,16},{48,24},{56,32},{64... | collective-permute-start | bytes 2359304 | tf_op jit(solution)/shard_map/ppermute | solution.py:42
  50.6 17.2 %collective-permute-start.5 = (bf16[192,512]{1,0:T(8,128)(2,1)S(1)}, bf16[192,512]{1,0:T(8,128)(2,1)S(1)}, u32[]{:S(2)}, u32[]{:S(2)}) collective-permute-start(bf16[192,512]{1,0:T(8,128)(2,1)S(1)} %pad_maximum_fusion.1.mid), channel_id=1, source_target_pairs={{0,24},{8,32},{16,40},{24,48},{32,56},{40,64},{48,72},{56,80},{64,... | collective-permute-start | bytes 589832 | tf_op jit(solution)/shard_map/ppermute | solution.py:42
  52.5 16.3 %collective-permute-start.6 = (bf16[192,512]{1,0:T(8,128)(2,1)S(1)}, bf16[192,512]{1,0:T(8,128)(2,1)S(1)}, u32[]{:S(2)}, u32[]{:S(2)}) collective-permute-start(bf16[192,512]{1,0:T(8,128)(2,1)S(1)} %pad_maximum_fusion.1.mid), channel_id=1, source_target_pairs={{0,488},{8,496},{16,504},{24,0},{32,8},{40,16},{48,24},{56,32},{64... | collective-permute-start | bytes 589832 | tf_op jit(solution)/shard_map/ppermute | solution.py:42
  69.0 10.1 %collective-permute-start.9 = (bf16[384,512]{1,0:T(8,128)(2,1)S(1)}, bf16[384,512]{1,0:T(8,128)(2,1)S(1)}, u32[]{:S(2)}, u32[]{:S(2)}) collective-permute-start(bf16[384,512]{1,0:T(8,128)(2,1)S(1)} %shard_map.87.rows), channel_id=1, source_target_pairs={{0,2},{2,4},{4,6},{6,0},{1,3},{3,5},{5,7},{7,1},{8,10},{10,12},{12... | collective-permute-start | bytes 1179656 | tf_op jit(solution)/shard_map/ppermute | solution.py:42
  71.2 11.1 %collective-permute-start.8 = (bf16[384,512]{1,0:T(8,128)(2,1)S(1)}, bf16[384,512]{1,0:T(8,128)(2,1)S(1)}, u32[]{:S(2)}, u32[]{:S(2)}) collective-permute-start(bf16[384,512]{1,0:T(8,128)(2,1)S(1)} %shard_map.87.rows), channel_id=1, source_target_pairs={{0,6},{2,0},{4,2},{6,4},{1,7},{3,1},{5,3},{7,5},{8,14},{10,8},{12,... | collective-permute-start | bytes 1179656 | tf_op jit(solution)/shard_map/ppermute | solution.py:42
  75.5 12.0 %collective-permute-start.7 = (bf16[384,512]{1,0:T(8,128)(2,1)S(1)}, bf16[384,512]{1,0:T(8,128)(2,1)S(1)}, u32[]{:S(2)}, u32[]{:S(2)}) collective-permute-start(bf16[384,512]{1,0:T(8,128)(2,1)S(1)} %shard_map.87.rows), channel_id=1, source_target_pairs={{0,4},{2,6},{4,0},{6,2},{1,5},{3,7},{5,1},{7,3},{8,12},{10,14},{12... | collective-permute-start | bytes 1179656 | tf_op jit(solution)/shard_map/ppermute | solution.py:42
  90.3 10.6 %collective-permute-start.10 = (f32[512,512]{1,0:T(8,128)S(1)}, f32[512,512]{1,0:T(8,128)S(1)}, u32[]{:S(2)}, u32[]{:S(2)}) collective-permute-start(f32[512,512]{1,0:T(8,128)S(1)} %shard_map.94), channel_id=1, source_target_pairs={{0,1},{1,0},{2,3},{3,2},{4,5},{5,4},{6,7},{7,6},{8,9},{9,8},{10,11... | collective-permute-start | bytes 3145736 | tf_op jit(solution)/shard_map/ppermute | solution.py:42

commit v6 on v5

--- a/solution.py
+++ b/solution.py
@@ -204,9 +204,9 @@
     half = out.shape[1]
     step = 256
     for at in range(0, half, step):
-        out[:, at : at + step] = jnp.dot(
-            duals[...], tapered[:, h * half + at : h * half + at + step], preferred_element_type=F32
-        )
+        span = slice(h * half + at, h * half + at + step)
+        gained = jnp.dot(duals[...], tapered[:, span], preferred_element_type=F32)
+        out[:, at : at + step] = gained.astype(out.dtype)
 
 
 def finish_body(mine, theirs, out, held, done):
@@ -219,7 +219,7 @@
     for q in range(parts):
         for l in range(levels):
             at = (slice(q * size, (q + 1) * size), slice(l * points, (l + 1) * points))
-            held[pl.ds(q * size * levels + l, size, stride=levels), :] = mine[at] + theirs[at]
+            held[pl.ds(q * size * levels + l, size, stride=levels), :] = mine[at] + theirs[at].astype(F32)
         span = pl.ds(q * size * levels, size * levels)
         copies.append(pltpu.make_async_copy(held.at[span], out.at[span], done.at[q]))
         copies[-1].start()
@@ -297,8 +297,17 @@
         scratch=[pltpu.VMEM((taper_blocks.shape[0], taper_blocks.shape[2], points), F32)],
     )
     width = levels * points
+    (flipped,) = kernel(
+        flip_body,
+        [array((members, NEAR * rows), BF16)],
+        [meta, w_low, w_mid, w_high],
+        1e9,
+        scalars=1,
+        scratch=[pltpu.VMEM((NEAR * owned, members), BF16)],
+    )
+    y3, y1, y2 = (lax.optimization_barrier((y, flipped))[0] for y in (y3, y1, y2))
     tapered = None
-    for rel, got in ((0, y0), (3, y3), (1, y1), (2, y2)):
+    for rel, got in ((0, y0), (2, y2), (3, y3), (1, y1)):
         inputs = [got, own, other, scaled] + ([] if tapered is None else [tapered])
         (tapered,) = kernel(
             functools.partial(covary_body, rel),
@@ -307,18 +316,10 @@
             4 * NEAR * owned * members * width,
             aliases={} if tapered is None else {4: 0},
         )
-    (flipped,) = kernel(
-        flip_body,
-        [array((members, NEAR * rows), BF16)],
-        [meta, w_low, w_mid, w_high],
-        1e9,
-        scalars=1,
-        scratch=[pltpu.VMEM((NEAR * owned, members), BF16)],
-    )
     sums = [
         kernel(
             functools.partial(gain_body, h),
-            [array((members, width), F32)],
+            [array((members, width), BF16 if h else F32)],
             [flipped, tapered],
             2 * NEAR * rows * members * width,
         )[0]

time: 103 us -> 100 us (0.971)
  starting transfers between devices: 51.3 us -> 47.2 us
  waiting for transfers between devices: 26.4 us -> 28.1 us
    ppermute x11, starting transfers between devices: 51.3 us -> 47.2 us  [move(): lax.ppermute(value, axis, [(i, (i + steps) % count) for i in range(count)])]
    ppermute x11, waiting for transfers between devices: 26.4 us -> 28.1 us  [move(): lax.ppermute(value, axis, [(i, (i + steps) % count) for i in range(count)])]
  transfers between devices with their start and end apart: 11 -> 11, of which waited for: 9 -> 7; matrix products, arithmetic and copies ran while one was open for 0% -> 0% of each run, Pallas kernels for 4% -> 4%
where the time goes in v6:
time: 100 us; the launch traced here: 99.5 us
  starting transfers between devices  47.2 us (47%)
  waiting for transfers between devices  28.1 us (28%)
  blocking collectives  14.4 us (14%)
  Pallas kernels  9.4 us (9%)
    ppermute x11, starting transfers between devices, move(): lax.ppermute(value, axis, [(i, (i + steps) % count) for i in range(count)])  47.2 us
    ppermute x11, waiting for transfers between devices, move(): lax.ppermute(value, axis, [(i, (i + steps) % count) for i in range(count)])  28.1 us
    all_to_all x1, blocking collectives, shards(): got = lax.all_to_all(pay, 'x', 0, 0, tiled=True)  14.4 us
    pallas_call x14, Pallas kernels, kernel(): pl.pallas_call(body, out_shape=[o if m is None else m(o.shape, o.dtype) f...  9.4 us
  transfers between devices with their start and end apart: 11, of which 7 were waited for; matrix products, arithmetic and copies ran while one was open for 0% of the time, Pallas kernels for 4%

profile of v6, /device:TPU:1, one launch (start us, length us, event | category | flops | bytes accessed | tf_op | source)
XLA Modules:
  0.0 99.5 jit_solution(12060133514122015256)
XLA Ops:
  0.0 1.3 %shard_map.82 = (s32[16]{0:T(128)S(4)}, bf16[528,512]{1,0:T(8,128)(2,1)S(1)}, f32[4,512]{1,0:T(4,128)S(1)}, bf16[512,128]{1,0:T(8,128)(2,1)S(1)}, bf16[64,512]{1,0:T(8,128)(2,1)S(1)}) custom-call(s32[6,64]{1,0:T(8,128)} %bitcast.4, s32[64]{0:T(128)} %refs_1_.1, s32[1,6]{1,0:T(1,128)} %refs_2_.1, bf16[2048,128]{1,0:T(8,128)(2,1)} %bitcast.3, ...), custom_call_target="tpu_custom_call" | custom-call | flops 100000000 | bytes 1000000 | tf_op jit(solution)/shard_map/pallas_call | solution.py:24
  1.3 8.7 %collective-permute-start = (bf16[528,512]{1,0:T(8,128)(2,1)S(1)}, bf16[528,512]{1,0:T(8,128)(2,1)S(1)}, u32[]{:S(2)}, u32[]{:S(2)}) collective-permute-start(bf16[528,512]{1,0:T(8,128)(2,1)S(1)} %get-tuple-element.16.cells.own), channel_id=1, source_target_pairs={{0,1},{1,0},{2,3},{3,2},{4,5},{5,4},{6,7},{7,6},{8,9},{9,8},{10,11... | collective-permute-start | bytes 1622024 | tf_op jit(solution)/shard_map/ppermute | solution.py:42
  10.1 0.5 shard_map.83.before
  10.6 1.0 %collective-permute-done.cells.other = bf16[528,512]{1,0:T(8,128)(2,1)S(1)} collective-permute-done((bf16[528,512]{1,0:T(8,128)(2,1)S(1)}, bf16[528,512]{1,0:T(8,128)(2,1)S(1)}, u32[]{:S(2)}, u32[]{:S(2)}) %collective-permute-start) | collective-permute-done | bytes 540704 | tf_op jit(solution)/shard_map/ppermute | solution.py:42
  11.6 0.6 shard_map.84
  12.2 14.4 %all_to_all.5.got = bf16[4,192,512]{2,1,0:T(8,128)(2,1)S(1)} all-to-all(bf16[4,192,512]{2,1,0:T(8,128)(2,1)S(1)} %shard_map.84), channel_id=1, replica_groups=mesh['z'=16,'y'=4,'x'=4,'c'=2] {'x'}, dimensions={0} | all-to-all | bytes 1572864 | tf_op jit(solution)/shard_map/all_to_all | solution.py:274
  26.6 0.1 shard_map.85
  26.7 1.9 %collective-permute-start.1 = (bf16[320,512]{1,0:T(8,128)(2,1)S(1)}, bf16[320,512]{1,0:T(8,128)(2,1)S(1)}, u32[]{:S(2)}, u32[]{:S(2)}) collective-permute-start(bf16[320,512]{1,0:T(8,128)(2,1)S(1)} %shard_map.85), channel_id=1, source_target_pairs={{0,8},{8,16},{16,24},{24,32},{32,40},{40,48},{48,56},{56,64},{64,7... | collective-permute-start | bytes 983048 | tf_op jit(solution)/shard_map/ppermute | solution.py:42
  28.6 9.0 %collective-permute-start.2 = (bf16[320,512]{1,0:T(8,128)(2,1)S(1)}, bf16[320,512]{1,0:T(8,128)(2,1)S(1)}, u32[]{:S(2)}, u32[]{:S(2)}) collective-permute-start(bf16[320,512]{1,0:T(8,128)(2,1)S(1)} %shard_map.85), channel_id=1, source_target_pairs={{0,504},{8,0},{16,8},{24,16},{32,24},{40,32},{48,40},{56,48},{64,5... | collective-permute-start | bytes 983048 | tf_op jit(solution)/shard_map/ppermute | solution.py:42
  37.7 4.3 %collective-permute-done.1 = bf16[320,512]{1,0:T(8,128)(2,1)S(1)} collective-permute-done((bf16[320,512]{1,0:T(8,128)(2,1)S(1)}, bf16[320,512]{1,0:T(8,128)(2,1)S(1)}, u32[]{:S(2)}, u32[]{:S(2)}) %collective-permute-start.1) | collective-permute-done | bytes 327712 | tf_op jit(solution)/shard_map/ppermute | solution.py:42
  42.0 0.9 collective-permute-done.2
  42.9 0.0 copy-start
  42.9 0.1 pad_maximum_fusion.mid
  43.0 2.1 %collective-permute-start.3 = (bf16[768,512]{1,0:T(8,128)(2,1)S(1)}, bf16[768,512]{1,0:T(8,128)(2,1)S(1)}, u32[]{:S(2)}, u32[]{:S(2)}) collective-permute-start(bf16[768,512]{1,0:T(8,128)(2,1)S(1)} %pad_maximum_fusion.mid), channel_id=1, source_target_pairs={{0,24},{8,32},{16,40},{24,48},{32,56},{40,64},{48,72},{56,80},{64,... | collective-permute-start | bytes 2359304 | tf_op jit(solution)/shard_map/ppermute | solution.py:42
  45.1 5.5 %collective-permute-start.4 = (bf16[768,512]{1,0:T(8,128)(2,1)S(1)}, bf16[768,512]{1,0:T(8,128)(2,1)S(1)}, u32[]{:S(2)}, u32[]{:S(2)}) collective-permute-start(bf16[768,512]{1,0:T(8,128)(2,1)S(1)} %pad_maximum_fusion.mid), channel_id=1, source_target_pairs={{0,488},{8,496},{16,504},{24,0},{32,8},{40,16},{48,24},{56,32},{64... | collective-permute-start | bytes 2359304 | tf_op jit(solution)/shard_map/ppermute | solution.py:42
  50.6 1.9 %collective-permute-start.5 = (bf16[192,512]{1,0:T(8,128)(2,1)S(1)}, bf16[192,512]{1,0:T(8,128)(2,1)S(1)}, u32[]{:S(2)}, u32[]{:S(2)}) collective-permute-start(bf16[192,512]{1,0:T(8,128)(2,1)S(1)} %pad_maximum_fusion.1.mid), channel_id=1, source_target_pairs={{0,24},{8,32},{16,40},{24,48},{32,56},{40,64},{48,72},{56,80},{64,... | collective-permute-start | bytes 589832 | tf_op jit(solution)/shard_map/ppermute | solution.py:42
  52.5 5.5 %collective-permute-start.6 = (bf16[192,512]{1,0:T(8,128)(2,1)S(1)}, bf16[192,512]{1,0:T(8,128)(2,1)S(1)}, u32[]{:S(2)}, u32[]{:S(2)}) collective-permute-start(bf16[192,512]{1,0:T(8,128)(2,1)S(1)} %pad_maximum_fusion.1.mid), channel_id=1, source_target_pairs={{0,488},{8,496},{16,504},{24,0},{32,8},{40,16},{48,24},{56,32},{64... | collective-permute-start | bytes 589832 | tf_op jit(solution)/shard_map/ppermute | solution.py:42
  58.0 9.8 %collective-permute-done.5.low = bf16[192,512]{1,0:T(8,128)(2,1)S(1)} collective-permute-done((bf16[192,512]{1,0:T(8,128)(2,1)S(1)}, bf16[192,512]{1,0:T(8,128)(2,1)S(1)}, u32[]{:S(2)}, u32[]{:S(2)}) %collective-permute-start.5) | collective-permute-done | bytes 196640 | tf_op jit(solution)/shard_map/ppermute | solution.py:42
  67.8 1.0 %collective-permute-done.6.high = bf16[192,512]{1,0:T(8,128)(2,1)S(1)} collective-permute-done((bf16[192,512]{1,0:T(8,128)(2,1)S(1)}, bf16[192,512]{1,0:T(8,128)(2,1)S(1)}, u32[]{:S(2)}, u32[]{:S(2)}) %collective-permute-start.6) | collective-permute-done | bytes 196640 | tf_op jit(solution)/shard_map/ppermute | solution.py:42
  68.8 0.1 shard_map.87.rows
  69.0 2.6 %collective-permute-start.9 = (bf16[384,512]{1,0:T(8,128)(2,1)S(1)}, bf16[384,512]{1,0:T(8,128)(2,1)S(1)}, u32[]{:S(2)}, u32[]{:S(2)}) collective-permute-start(bf16[384,512]{1,0:T(8,128)(2,1)S(1)} %shard_map.87.rows), channel_id=1, source_target_pairs={{0,4},{2,6},{4,0},{6,2},{1,5},{3,7},{5,1},{7,3},{8,12},{10,14},{12... | collective-permute-start | bytes 1179656 | tf_op jit(solution)/shard_map/ppermute | solution.py:42
  71.5 2.7 %collective-permute-start.8 = (bf16[384,512]{1,0:T(8,128)(2,1)S(1)}, bf16[384,512]{1,0:T(8,128)(2,1)S(1)}, u32[]{:S(2)}, u32[]{:S(2)}) collective-permute-start(bf16[384,512]{1,0:T(8,128)(2,1)S(1)} %shard_map.87.rows), channel_id=1, source_target_pairs={{0,2},{2,4},{4,6},{6,0},{1,3},{3,5},{5,7},{7,1},{8,10},{10,12},{12... | collective-permute-start | bytes 1179656 | tf_op jit(solution)/shard_map/ppermute | solution.py:42
  74.3 3.8 %collective-permute-start.7 = (bf16[384,512]{1,0:T(8,128)(2,1)S(1)}, bf16[384,512]{1,0:T(8,128)(2,1)S(1)}, u32[]{:S(2)}, u32[]{:S(2)}) collective-permute-start(bf16[384,512]{1,0:T(8,128)(2,1)S(1)} %shard_map.87.rows), channel_id=1, source_target_pairs={{0,6},{2,0},{4,2},{6,4},{1,7},{3,1},{5,3},{7,5},{8,14},{10,8},{12,... | collective-permute-start | bytes 1179656 | tf_op jit(solution)/shard_map/ppermute | solution.py:42
  78.0 0.0 copy-done
  78.1 0.3 shard_map.88.scaled
  78.3 0.6 shard_map.89.refs_0_
  78.9 0.0 collective-permute-done.3.low
  78.9 0.0 collective-permute-done.4.high
  78.9 1.3 %shard_map.86.duals = bf16[512,1536]{1,0:T(8,128)(2,1)S(1)} custom-call(s32[16]{0:T(128)S(4)} %get-tuple-element.14.meta, bf16[768,512]{1,0:T(8,128)(2,1)S(1)} %collective-permute-done.3.low, bf16[768,512]{1,0:T(8,128)(2,1)S(1)} %pad_maximum_fusion.mid, bf16[768,512]{1,0:T(8,128)(2,1)S(1)} %collective-permute-done.4.high), custom_call_target="tpu_custom_call" | custom-call | flops 1000000000 | bytes 1000000 | tf_op jit(solution)/shard_map/pallas_call | solution.py:24
  80.2 0.0 collective-permute-done.9.rows
  80.2 10.5 %collective-permute-done.8.rows = bf16[384,512]{1,0:T(8,128)(2,1)S(1)} collective-permute-done((bf16[384,512]{1,0:T(8,128)(2,1)S(1)}, bf16[384,512]{1,0:T(8,128)(2,1)S(1)}, u32[]{:S(2)}, u32[]{:S(2)}) %collective-permute-start.8) | collective-permute-done | bytes 393248 | tf_op jit(solution)/shard_map/ppermute | solution.py:42
  90.8 0.0 collective-permute-done.7.rows
  90.8 0.6 shard_map.90.refs_0_
  91.3 0.6 shard_map.91.refs_0_
  91.9 0.6 shard_map.92.tapered
  92.5 1.0 shard_map.94
  93.5 3.5 %collective-permute-start.10 = (bf16[512,512]{1,0:T(8,128)(2,1)S(1)}, bf16[512,512]{1,0:T(8,128)(2,1)S(1)}, u32[]{:S(2)}, u32[]{:S(2)}) collective-permute-start(bf16[512,512]{1,0:T(8,128)(2,1)S(1)} %shard_map.94), channel_id=1, source_target_pairs={{0,1},{1,0},{2,3},{3,2},{4,5},{5,4},{6,7},{7,6},{8,9},{9,8},{10,11... | collective-permute-start | bytes 1572872 | tf_op jit(solution)/shard_map/ppermute | solution.py:42
  97.0 1.0 shard_map.93.mine
  97.9 0.5 collective-permute-done.10.theirs
  98.5 1.0 %shard_map.95 = f32[2048,128]{1,0:T(8,128)} custom-call(f32[512,512]{1,0:T(8,128)S(1)} %shard_map.93.mine, bf16[512,512]{1,0:T(8,128)(2,1)S(1)} %collective-permute-done.10.theirs), custom_call_target="tpu_custom_call" | custom-call | flops 100000000 | bytes 1000000 | tf_op jit(solution)/shard_map/pallas_call | solution.py:24
  (7 shorter events, 0.1 us)
Async XLA Ops:
  1.3 10.3 %collective-permute-start = (bf16[528,512]{1,0:T(8,128)(2,1)S(1)}, bf16[528,512]{1,0:T(8,128)(2,1)S(1)}, u32[]{:S(2)}, u32[]{:S(2)}) collective-permute-start(bf16[528,512]{1,0:T(8,128)(2,1)S(1)} %get-tuple-element.16.cells.own), channel_id=1, source_target_pairs={{0,1},{1,0},{2,3},{3,2},{4,5},{5,4},{6,7},{7,6},{8,9},{9,8},{10,11... | collective-permute-start | bytes 1622024 | tf_op jit(solution)/shard_map/ppermute | solution.py:42
  26.7 15.3 %collective-permute-start.1 = (bf16[320,512]{1,0:T(8,128)(2,1)S(1)}, bf16[320,512]{1,0:T(8,128)(2,1)S(1)}, u32[]{:S(2)}, u32[]{:S(2)}) collective-permute-start(bf16[320,512]{1,0:T(8,128)(2,1)S(1)} %shard_map.85), channel_id=1, source_target_pairs={{0,8},{8,16},{16,24},{24,32},{32,40},{40,48},{48,56},{56,64},{64,7... | collective-permute-start | bytes 983048 | tf_op jit(solution)/shard_map/ppermute | solution.py:42
  28.6 14.3 %collective-permute-start.2 = (bf16[320,512]{1,0:T(8,128)(2,1)S(1)}, bf16[320,512]{1,0:T(8,128)(2,1)S(1)}, u32[]{:S(2)}, u32[]{:S(2)}) collective-permute-start(bf16[320,512]{1,0:T(8,128)(2,1)S(1)} %shard_map.85), channel_id=1, source_target_pairs={{0,504},{8,0},{16,8},{24,16},{32,24},{40,32},{48,40},{56,48},{64,5... | collective-permute-start | bytes 983048 | tf_op jit(solution)/shard_map/ppermute | solution.py:42
  42.9 35.1 %copy-start = (bf16[4,128,512]{2,1,0:T(8,128)(2,1)S(1)}, bf16[4,128,512]{2,1,0:T(8,128)(2,1)}, u32[]{:S(2)}) copy-start(bf16[4,128,512]{2,1,0:T(8,128)(2,1)} %taper) | copy-start | bytes 1572868
  43.0 35.9 %collective-permute-start.3 = (bf16[768,512]{1,0:T(8,128)(2,1)S(1)}, bf16[768,512]{1,0:T(8,128)(2,1)S(1)}, u32[]{:S(2)}, u32[]{:S(2)}) collective-permute-start(bf16[768,512]{1,0:T(8,128)(2,1)S(1)} %pad_maximum_fusion.mid), channel_id=1, source_target_pairs={{0,24},{8,32},{16,40},{24,48},{32,56},{40,64},{48,72},{56,80},{64,... | collective-permute-start | bytes 2359304 | tf_op jit(solution)/shard_map/ppermute | solution.py:42
  45.1 33.8 %collective-permute-start.4 = (bf16[768,512]{1,0:T(8,128)(2,1)S(1)}, bf16[768,512]{1,0:T(8,128)(2,1)S(1)}, u32[]{:S(2)}, u32[]{:S(2)}) collective-permute-start(bf16[768,512]{1,0:T(8,128)(2,1)S(1)} %pad_maximum_fusion.mid), channel_id=1, source_target_pairs={{0,488},{8,496},{16,504},{24,0},{32,8},{40,16},{48,24},{56,32},{64... | collective-permute-start | bytes 2359304 | tf_op jit(solution)/shard_map/ppermute | solution.py:42
  50.6 17.2 %collective-permute-start.5 = (bf16[192,512]{1,0:T(8,128)(2,1)S(1)}, bf16[192,512]{1,0:T(8,128)(2,1)S(1)}, u32[]{:S(2)}, u32[]{:S(2)}) collective-permute-start(bf16[192,512]{1,0:T(8,128)(2,1)S(1)} %pad_maximum_fusion.1.mid), channel_id=1, source_target_pairs={{0,24},{8,32},{16,40},{24,48},{32,56},{40,64},{48,72},{56,80},{64,... | collective-permute-start | bytes 589832 | tf_op jit(solution)/shard_map/ppermute | solution.py:42
  52.5 16.3 %collective-permute-start.6 = (bf16[192,512]{1,0:T(8,128)(2,1)S(1)}, bf16[192,512]{1,0:T(8,128)(2,1)S(1)}, u32[]{:S(2)}, u32[]{:S(2)}) collective-permute-start(bf16[192,512]{1,0:T(8,128)(2,1)S(1)} %pad_maximum_fusion.1.mid), channel_id=1, source_target_pairs={{0,488},{8,496},{16,504},{24,0},{32,8},{40,16},{48,24},{56,32},{64... | collective-permute-start | bytes 589832 | tf_op jit(solution)/shard_map/ppermute | solution.py:42
  69.0 11.3 %collective-permute-start.9 = (bf16[384,512]{1,0:T(8,128)(2,1)S(1)}, bf16[384,512]{1,0:T(8,128)(2,1)S(1)}, u32[]{:S(2)}, u32[]{:S(2)}) collective-permute-start(bf16[384,512]{1,0:T(8,128)(2,1)S(1)} %shard_map.87.rows), channel_id=1, source_target_pairs={{0,4},{2,6},{4,0},{6,2},{1,5},{3,7},{5,1},{7,3},{8,12},{10,14},{12... | collective-permute-start | bytes 1179656 | tf_op jit(solution)/shard_map/ppermute | solution.py:42
  71.5 19.2 %collective-permute-start.8 = (bf16[384,512]{1,0:T(8,128)(2,1)S(1)}, bf16[384,512]{1,0:T(8,128)(2,1)S(1)}, u32[]{:S(2)}, u32[]{:S(2)}) collective-permute-start(bf16[384,512]{1,0:T(8,128)(2,1)S(1)} %shard_map.87.rows), channel_id=1, source_target_pairs={{0,2},{2,4},{4,6},{6,0},{1,3},{3,5},{5,7},{7,1},{8,10},{10,12},{12... | collective-permute-start | bytes 1179656 | tf_op jit(solution)/shard_map/ppermute | solution.py:42
  74.3 16.5 %collective-permute-start.7 = (bf16[384,512]{1,0:T(8,128)(2,1)S(1)}, bf16[384,512]{1,0:T(8,128)(2,1)S(1)}, u32[]{:S(2)}, u32[]{:S(2)}) collective-permute-start(bf16[384,512]{1,0:T(8,128)(2,1)S(1)} %shard_map.87.rows), channel_id=1, source_target_pairs={{0,6},{2,0},{4,2},{6,4},{1,7},{3,1},{5,3},{7,5},{8,14},{10,8},{12,... | collective-permute-start | bytes 1179656 | tf_op jit(solution)/shard_map/ppermute | solution.py:42
  93.5 5.0 %collective-permute-start.10 = (bf16[512,512]{1,0:T(8,128)(2,1)S(1)}, bf16[512,512]{1,0:T(8,128)(2,1)S(1)}, u32[]{:S(2)}, u32[]{:S(2)}) collective-permute-start(bf16[512,512]{1,0:T(8,128)(2,1)S(1)} %shard_map.94), channel_id=1, source_target_pairs={{0,1},{1,0},{2,3},{3,2},{4,5},{5,4},{6,7},{7,6},{8,9},{9,8},{10,11... | collective-permute-start | bytes 1572872 | tf_op jit(solution)/shard_map/ppermute | solution.py:42

commit v7 on v6

--- a/solution.py
+++ b/solution.py
@@ -185,28 +185,25 @@
             out[r, k * owned : (k + 1) * owned] = tall[meta[CLASS + k], pl.ds(start, owned), :]
 
 
-def covary_body(rel, rows, own, other, scaled, *refs):
-    out = refs[-1]
-    members = rows.shape[1]
-    size = rows.shape[0]
-    half = own.shape[1]
+def analyse_body(rels, count, *refs):
+    rows, (scaled, flipped) = refs[: len(rels)], refs[len(rels) : len(rels) + 2]
+    cells = refs[len(rels) + 2 : len(rels) + 2 + count]
+    before, outs = refs[len(rels) + 2 + count : -count], refs[-count:]
+    size, members = rows[0].shape
     step = 256
-    taper = scaled[rel]
-    wide = jnp.concatenate([taper] * (step // taper.shape[1]), axis=1)
-    for h, cells in enumerate((own, other)):
-        for at in range(0, half, step):
-            covar = jnp.dot(rows[...], cells[:members, at : at + step], preferred_element_type=F32)
-            tapered = (covar * wide).astype(BF16)
-            out[rel * size : (rel + 1) * size, h * half + at : h * half + at + step] = tapered
-
-
-def gain_body(h, duals, tapered, out):
-    half = out.shape[1]
-    step = 256
-    for at in range(0, half, step):
-        span = slice(h * half + at, h * half + at + step)
-        gained = jnp.dot(duals[...], tapered[:, span], preferred_element_type=F32)
-        out[:, at : at + step] = gained.astype(out.dtype)
+    for h in range(count):
+        for at in range(0, outs[h].shape[1], step):
+            span = slice(at, at + step)
+            total = before[h][:, span] if before else None
+            for rel, got in zip(rels, rows):
+                taper = scaled[rel]
+                wide = jnp.concatenate([taper] * (step // taper.shape[1]), axis=1)
+                covar = jnp.dot(got[...], cells[h][:members, span], preferred_element_type=F32)
+                tapered = (covar * wide).astype(BF16)
+                duals = flipped[:, rel * size : (rel + 1) * size]
+                gained = jnp.dot(duals, tapered, preferred_element_type=F32)
+                total = gained if total is None else total + gained
+            outs[h][:, span] = total.astype(outs[h].dtype)
 
 
 def finish_body(mine, theirs, out, held, done):
@@ -305,31 +302,25 @@
         scalars=1,
         scratch=[pltpu.VMEM((NEAR * owned, members), BF16)],
     )
-    y3, y1, y2 = (lax.optimization_barrier((y, flipped))[0] for y in (y3, y1, y2))
-    tapered = None
-    for rel, got in ((0, y0), (2, y2), (3, y3), (1, y1)):
-        inputs = [got, own, other, scaled] + ([] if tapered is None else [tapered])
-        (tapered,) = kernel(
-            functools.partial(covary_body, rel),
-            [array((NEAR * rows, 2 * width), BF16)],
-            inputs,
-            4 * NEAR * owned * members * width,
-            aliases={} if tapered is None else {4: 0},
+
+    def analyse(rels, rows, halves, before, kind):
+        planes = [(own, other)[h] for h in halves]
+        return kernel(
+            functools.partial(analyse_body, rels, len(halves)),
+            [array((members, width), kind)] * len(halves),
+            [*rows, scaled, flipped, *planes, *before],
+            4 * NEAR * owned * members * width * len(halves) * len(rels),
         )
-    sums = [
-        kernel(
-            functools.partial(gain_body, h),
-            [array((members, width), BF16 if h else F32)],
-            [flipped, tapered],
-            2 * NEAR * rows * members * width,
-        )[0]
-        for h in (0, 1)
-    ]
-    theirs = move(sums[1], "c", 1)
+
+    sums = analyse((0,), (y0,), (0, 1), (), F32)
+    sums = analyse((2,), (y2,), (0, 1), sums, F32)
+    (given,) = analyse((3, 1), (y3, y1), (1,), sums[1:], BF16)
+    (kept,) = analyse((3, 1), (y3, y1), (0,), sums[:1], F32)
+    theirs = move(given, "c", 1)
     (out,) = kernel(
         finish_body,
         [array((members * levels, points), F32)],
-        [sums[0], theirs],
+        [kept, theirs],
         1e8,
         scratch=[pltpu.VMEM((members * levels, points), F32), pltpu.SemaphoreType.DMA((4,))],
         spaces=[None],

time: 100 us -> 99.1 us (level)
  waiting for transfers between devices: 28.1 us -> 25.3 us
  Pallas kernels: 9.4 us -> 11.3 us
    ppermute x11, waiting for transfers between devices: 28.1 us -> 25.3 us  [move(): lax.ppermute(value, axis, [(i, (i + steps) % count) for i in range(count)])]
    pallas_call x14 -> x12, Pallas kernels: 9.4 us -> 11.3 us  [kernel(): pl.pallas_call(body, out_shape=[o if m is None else m(o.shape, o.dtype) f...]
  transfers between devices with their start and end apart: 11 -> 11, of which waited for: 7 -> 6; matrix products, arithmetic and copies ran while one was open for 0% -> 0% of each run, Pallas kernels for 4% -> 7%
where the time goes in v7:
time: 99.1 us; the launch traced here: 98.6 us
  starting transfers between devices  47.2 us (48%)
  waiting for transfers between devices  25.3 us (26%)
  blocking collectives  14.4 us (15%)
  Pallas kernels  11.3 us (11%)
    ppermute x11, starting transfers between devices, move(): lax.ppermute(value, axis, [(i, (i + steps) % count) for i in range(count)])  47.2 us
    ppermute x11, waiting for transfers between devices, move(): lax.ppermute(value, axis, [(i, (i + steps) % count) for i in range(count)])  25.3 us
    all_to_all x1, blocking collectives, shards(): got = lax.all_to_all(pay, 'x', 0, 0, tiled=True)  14.4 us
    pallas_call x12, Pallas kernels, kernel(): pl.pallas_call(body, out_shape=[o if m is None else m(o.shape, o.dtype) f...  11.3 us
  transfers between devices with their start and end apart: 11, of which 6 were waited for; matrix products, arithmetic and copies ran while one was open for 0% of the time, Pallas kernels for 7%

profile of v7, /device:TPU:1, one launch (start us, length us, event | category | flops | bytes accessed | tf_op | source)
XLA Modules:
  0.0 98.6 jit_solution(12375167431858883942)
XLA Ops:
  0.0 1.3 %shard_map.82 = (s32[16]{0:T(128)S(4)}, bf16[528,512]{1,0:T(8,128)(2,1)S(1)}, f32[4,512]{1,0:T(4,128)S(1)}, bf16[512,128]{1,0:T(8,128)(2,1)S(1)}, bf16[64,512]{1,0:T(8,128)(2,1)S(1)}) custom-call(s32[6,64]{1,0:T(8,128)} %bitcast.4, s32[64]{0:T(128)} %refs_1_.1, s32[1,6]{1,0:T(1,128)} %refs_2_.1, bf16[2048,128]{1,0:T(8,128)(2,1)} %bitcast.3, ...), custom_call_target="tpu_custom_call" | custom-call | flops 100000000 | bytes 1000000 | tf_op jit(solution)/shard_map/pallas_call | solution.py:24
  1.3 8.7 %collective-permute-start = (bf16[528,512]{1,0:T(8,128)(2,1)S(1)}, bf16[528,512]{1,0:T(8,128)(2,1)S(1)}, u32[]{:S(2)}, u32[]{:S(2)}) collective-permute-start(bf16[528,512]{1,0:T(8,128)(2,1)S(1)} %get-tuple-element.17.cells.refs_3_.refs_4_), channel_id=1, source_target_pairs={{0,1},{1,0},{2,3},{3,2},{4,5},{5,4},{6,7},{7,6},{8,9},{9,8},{10,11... | collective-permute-start | bytes 1622024 | tf_op jit(solution)/shard_map/ppermute | solution.py:42
  10.1 0.5 shard_map.83.before
  10.6 1.0 %collective-permute-done.cells.refs_4_ = bf16[528,512]{1,0:T(8,128)(2,1)S(1)} collective-permute-done((bf16[528,512]{1,0:T(8,128)(2,1)S(1)}, bf16[528,512]{1,0:T(8,128)(2,1)S(1)}, u32[]{:S(2)}, u32[]{:S(2)}) %collective-permute-start) | collective-permute-done | bytes 540704 | tf_op jit(solution)/shard_map/ppermute | solution.py:42
  11.6 0.6 shard_map.84
  12.2 14.4 %all_to_all.5.got = bf16[4,192,512]{2,1,0:T(8,128)(2,1)S(1)} all-to-all(bf16[4,192,512]{2,1,0:T(8,128)(2,1)S(1)} %shard_map.84), channel_id=1, replica_groups=mesh['z'=16,'y'=4,'x'=4,'c'=2] {'x'}, dimensions={0} | all-to-all | bytes 1572864 | tf_op jit(solution)/shard_map/all_to_all | solution.py:271
  26.6 0.1 shard_map.85
  26.7 1.9 %collective-permute-start.1 = (bf16[320,512]{1,0:T(8,128)(2,1)S(1)}, bf16[320,512]{1,0:T(8,128)(2,1)S(1)}, u32[]{:S(2)}, u32[]{:S(2)}) collective-permute-start(bf16[320,512]{1,0:T(8,128)(2,1)S(1)} %shard_map.85), channel_id=1, source_target_pairs={{0,8},{8,16},{16,24},{24,32},{32,40},{40,48},{48,56},{56,64},{64,7... | collective-permute-start | bytes 983048 | tf_op jit(solution)/shard_map/ppermute | solution.py:42
  28.6 9.0 %collective-permute-start.2 = (bf16[320,512]{1,0:T(8,128)(2,1)S(1)}, bf16[320,512]{1,0:T(8,128)(2,1)S(1)}, u32[]{:S(2)}, u32[]{:S(2)}) collective-permute-start(bf16[320,512]{1,0:T(8,128)(2,1)S(1)} %shard_map.85), channel_id=1, source_target_pairs={{0,504},{8,0},{16,8},{24,16},{32,24},{40,32},{48,40},{56,48},{64,5... | collective-permute-start | bytes 983048 | tf_op jit(solution)/shard_map/ppermute | solution.py:42
  37.7 4.3 %collective-permute-done.1 = bf16[320,512]{1,0:T(8,128)(2,1)S(1)} collective-permute-done((bf16[320,512]{1,0:T(8,128)(2,1)S(1)}, bf16[320,512]{1,0:T(8,128)(2,1)S(1)}, u32[]{:S(2)}, u32[]{:S(2)}) %collective-permute-start.1) | collective-permute-done | bytes 327712 | tf_op jit(solution)/shard_map/ppermute | solution.py:42
  42.0 0.9 collective-permute-done.2
  42.9 0.0 copy-start
  42.9 0.1 pad_maximum_fusion.mid
  43.0 2.1 %collective-permute-start.7 = (bf16[768,512]{1,0:T(8,128)(2,1)S(1)}, bf16[768,512]{1,0:T(8,128)(2,1)S(1)}, u32[]{:S(2)}, u32[]{:S(2)}) collective-permute-start(bf16[768,512]{1,0:T(8,128)(2,1)S(1)} %pad_maximum_fusion.mid), channel_id=1, source_target_pairs={{0,24},{8,32},{16,40},{24,48},{32,56},{40,64},{48,72},{56,80},{64,... | collective-permute-start | bytes 2359304 | tf_op jit(solution)/shard_map/ppermute | solution.py:42
  45.1 5.5 %collective-permute-start.8 = (bf16[768,512]{1,0:T(8,128)(2,1)S(1)}, bf16[768,512]{1,0:T(8,128)(2,1)S(1)}, u32[]{:S(2)}, u32[]{:S(2)}) collective-permute-start(bf16[768,512]{1,0:T(8,128)(2,1)S(1)} %pad_maximum_fusion.mid), channel_id=1, source_target_pairs={{0,488},{8,496},{16,504},{24,0},{32,8},{40,16},{48,24},{56,32},{64... | collective-permute-start | bytes 2359304 | tf_op jit(solution)/shard_map/ppermute | solution.py:42
  50.6 1.9 %collective-permute-start.3 = (bf16[192,512]{1,0:T(8,128)(2,1)S(1)}, bf16[192,512]{1,0:T(8,128)(2,1)S(1)}, u32[]{:S(2)}, u32[]{:S(2)}) collective-permute-start(bf16[192,512]{1,0:T(8,128)(2,1)S(1)} %pad_maximum_fusion.1.mid), channel_id=1, source_target_pairs={{0,24},{8,32},{16,40},{24,48},{32,56},{40,64},{48,72},{56,80},{64,... | collective-permute-start | bytes 589832 | tf_op jit(solution)/shard_map/ppermute | solution.py:42
  52.5 5.5 %collective-permute-start.4 = (bf16[192,512]{1,0:T(8,128)(2,1)S(1)}, bf16[192,512]{1,0:T(8,128)(2,1)S(1)}, u32[]{:S(2)}, u32[]{:S(2)}) collective-permute-start(bf16[192,512]{1,0:T(8,128)(2,1)S(1)} %pad_maximum_fusion.1.mid), channel_id=1, source_target_pairs={{0,488},{8,496},{16,504},{24,0},{32,8},{40,16},{48,24},{56,32},{64... | collective-permute-start | bytes 589832 | tf_op jit(solution)/shard_map/ppermute | solution.py:42
  58.0 9.8 %collective-permute-done.3.low = bf16[192,512]{1,0:T(8,128)(2,1)S(1)} collective-permute-done((bf16[192,512]{1,0:T(8,128)(2,1)S(1)}, bf16[192,512]{1,0:T(8,128)(2,1)S(1)}, u32[]{:S(2)}, u32[]{:S(2)}) %collective-permute-start.3) | collective-permute-done | bytes 196640 | tf_op jit(solution)/shard_map/ppermute | solution.py:42
  67.8 1.0 %collective-permute-done.4.high = bf16[192,512]{1,0:T(8,128)(2,1)S(1)} collective-permute-done((bf16[192,512]{1,0:T(8,128)(2,1)S(1)}, bf16[192,512]{1,0:T(8,128)(2,1)S(1)}, u32[]{:S(2)}, u32[]{:S(2)}) %collective-permute-start.4) | collective-permute-done | bytes 196640 | tf_op jit(solution)/shard_map/ppermute | solution.py:42
  68.8 0.1 shard_map.86.refs_0_
  69.0 2.6 %collective-permute-start.9 = (bf16[384,512]{1,0:T(8,128)(2,1)S(1)}, bf16[384,512]{1,0:T(8,128)(2,1)S(1)}, u32[]{:S(2)}, u32[]{:S(2)}) collective-permute-start(bf16[384,512]{1,0:T(8,128)(2,1)S(1)} %shard_map.86.refs_0_), channel_id=1, source_target_pairs={{0,4},{2,6},{4,0},{6,2},{1,5},{3,7},{5,1},{7,3},{8,12},{10,14},{12... | collective-permute-start | bytes 1179656 | tf_op jit(solution)/shard_map/ppermute | solution.py:42
  71.5 2.7 %collective-permute-start.5 = (bf16[384,512]{1,0:T(8,128)(2,1)S(1)}, bf16[384,512]{1,0:T(8,128)(2,1)S(1)}, u32[]{:S(2)}, u32[]{:S(2)}) collective-permute-start(bf16[384,512]{1,0:T(8,128)(2,1)S(1)} %shard_map.86.refs_0_), channel_id=1, source_target_pairs={{0,2},{2,4},{4,6},{6,0},{1,3},{3,5},{5,7},{7,1},{8,10},{10,12},{12... | collective-permute-start | bytes 1179656 | tf_op jit(solution)/shard_map/ppermute | solution.py:42
  74.3 3.8 %collective-permute-start.6 = (bf16[384,512]{1,0:T(8,128)(2,1)S(1)}, bf16[384,512]{1,0:T(8,128)(2,1)S(1)}, u32[]{:S(2)}, u32[]{:S(2)}) collective-permute-start(bf16[384,512]{1,0:T(8,128)(2,1)S(1)} %shard_map.86.refs_0_), channel_id=1, source_target_pairs={{0,6},{2,0},{4,2},{6,4},{1,7},{3,1},{5,3},{7,5},{8,14},{10,8},{12,... | collective-permute-start | bytes 1179656 | tf_op jit(solution)/shard_map/ppermute | solution.py:42
  78.0 0.0 copy-done
  78.1 0.3 shard_map.87.refs_1_.refs_2_
  78.3 0.0 collective-permute-done.7.low
  78.3 0.0 collective-permute-done.8.high
  78.3 1.3 %shard_map.88.refs_2_.refs_3_ = bf16[512,1536]{1,0:T(8,128)(2,1)S(1)} custom-call(s32[16]{0:T(128)S(4)} %get-tuple-element.15.meta, bf16[768,512]{1,0:T(8,128)(2,1)S(1)} %collective-permute-done.7.low, bf16[768,512]{1,0:T(8,128)(2,1)S(1)} %pad_maximum_fusion.mid, bf16[768,512]{1,0:T(8,128)(2,1)S(1)} %collective-permute-done.8.high), custom_call_target="tpu_custom_call" | custom-call | flops 1000000000 | bytes 1000000 | tf_op jit(solution)/shard_map/pallas_call | solution.py:24
  79.7 1.4 %shard_map.89 = (f32[512,512]{1,0:T(8,128)S(1)}, f32[512,512]{1,0:T(8,128)S(1)}) custom-call(bf16[384,512]{1,0:T(8,128)(2,1)S(1)} %shard_map.86.refs_0_, f32[4,384,128]{2,1,0:T(8,128)S(1)} %shard_map.87.refs_1_.refs_2_, bf16[512,1536]{1,0:T(8,128)(2,1)S(1)} %shard_map.88.refs_2_.refs_3_, bf16[528,512]{1,0:T(8,128)(2,1)S(1)} %get-tuple-element.17.cells.refs_3_.refs_4_, ...), custom_call_target="tpu_custom_call" | custom-call | flops 805306368 | bytes 1000000 | tf_op jit(solution)/shard_map/pallas_call | solution.py:24
  81.1 0.0 collective-permute-done.9.refs_0_
  81.1 1.4 %shard_map.90 = (f32[512,512]{1,0:T(8,128)S(1)}, f32[512,512]{1,0:T(8,128)S(1)}) custom-call(bf16[384,512]{1,0:T(8,128)(2,1)S(1)} %collective-permute-done.9.refs_0_, f32[4,384,128]{2,1,0:T(8,128)S(1)} %shard_map.87.refs_1_.refs_2_, bf16[512,1536]{1,0:T(8,128)(2,1)S(1)} %shard_map.88.refs_2_.refs_3_, ...), custom_call_target="tpu_custom_call" | custom-call | flops 805306368 | bytes 1000000 | tf_op jit(solution)/shard_map/pallas_call | solution.py:24
  82.5 8.3 %collective-permute-done.5.refs_0_ = bf16[384,512]{1,0:T(8,128)(2,1)S(1)} collective-permute-done((bf16[384,512]{1,0:T(8,128)(2,1)S(1)}, bf16[384,512]{1,0:T(8,128)(2,1)S(1)}, u32[]{:S(2)}, u32[]{:S(2)}) %collective-permute-start.5) | collective-permute-done | bytes 393248 | tf_op jit(solution)/shard_map/ppermute | solution.py:42
  90.8 0.0 collective-permute-done.6.refs_1_
  90.8 1.7 %shard_map.92 = bf16[512,512]{1,0:T(8,128)(2,1)S(1)} custom-call(bf16[384,512]{1,0:T(8,128)(2,1)S(1)} %collective-permute-done.5.refs_0_, bf16[384,512]{1,0:T(8,128)(2,1)S(1)} %collective-permute-done.6.refs_1_, f32[4,384,128]{2,1,0:T(8,128)S(1)} %shard_map.87.refs_1_.refs_2_, bf16[512,1536]{1,0:T(8,128)(2,1)S(1)} %shard_map.88.refs_2_.refs_3_, ...), custom_call_target="tpu_custom_call" | custom-call | flops 805306368 | bytes 1000000 | tf_op jit(solution)/shard_map/pallas_call | solution.py:24
  92.4 3.5 %collective-permute-start.10 = (bf16[512,512]{1,0:T(8,128)(2,1)S(1)}, bf16[512,512]{1,0:T(8,128)(2,1)S(1)}, u32[]{:S(2)}, u32[]{:S(2)}) collective-permute-start(bf16[512,512]{1,0:T(8,128)(2,1)S(1)} %shard_map.92), channel_id=1, source_target_pairs={{0,1},{1,0},{2,3},{3,2},{4,5},{5,4},{6,7},{7,6},{8,9},{9,8},{10,11... | collective-permute-start | bytes 1572872 | tf_op jit(solution)/shard_map/ppermute | solution.py:42
  95.9 1.7 %shard_map.91.mine = f32[512,512]{1,0:T(8,128)S(1)} custom-call(bf16[384,512]{1,0:T(8,128)(2,1)S(1)} %collective-permute-done.5.refs_0_, bf16[384,512]{1,0:T(8,128)(2,1)S(1)} %collective-permute-done.6.refs_1_, f32[4,384,128]{2,1,0:T(8,128)S(1)} %shard_map.87.refs_1_.refs_2_, bf16[512,1536]{1,0:T(8,128)(2,1)S(1)} %shard_map.88.refs_2_.refs_3_, ...), custom_call_target="tpu_custom_call" | custom-call | flops 805306368 | bytes 1000000 | tf_op jit(solution)/shard_map/pallas_call | solution.py:24
  97.6 0.0 collective-permute-done.10.theirs
  97.6 1.0 %shard_map.93 = f32[2048,128]{1,0:T(8,128)} custom-call(f32[512,512]{1,0:T(8,128)S(1)} %shard_map.91.mine, bf16[512,512]{1,0:T(8,128)(2,1)S(1)} %collective-permute-done.10.theirs), custom_call_target="tpu_custom_call" | custom-call | flops 100000000 | bytes 1000000 | tf_op jit(solution)/shard_map/pallas_call | solution.py:24
  (7 shorter events, 0.1 us)
Async XLA Ops:
  1.3 10.3 %collective-permute-start = (bf16[528,512]{1,0:T(8,128)(2,1)S(1)}, bf16[528,512]{1,0:T(8,128)(2,1)S(1)}, u32[]{:S(2)}, u32[]{:S(2)}) collective-permute-start(bf16[528,512]{1,0:T(8,128)(2,1)S(1)} %get-tuple-element.17.cells.refs_3_.refs_4_), channel_id=1, source_target_pairs={{0,1},{1,0},{2,3},{3,2},{4,5},{5,4},{6,7},{7,6},{8,9},{9,8},{10,11... | collective-permute-start | bytes 1622024 | tf_op jit(solution)/shard_map/ppermute | solution.py:42
  26.7 15.3 %collective-permute-start.1 = (bf16[320,512]{1,0:T(8,128)(2,1)S(1)}, bf16[320,512]{1,0:T(8,128)(2,1)S(1)}, u32[]{:S(2)}, u32[]{:S(2)}) collective-permute-start(bf16[320,512]{1,0:T(8,128)(2,1)S(1)} %shard_map.85), channel_id=1, source_target_pairs={{0,8},{8,16},{16,24},{24,32},{32,40},{40,48},{48,56},{56,64},{64,7... | collective-permute-start | bytes 983048 | tf_op jit(solution)/shard_map/ppermute | solution.py:42
  28.6 14.3 %collective-permute-start.2 = (bf16[320,512]{1,0:T(8,128)(2,1)S(1)}, bf16[320,512]{1,0:T(8,128)(2,1)S(1)}, u32[]{:S(2)}, u32[]{:S(2)}) collective-permute-start(bf16[320,512]{1,0:T(8,128)(2,1)S(1)} %shard_map.85), channel_id=1, source_target_pairs={{0,504},{8,0},{16,8},{24,16},{32,24},{40,32},{48,40},{56,48},{64,5... | collective-permute-start | bytes 983048 | tf_op jit(solution)/shard_map/ppermute | solution.py:42
  42.9 35.1 %copy-start = (bf16[4,128,512]{2,1,0:T(8,128)(2,1)S(1)}, bf16[4,128,512]{2,1,0:T(8,128)(2,1)}, u32[]{:S(2)}) copy-start(bf16[4,128,512]{2,1,0:T(8,128)(2,1)} %taper) | copy-start | bytes 1572868
  43.0 35.3 %collective-permute-start.7 = (bf16[768,512]{1,0:T(8,128)(2,1)S(1)}, bf16[768,512]{1,0:T(8,128)(2,1)S(1)}, u32[]{:S(2)}, u32[]{:S(2)}) collective-permute-start(bf16[768,512]{1,0:T(8,128)(2,1)S(1)} %pad_maximum_fusion.mid), channel_id=1, source_target_pairs={{0,24},{8,32},{16,40},{24,48},{32,56},{40,64},{48,72},{56,80},{64,... | collective-permute-start | bytes 2359304 | tf_op jit(solution)/shard_map/ppermute | solution.py:42
  45.1 33.3 %collective-permute-start.8 = (bf16[768,512]{1,0:T(8,128)(2,1)S(1)}, bf16[768,512]{1,0:T(8,128)(2,1)S(1)}, u32[]{:S(2)}, u32[]{:S(2)}) collective-permute-start(bf16[768,512]{1,0:T(8,128)(2,1)S(1)} %pad_maximum_fusion.mid), channel_id=1, source_target_pairs={{0,488},{8,496},{16,504},{24,0},{32,8},{40,16},{48,24},{56,32},{64... | collective-permute-start | bytes 2359304 | tf_op jit(solution)/shard_map/ppermute | solution.py:42
  50.6 17.2 %collective-permute-start.3 = (bf16[192,512]{1,0:T(8,128)(2,1)S(1)}, bf16[192,512]{1,0:T(8,128)(2,1)S(1)}, u32[]{:S(2)}, u32[]{:S(2)}) collective-permute-start(bf16[192,512]{1,0:T(8,128)(2,1)S(1)} %pad_maximum_fusion.1.mid), channel_id=1, source_target_pairs={{0,24},{8,32},{16,40},{24,48},{32,56},{40,64},{48,72},{56,80},{64,... | collective-permute-start | bytes 589832 | tf_op jit(solution)/shard_map/ppermute | solution.py:42
  52.5 16.3 %collective-permute-start.4 = (bf16[192,512]{1,0:T(8,128)(2,1)S(1)}, bf16[192,512]{1,0:T(8,128)(2,1)S(1)}, u32[]{:S(2)}, u32[]{:S(2)}) collective-permute-start(bf16[192,512]{1,0:T(8,128)(2,1)S(1)} %pad_maximum_fusion.1.mid), channel_id=1, source_target_pairs={{0,488},{8,496},{16,504},{24,0},{32,8},{40,16},{48,24},{56,32},{64... | collective-permute-start | bytes 589832 | tf_op jit(solution)/shard_map/ppermute | solution.py:42
  69.0 12.1 %collective-permute-start.9 = (bf16[384,512]{1,0:T(8,128)(2,1)S(1)}, bf16[384,512]{1,0:T(8,128)(2,1)S(1)}, u32[]{:S(2)}, u32[]{:S(2)}) collective-permute-start(bf16[384,512]{1,0:T(8,128)(2,1)S(1)} %shard_map.86.refs_0_), channel_id=1, source_target_pairs={{0,4},{2,6},{4,0},{6,2},{1,5},{3,7},{5,1},{7,3},{8,12},{10,14},{12... | collective-permute-start | bytes 1179656 | tf_op jit(solution)/shard_map/ppermute | solution.py:42
  71.5 19.2 %collective-permute-start.5 = (bf16[384,512]{1,0:T(8,128)(2,1)S(1)}, bf16[384,512]{1,0:T(8,128)(2,1)S(1)}, u32[]{:S(2)}, u32[]{:S(2)}) collective-permute-start(bf16[384,512]{1,0:T(8,128)(2,1)S(1)} %shard_map.86.refs_0_), channel_id=1, source_target_pairs={{0,2},{2,4},{4,6},{6,0},{1,3},{3,5},{5,7},{7,1},{8,10},{10,12},{12... | collective-permute-start | bytes 1179656 | tf_op jit(solution)/shard_map/ppermute | solution.py:42
  74.3 16.5 %collective-permute-start.6 = (bf16[384,512]{1,0:T(8,128)(2,1)S(1)}, bf16[384,512]{1,0:T(8,128)(2,1)S(1)}, u32[]{:S(2)}, u32[]{:S(2)}) collective-permute-start(bf16[384,512]{1,0:T(8,128)(2,1)S(1)} %shard_map.86.refs_0_), channel_id=1, source_target_pairs={{0,6},{2,0},{4,2},{6,4},{1,7},{3,1},{5,3},{7,5},{8,14},{10,8},{12,... | collective-permute-start | bytes 1179656 | tf_op jit(solution)/shard_map/ppermute | solution.py:42
  92.4 5.2 %collective-permute-start.10 = (bf16[512,512]{1,0:T(8,128)(2,1)S(1)}, bf16[512,512]{1,0:T(8,128)(2,1)S(1)}, u32[]{:S(2)}, u32[]{:S(2)}) collective-permute-start(bf16[512,512]{1,0:T(8,128)(2,1)S(1)} %shard_map.92), channel_id=1, source_target_pairs={{0,1},{1,0},{2,3},{3,2},{4,5},{5,4},{6,7},{7,6},{8,9},{9,8},{10,11... | collective-permute-start | bytes 1572872 | tf_op jit(solution)/shard_map/ppermute | solution.py:42
